TPU v7x, 32 devices: a whole 2x2x4 slice. The times are simulated.
32 devices in a mesh: cube: 2 (over x), chan: 8 (over z, y), split: 2 (over core).
Axes of the slice: x: 2, y: 2, z: 4, core: 2. Of those that a mesh axis runs over, the one named last changes fastest.
Arguments:
- sky_image: bfloat16 [16, 8, 1, 2, 512, 128], P(('cube', 'chan'), None, None, 'split'), parts along dimension 0, may hold values from 0 to 8
- dirty_image: bfloat16 [16, 8, 1, 2, 512, 128], P(('cube', 'chan'), None, None, 'split'), parts along dimension 0, may hold values from -6 to 6
- uv_weights: int32 [16, 1024, 512], P(('cube', 'chan'), 'split'), parts along dimension 0, may hold values from 0 to 7
- dual_coeffs: bfloat16 [4, 16, 8, 2, 512, 128], P(None, 'cube', 'chan', 'split'), parts along dimension 1, may hold values from -3 to 3
- support_mask: int32 [8, 2, 512, 128], P('chan', 'split'), may hold values 0 or 1
- row_taps: float32 [4, 17], replicated, may hold values from -1.5 to 1.5
- col_taps: float32 [4, 17], replicated, may hold values from -1.5 to 1.5
Outputs:
- new_image: bfloat16 [16, 8, 1, 2, 512, 128], P(('cube', 'chan'), None, None, 'split'), parts along dimension 0
- new_dual: bfloat16 [4, 16, 8, 2, 512, 128], P(None, 'cube', 'chan', 'split'), parts along dimension 1
There are 2 independent parts, one for each index of `cube`. A program takes and returns all parts, laid end to end along the dimension named above; an argument that names none is the same for every part. Nothing has to cross between parts.
All inputs are finite; a program needn't handle non-finite values. No bound on the sum of `support_mask` on one device may be relied on, other than what follows from the above.
Results may differ from a plain program's by a relative error of at most 0.015.
Values may be sent and summed in bfloat16 or wider, within the bound.
No kernel may reach another device: no remote copies, remote signals or barrier semaphores. Data moves between devices by JAX's collectives and lax.ppermute only.
A program may use at most 128 MiB of HBM per device.

v0:
```python
import functools
import math

import jax
import jax.numpy as jnp
import numpy as np
from jax import lax
from jax.experimental import pallas as pl
from jax.experimental.pallas import tpu as pltpu
from jax.sharding import PartitionSpec as P


LANES = 128
WIDE = 2 * LANES
BAND_ROWS = 224
primal_step = 0.5
dual_step = 0.5
radius = 6.0
weight_unit = 0.25


def whole_block(shape):
    zeros = (0,) * len(shape)
    return pl.BlockSpec(tuple(shape), lambda *_: zeros)


def in_scalar_memory():
    return pl.BlockSpec(memory_space=pltpu.SMEM)


def exact_dot(left, right):
    return jnp.dot(left, right, preferred_element_type=jnp.float32)


def each(count, body):
    if count <= 8:
        for index in range(count):
            body(index)
    else:

        def step(index, carry):
            body(index)
            return carry

        lax.fori_loop(0, count, step, 0)


def hint(value, multiple):
    return value if isinstance(value, int) else pl.multiple_of(value, multiple)


def band_seed(taps, basis, positions):
    lane = lax.broadcasted_iota(jnp.int32, (8, WIDE), 1)
    row = lax.broadcasted_iota(jnp.int32, (8, WIDE), 0)
    offset = lane - row & WIDE - 1
    seed = jnp.zeros((8, WIDE), jnp.float32)
    for tap, position in enumerate(positions):
        seed = jnp.where(offset == position % WIDE, taps[basis, tap], seed)
    return seed


def fill_band(target, first_row, rows, seed):
    for start in range(0, rows, 16):
        upper = seed if start == 0 else pltpu.roll(seed, start, axis=1)
        lower = pltpu.roll(seed, start + 8, axis=1)
        target[first_row + start : first_row + start + 16, :] = jnp.concatenate(
            [upper, lower], axis=0
        ).astype(jnp.bfloat16)


def fill_col_bands(target, taps, bases, margin):
    for basis in range(bases):
        count = taps.shape[1]
        seed = band_seed(taps, basis, [tap - margin for tap in range(count)])
        fill_band(target, basis * LANES, LANES, seed)


def pack_height(rows):
    return -(-rows // (8 * 16)) * 16


def payload_rows(rows):
    return rows + pack_height(rows)


def row_groups(rows):
    height = pack_height(rows)
    return [(g, g * height, min(height, rows - g * height)) for g in range(-(-rows // height))]


def padded_rows(strip_rows):
    chunks = -(-strip_rows // BAND_ROWS)
    return (chunks - 1) * BAND_ROWS + WIDE


def edge_band_of(taps, basis, margin):
    halo = 2 * margin
    lane = lax.broadcasted_iota(jnp.int32, (halo, LANES), 1)
    row = lax.broadcasted_iota(jnp.int32, (halo, LANES), 0)
    source = jnp.where(
        row < margin,
        jnp.where(lane < 2 * halo, halo + row - lane, -1),
        jnp.where(lane >= 2 * halo, row + 3 * halo - lane, -1),
    )
    edge = jnp.zeros((halo, LANES), jnp.float32)
    for tap in range(taps.shape[1]):
        edge = jnp.where(source == tap, taps[basis, tap], edge)
    return edge


def products(far_re, far_im, near_re, near_im):
    return (
        (far_re * near_re - far_im * near_im).astype(jnp.bfloat16),
        (far_re * near_im + far_im * near_re).astype(jnp.bfloat16),
    )


def fill_transforms(seeds, cosine, sine, freq):
    big_re, big_im, small_re, small_im, even_re, even_im = seeds
    split = lax.axis_index("split")
    coarse = small_re.shape[0]
    half = cosine.shape[0]
    part = half // 2

    def even_rows(group, carry):
        at = pl.ds(pl.multiple_of(group * coarse, coarse), coarse)
        one = pl.ds(group, 1)
        cosine[at, :], sine[at, :] = products(
            even_re[one, :], even_im[one, :], even_re[half // coarse :, :], even_im[half // coarse :, :]
        )
        return carry

    lax.fori_loop(0, half // coarse, even_rows, 0)

    def freq_rows(group, carry):
        at = pl.ds(pl.multiple_of(group * coarse, coarse), coarse)
        one = pl.ds(group, 1)
        for place in range(2):
            side = jnp.where(split == place, 0, 1) * part
            lanes = pl.ds(pl.multiple_of(side, part), part)
            re, im = products(
                big_re[one, lanes], big_im[one, lanes], small_re[:, lanes], small_im[:, lanes]
            )
            freq[at, 2 * place * part : (2 * place + 1) * part] = re
            freq[at, (2 * place + 1) * part : (2 * place + 2) * part] = im
        return carry

    lax.fori_loop(0, 2 * half // coarse, freq_rows, 0)


def fill_adjoint_bands(row_taps, col_taps, row_band, edge_band, col_band, margin):
    bases, taps = row_taps.shape
    for basis in range(bases):
        seed = band_seed(row_taps, basis, [3 * margin - tap for tap in range(taps)])
        fill_band(row_band.at[basis], 0, BAND_ROWS, seed)
        edge_band[basis] = edge_band_of(row_taps, basis, margin).astype(jnp.bfloat16)
    fill_col_bands(col_band, col_taps, bases, margin)


def is_at_ends(facet_rows):
    split = lax.axis_index("split")
    facet_row = lax.rem(lax.axis_index("chan"), facet_rows)
    return (facet_row == 0) & (split == 0), (facet_row == facet_rows - 1) & (split == 1)


def adjoint_of(tall, bands, mixed, wide, strip_rows, margin):
    row_band, edge_band, col_band = bands
    bases = tall.shape[0]
    width = tall.shape[2] // LANES
    halo = 2 * margin
    for basis in range(bases):
        into = slice(basis * LANES, (basis + 1) * LANES)

        def put(first, count, value):
            for side in range(width):
                mixed[side, first : first + count, into] = value[
                    :, side * LANES : (side + 1) * LANES
                ].astype(jnp.bfloat16)

        for first in range(0, strip_rows, BAND_ROWS):
            count = min(BAND_ROWS, strip_rows - first)
            put(first, count, exact_dot(row_band[basis, :count], tall[basis, first : first + WIDE]))
        ends = jnp.concatenate(
            [
                tall[basis, : 2 * halo],
                tall[basis, strip_rows : strip_rows + 2 * halo],
                jnp.zeros((LANES - 4 * halo, width * LANES), jnp.bfloat16),
            ],
            axis=0,
        )
        put(strip_rows, halo, exact_dot(edge_band[basis], ends))
    for side in range(width):
        wide[side] = exact_dot(mixed[side], col_band[...])


def write_payload(out, wide, margin):
    rows = wide.shape[0]
    height = pack_height(rows)
    packed = jnp.zeros((height, LANES), jnp.float32)
    for group, first, count in row_groups(rows):
        out[first : first + count, :] = wide[first : first + count, :LANES].astype(jnp.bfloat16)
        piece = wide[first : first + count, LANES:]
        piece = pltpu.roll(piece, margin + 2 * margin * group, axis=1)
        if count < height:
            piece = jnp.concatenate(
                [piece, jnp.zeros((height - count, LANES), jnp.float32)], axis=0
            )
        packed = packed + piece
    out[rows : rows + height, :] = packed.astype(jnp.bfloat16)


def tall_height(strip_rows, margin):
    return max(padded_rows(strip_rows), strip_rows + 4 * margin)


def band_scratch(bases, margin):
    return [
        pltpu.VMEM((bases, BAND_ROWS, WIDE), jnp.bfloat16),
        pltpu.VMEM((bases, 2 * margin, LANES), jnp.bfloat16),
        pltpu.VMEM((bases * LANES, WIDE), jnp.bfloat16),
    ]


def all_adjoint_kernel(row_taps, col_taps, dual, above, below, out, *scratch, margin, facet_rows):
    bands, (tall, mixed, wide) = scratch[:3], scratch[3:]
    bases, width, strip_rows, _ = dual.shape
    halo = 2 * margin

    @pl.when(pl.program_id(0) == 0)
    def _():
        fill_adjoint_bands(row_taps, col_taps, *bands, margin)
        tall[...] = jnp.zeros(tall.shape, tall.dtype)

    is_top, is_low = is_at_ends(facet_rows)
    for basis in range(bases):
        for side in range(width):
            lanes = slice(side * LANES, (side + 1) * LANES)
            top = above[basis, side]
            low = below[basis, side]
            tall[basis, :halo, lanes] = jnp.where(is_top, jnp.zeros_like(top), top)
            tall[basis, halo : halo + strip_rows, lanes] = dual[basis, side]
            tall[basis, halo + strip_rows : 2 * halo + strip_rows, lanes] = jnp.where(
                is_low, jnp.zeros_like(low), low
            )
    adjoint_of(tall, bands, mixed, wide, strip_rows, margin)
    for side in range(width):
        write_payload(out.at[side], wide.at[side], margin)


def all_adjoint(dual, above, below, row_taps, col_taps, facet_rows):
    bases, count, strip_rows, _ = dual.shape
    margin = row_taps.shape[1] // 2
    width = 2 if count % 2 == 0 else 1
    rows = strip_rows + 2 * margin

    def picked(height):
        return pl.BlockSpec((bases, width, height, LANES), lambda j: (0, j, 0, 0))

    return pl.pallas_call(
        functools.partial(all_adjoint_kernel, margin=margin, facet_rows=facet_rows),
        out_shape=jax.ShapeDtypeStruct((count, payload_rows(rows), LANES), jnp.bfloat16),
        grid=(count // width,),
        in_specs=[in_scalar_memory()] * 2
        + [picked(height) for height in (strip_rows, 2 * margin, 2 * margin)],
        out_specs=pl.BlockSpec((width, payload_rows(rows), LANES), lambda j: (j, 0, 0)),
        scratch_shapes=band_scratch(bases, margin)
        + [
            pltpu.VMEM((bases, tall_height(strip_rows, margin), width * LANES), jnp.bfloat16),
            pltpu.VMEM((width, rows, bases * LANES), jnp.bfloat16),
            pltpu.VMEM((width, rows, WIDE), jnp.float32),
        ],
        name="all_adjoint",
    )(row_taps, col_taps, dual, above, below)


def part_scratch(bases, strip_rows, margin, count):
    rows = strip_rows + 2 * margin
    height = tall_height(strip_rows, margin)
    return band_scratch(bases, margin) + [
        pltpu.VMEM((-(-count // 2), bases, height, 2 * LANES), jnp.bfloat16),
        pltpu.VMEM((2, rows, bases * LANES), jnp.bfloat16),
        pltpu.VMEM((2, rows, WIDE), jnp.float32),
        pltpu.VMEM((count, payload_rows(rows), LANES), jnp.bfloat16),
        pltpu.SemaphoreType.DMA((3 * count,)),
        pltpu.SemaphoreType.DMA((count,)),
    ]


class PartAdjoint:
    def __init__(self, places, dual, above, below, outs, scratch, facet_rows):
        *self.bands, self.tall, self.mixed, self.wide, self.held, loads, self.stores = scratch
        self.places, self.outs = places, outs
        self.strip_rows = dual.shape[2]
        self.halo = above.shape[2]
        self.margin = self.halo // 2
        self.ends = is_at_ends(facet_rows)
        me = lax.axis_index("chan")
        self.copies = []
        for at, place in enumerate(places):
            lanes = pl.ds(at % 2 * LANES, LANES)
            group = []
            for source, first, height in (
                (dual, self.halo, self.strip_rows),
                (above, 0, self.halo),
                (below, self.halo + self.strip_rows, self.halo),
            ):
                group.append(
                    pltpu.make_async_copy(
                        source.at[:, me ^ place],
                        self.tall.at[at // 2, :, pl.ds(first, height), lanes],
                        loads.at[3 * at + len(group)],
                    )
                )
            self.copies.append(group)

    def start(self):
        for group in self.copies:
            for copy in group:
                copy.start()

    def fill(self, row_taps, col_taps):
        fill_adjoint_bands(row_taps, col_taps, *self.bands, self.margin)
        used = self.strip_rows + 2 * self.halo
        pairs, bases, height, lanes = self.tall.shape
        if used < height:
            blank = jnp.zeros((height - used, lanes), jnp.bfloat16)
            for pair in range(pairs):
                for basis in range(bases):
                    self.tall[pair, basis, used:] = blank

    def run(self):
        stores = []
        halo, strip_rows = self.halo, self.strip_rows
        bases, lanes = self.tall.shape[1], self.tall.shape[3]
        for pair in range(len(self.places) // 2):
            for group in self.copies[2 * pair : 2 * pair + 2]:
                for copy in group:
                    copy.wait()
            blank = jnp.zeros((halo, lanes), jnp.bfloat16)
            for condition, first in zip(self.ends, (0, halo + strip_rows)):

                @pl.when(condition)
                def _(first=first):
                    for basis in range(bases):
                        self.tall[pair, basis, first : first + halo] = blank

            adjoint_of(
                self.tall.at[pair], self.bands, self.mixed, self.wide, strip_rows, self.margin
            )
            for side in range(2):
                at = 2 * pair + side
                write_payload(self.held.at[at], self.wide.at[side], self.margin)
                stores.append(
                    pltpu.make_async_copy(self.held.at[at], self.outs[at], self.stores.at[at])
                )
                stores[-1].start()
        return stores


def far_adjoint_kernel(row_taps, col_taps, dual, above, below, *rest, places, facet_rows):
    count = len(places)
    part = PartAdjoint(places, dual, above, below, rest[:count], rest[count:], facet_rows)
    part.start()
    part.fill(row_taps, col_taps)
    for copy in part.run():
        copy.wait()


def far_adjoint(dual, above, below, row_taps, col_taps, places, facet_rows):
    bases, _, strip_rows, _ = dual.shape
    margin = row_taps.shape[1] // 2
    anywhere = pl.BlockSpec(memory_space=pl.ANY)
    rows = payload_rows(strip_rows + 2 * margin)
    return pl.pallas_call(
        functools.partial(far_adjoint_kernel, places=places, facet_rows=facet_rows),
        out_shape=[jax.ShapeDtypeStruct((rows, LANES), jnp.bfloat16)] * len(places),
        in_specs=[in_scalar_memory()] * 2 + [anywhere] * 3,
        out_specs=[anywhere] * len(places),
        scratch_shapes=part_scratch(bases, strip_rows, margin, len(places)),
        name="far_adjoint",
    )(row_taps, col_taps, dual, above, below)


def phase_seeds(pixels):
    step = 2.0 * math.pi / pixels
    coarse = 32
    half = pixels // 2
    scale = 1.0 / math.sqrt(pixels)
    where = np.arange(half)

    def of(rows, factor):
        angle = rows[:, None] * where[None, :] % pixels * step
        return np.cos(angle) * factor, -np.sin(angle) * factor

    big = of(np.arange(pixels // coarse) * coarse, 1.0)
    small = of(np.arange(coarse), scale)
    far = of(np.arange(half // coarse) * coarse * 2, 1.0)
    near = of(np.arange(coarse) * 2, scale)
    even = tuple(np.concatenate([x, y], axis=0) for x, y in zip(far, near))
    return tuple(np.asarray(v, np.float32) for v in (*big, *small, *even))


def twiddles(pixels):
    angle = 2.0 * math.pi / pixels * np.arange(pixels // 2)[:, None] * np.ones((1, LANES))
    return tuple(np.asarray(v, np.float32) for v in (np.cos(angle), -np.sin(angle)))


def spectrum_kernel(
    row_taps, col_taps, dual, above, below, own, other, own_counts, other_counts, *rest,
    places, margin, facet_rows,
):
    seeds, (turn_from_re, turn_from_im, _) = rest[:6], rest[6:9]
    near_outs, rest = rest[9 : 9 + len(places)], rest[9 + len(places) :]
    freq_out, keep, send = rest[:3]
    (
        picture, counts, cosine, sine, freq, turn_re, turn_im, top, low, whole, wide, loads
    ) = rest[3:15]
    split = lax.axis_index("split")
    cols, _, strip_rows, _ = own.shape
    pixels = picture.shape[0]
    half = pixels // 2
    part = half // 2
    if places:
        near = PartAdjoint(places, dual, above, below, near_outs, rest[15:], facet_rows)
        near.start()

    def strip_at(facet_row, which):
        return pl.multiple_of((2 * facet_row + which) * strip_rows, strip_rows)

    copies = []
    for facet_row in range(facet_rows):
        for col in range(cols):
            lanes = pl.ds(col * LANES, LANES)
            for source, which in ((own, split), (other, 1 - split)):
                copies.append(
                    pltpu.make_async_copy(
                        source.at[col, facet_row],
                        picture.at[pl.ds(strip_at(facet_row, which), strip_rows), lanes],
                        loads.at[len(copies)],
                    )
                )
    for source, target in ((turn_from_re, turn_re), (turn_from_im, turn_im)):
        copies.append(pltpu.make_async_copy(source, target, loads.at[len(copies)]))
    count_copies = []
    for source, which in ((own_counts, split), (other_counts, 1 - split)):
        for tile in range(part // LANES):
            lanes = pl.ds(pl.multiple_of(split * part + tile * LANES, LANES), LANES)
            count_copies.append(
                pltpu.make_async_copy(
                    source.at[:, lanes],
                    counts.at[tile, pl.ds(pl.multiple_of(which * half, half), half), :],
                    loads.at[len(copies) + len(count_copies)],
                )
            )
    for copy in (*copies, *count_copies):
        copy.start()
    if places:
        near.fill(row_taps, col_taps)
    fill_transforms(seeds, cosine, sine, freq)
    stores = [
        pltpu.make_async_copy(freq, freq_out, loads.at[len(copies) + len(count_copies)])
    ]
    stores[0].start()
    if places:
        stores += near.run()
    for copy in copies:
        copy.wait()
    block = min(256, half)
    first_table = freq.at[:, pl.ds(0, half)]

    def first(step, carry):
        at = pl.ds(pl.multiple_of(step * block, block), block)
        beyond = pl.ds(pl.multiple_of(half + step * block, block), block)
        one = exact_dot(picture[at, :], first_table[...])
        two = exact_dot(picture[beyond, :], first_table[...])
        total = one + two
        apart = one - two
        re, im = apart[:, :part], apart[:, part:]
        turn_r = jnp.concatenate([turn_re[at, :]] * (part // LANES), axis=1)
        turn_i = jnp.concatenate([turn_im[at, :]] * (part // LANES), axis=1)
        odd_re = (re * turn_r - im * turn_i).astype(jnp.bfloat16)
        odd_im = (re * turn_i + im * turn_r).astype(jnp.bfloat16)
        sum_re = total[:, :part].astype(jnp.bfloat16)
        sum_im = total[:, part:].astype(jnp.bfloat16)
        for place, value in enumerate((sum_re, sum_im, odd_re, odd_im)):
            top[at, place * part : (place + 1) * part] = value
        for place, value in enumerate((-sum_im, sum_re, -odd_im, odd_re)):
            low[at, place * part : (place + 1) * part] = value
        return carry

    lax.fori_loop(0, half // block, first, 0)
    for copy in count_copies:
        copy.wait()

    def second(step, carry):
        at = pl.ds(pl.multiple_of(step * block, block), block)
        vis = exact_dot(cosine[at, :], top[...]) + exact_dot(sine[at, :], low[...])
        for parity in range(2):
            picked = jnp.concatenate(
                [
                    counts.at[tile][pl.ds(2 * step * block + parity, block, stride=2), :]
                    for tile in range(part // LANES)
                ],
                axis=1,
            )
            scale = weight_unit * picked.astype(jnp.float32)
            re = parity * 2 * part
            im = re + part
            whole[at, re : re + part] = (vis[:, re : re + part] * scale).astype(jnp.bfloat16)
            whole[at, im : im + part] = (vis[:, im : im + part] * scale).astype(jnp.bfloat16)
        return carry

    lax.fori_loop(0, half // block, second, 0)
    for parity in range(2):
        re = slice(parity * 2 * part, (parity * 2 + 1) * part)
        im = slice((parity * 2 + 1) * part, (parity * 2 + 2) * part)
        low[:, re] = whole[:, im]
        low[:, im] = -whole[:, re]

    def third(step, carry):
        at = pl.ds(pl.multiple_of(step * block, block), block)
        beyond = pl.ds(pl.multiple_of(half + step * block, block), block)
        value = exact_dot(cosine[at, :], whole[...]) + exact_dot(sine[at, :], low[...])
        even, re, im = value[:, :half], value[:, half : half + part], value[:, half + part :]
        turn_r = jnp.concatenate([turn_re[at, :]] * (part // LANES), axis=1)
        turn_i = jnp.concatenate([turn_im[at, :]] * (part // LANES), axis=1)
        odd = jnp.concatenate([re * turn_r + im * turn_i, im * turn_r - re * turn_i], axis=1)
        wide[at, :] = (even + odd).astype(jnp.bfloat16)
        wide[beyond, :] = (even - odd).astype(jnp.bfloat16)
        return carry

    lax.fori_loop(0, half // block, third, 0)
    rows = strip_rows + 2 * margin
    for facet_row in range(facet_rows):
        for target, which in ((keep, split), (send, 1 - split)):
            at = strip_at(facet_row, which)
            base = facet_row * rows
            target[base : base + strip_rows, :] = wide[pl.ds(at, strip_rows), :]
            before = pl.multiple_of(lax.rem(at + pixels - 16, pixels), 16)
            after = pl.multiple_of(lax.rem(at + strip_rows, pixels), 16)
            ends = jnp.concatenate(
                [
                    wide[pl.ds(before, 16), :].astype(jnp.float32)[16 - margin :],
                    wide[pl.ds(after, 16), :].astype(jnp.float32)[:margin],
                ],
                axis=0,
            )
            target[base + strip_rows : base + rows, :] = ends.astype(jnp.bfloat16)
    for copy in stores:
        copy.wait()


def spectrum(
    own, other, own_counts, other_counts, dual, above, below, row_taps, col_taps, places, margin, after
):
    cols, facet_rows, strip_rows, lanes = own.shape
    bases = dual.shape[0]
    pixels = cols * lanes
    half = pixels // 2
    rows = facet_rows * (strip_rows + 2 * margin)
    shape = jax.ShapeDtypeStruct((rows, half), jnp.bfloat16)
    anywhere = pl.BlockSpec(memory_space=pl.ANY)
    inside = pl.BlockSpec(memory_space=pltpu.VMEM)
    payload = jax.ShapeDtypeStruct((payload_rows(strip_rows + 2 * margin), lanes), jnp.bfloat16)
    result = pl.pallas_call(
        functools.partial(
            spectrum_kernel, places=places, margin=margin, facet_rows=facet_rows
        ),
        out_shape=[payload] * len(places)
        + [jax.ShapeDtypeStruct((pixels, pixels), jnp.bfloat16), shape, shape],
        in_specs=[in_scalar_memory()] * 2 + [anywhere] * 7 + [inside] * 6 + [anywhere] * 3,
        out_specs=[anywhere] * (len(places) + 1) + [inside] * 2,
        scratch_shapes=[
            pltpu.VMEM((pixels, pixels), jnp.bfloat16),
            pltpu.VMEM((half // 2 // LANES, pixels, LANES), jnp.int32),
            pltpu.VMEM((half, half), jnp.bfloat16),
            pltpu.VMEM((half, half), jnp.bfloat16),
            pltpu.VMEM((pixels, pixels), jnp.bfloat16),
            pltpu.VMEM((half, LANES), jnp.float32),
            pltpu.VMEM((half, LANES), jnp.float32),
            pltpu.VMEM((half, pixels), jnp.bfloat16),
            pltpu.VMEM((half, pixels), jnp.bfloat16),
            pltpu.VMEM((half, pixels), jnp.bfloat16),
            pltpu.VMEM((pixels, half), jnp.bfloat16),
            pltpu.SemaphoreType.DMA((2 * cols * facet_rows + 3 + half // LANES,)),
        ]
        + (part_scratch(bases, strip_rows, margin, len(places)) if places else []),
        name="spectrum",
    )(
        row_taps, col_taps, dual, above, below, own, other, own_counts, other_counts,
        *phase_seeds(pixels), *twiddles(pixels), after,
    )
    return result[: len(places)], *result[len(places) :]


def gradient_kernel(
    kept, got, freq, own, above, below, own_dirty, dirty_above, dirty_below,
    stepped, edge_out, joined, *, margin
):
    split = lax.axis_index("split")
    cols, facet_rows, strip_rows, _ = own.shape
    half = kept.shape[1]
    rows = strip_rows + 2 * margin

    @pl.when(pl.program_id(0) == 0)
    def _():
        joined[:, :half] = kept[...]
        joined[:, half:] = got[...]

    def edges(upper, lower, col, facet_row):
        over = jnp.maximum(facet_row - 1 + split, 0)
        under = jnp.minimum(facet_row + split, facet_rows - 1)
        return jnp.concatenate(
            [
                upper[col, over].astype(jnp.float32)[16 - margin :],
                lower[col, under].astype(jnp.float32)[:margin],
            ],
            axis=0,
        )

    value = lax.dot_general(
        joined[...], freq[...], (((1,), (1,)), ((), ())), preferred_element_type=jnp.float32
    )
    for col in range(cols):
        for facet_row in range(facet_rows):
            base = facet_row * rows
            grad = value[base : base + rows, col * LANES : (col + 1) * LANES]
            image = own[col, facet_row]
            dirty = own_dirty[col, facet_row].astype(jnp.float32)
            moved = image.astype(jnp.float32) - primal_step * (grad[:strip_rows] - dirty)
            stepped[col, facet_row, :strip_rows] = moved.astype(jnp.bfloat16)
            image = edges(above, below, col, facet_row)
            dirty = edges(dirty_above, dirty_below, col, facet_row)
            moved = image - primal_step * (grad[strip_rows:] - dirty)
            stepped[col, facet_row, strip_rows:] = moved.astype(jnp.bfloat16)
            edge_out[col, facet_row] = image.astype(jnp.bfloat16)


def gradient_step(kept, got, freq, own, other, own_dirty, other_dirty, margin):
    cols, facet_rows, strip_rows, lanes = own.shape
    pixels = cols * lanes
    rows = strip_rows + 2 * margin
    pair = 2 if cols % 2 == 0 else 1

    def block(height, place):
        return pl.BlockSpec((pair, facet_rows, height, lanes), lambda j: (j, 0, place, 0))

    whole_strip, last, first = block(strip_rows, 0), block(16, strip_rows // 16 - 1), block(16, 0)
    return pl.pallas_call(
        functools.partial(gradient_kernel, margin=margin),
        out_shape=[
            jax.ShapeDtypeStruct((cols, facet_rows, rows, lanes), jnp.bfloat16),
            jax.ShapeDtypeStruct((cols, facet_rows, 2 * margin, lanes), jnp.bfloat16),
        ],
        grid=(cols // pair,),
        in_specs=[
            whole_block(kept.shape),
            whole_block(got.shape),
            pl.BlockSpec((pair * lanes, pixels), lambda j: (j, 0)),
            whole_strip, last, first, whole_strip, last, first,
        ],
        out_specs=[block(rows, 0), block(2 * margin, 0)],
        scratch_shapes=[pltpu.VMEM((kept.shape[0], pixels), jnp.bfloat16)],
        name="gradient",
    )(kept, got, freq, own, other, other, own_dirty, other_dirty, other_dirty)


def unpacked(packed, group, count, margin):
    return pltpu.roll(
        packed[:count], LANES - (margin + 2 * margin * group) % LANES, axis=1
    )


def update_kernel(stepped_from, image_from, edges, *rest, margin, facets, single):
    arrivals = 1 if single else facets
    blocks = rest[:arrivals]
    new_out = rest[arrivals]
    outs = rest[arrivals + 1 : 2 * arrivals + 1]
    stepped, image, new_image, adjoint, extrapolated, leaving, loads, arriving, stores = rest[
        2 * arrivals + 1 :
    ]
    me = lax.axis_index("chan")
    split = lax.axis_index("split")
    cols, facet_rows, rows, _ = stepped.shape
    strip_rows = rows - 2 * margin
    height = pack_height(rows)
    lane = lax.broadcasted_iota(jnp.int32, (1, LANES), 1)
    arrive = []
    for place, block in enumerate(blocks):
        target = adjoint if single else adjoint.at[me ^ place]
        arrive.append(pltpu.make_async_copy(block, target, arriving.at[place]))
        arrive[-1].start()
    load = []
    for col in range(cols):
        load.append(
            (
                pltpu.make_async_copy(stepped_from.at[col], stepped.at[col], loads.at[2 * col]),
                pltpu.make_async_copy(image_from.at[col], image.at[col], loads.at[2 * col + 1]),
            )
        )
        for copy in load[-1]:
            copy.start()
    for copy in arrive:
        copy.wait()

    def sides(take, group, count, left, has_left, right, has_right):
        from_left = take(left, group, count)
        from_right = take(right, group, count)
        return (
            jnp.where(lane < jnp.where(has_left, margin, 0), from_left, 0.0),
            jnp.where(lane >= jnp.where(has_right, LANES - margin, LANES), from_right, 0.0),
        )

    def packed_of(facet, group, count):
        tile = adjoint[facet, rows : rows + height, :].astype(jnp.float32)
        return unpacked(tile, group, count, margin)

    def update(facet):
        col = facet // facet_rows
        facet_row = facet % facet_rows
        left, has_left = jnp.maximum(facet - facet_rows, 0), facet >= facet_rows
        right, has_right = jnp.minimum(facet + facet_rows, facets - 1), facet < facets - facet_rows
        for group, first, count in row_groups(rows):
            add_left, add_right = sides(packed_of, group, count, left, has_left, right, has_right)
            at = slice(first, first + count)
            total = adjoint[facet, at, :].astype(jnp.float32) + add_left + add_right
            value = stepped[col, facet_row, at, :].astype(jnp.float32) - primal_step * total
            value = jnp.maximum(value, 0.0).astype(jnp.bfloat16).astype(jnp.float32)
            main = max(min(first + count, strip_rows) - first, 0)
            before = []
            if main > 0:
                before.append(image[col, facet_row, first : first + main, :].astype(jnp.float32))
            if main < count:
                after = first + main - strip_rows
                before.append(
                    edges[col, facet_row, after : after + count - main, :].astype(jnp.float32)
                )
            ahead = 2.0 * value - (before[0] if len(before) == 1 else jnp.concatenate(before, 0))
            if first + count > strip_rows:
                row = first + lax.broadcasted_iota(jnp.int32, (count, LANES), 0)
                top_there = (facet_row > 0) | (split > 0)
                low_there = (facet_row < facet_rows - 1) | (split < 1)
                middle = strip_rows + margin
                from_top = jnp.where(top_there, middle, strip_rows)
                to_low = jnp.where(low_there, rows, middle)
                ahead = jnp.where((row >= from_top) & (row < middle), 0.0, ahead)
                ahead = jnp.where(row >= to_low, 0.0, ahead)
            extrapolated[facet, at, :] = ahead.astype(jnp.bfloat16)
            if main > 0:
                new_image[col, facet_row, first : first + main, :] = value[:main].astype(jnp.bfloat16)

    stored = []
    for col in range(cols):
        for copy in load[col]:
            copy.wait()
        for facet_row in range(facet_rows):
            update(col * facet_rows + facet_row)
        stored.append(
            pltpu.make_async_copy(new_image.at[col], new_out.at[col], stores.at[col])
        )
        stored[-1].start()

    def whole_of(facet, group, count):
        first = group * height
        return extrapolated[facet, first : first + count, :].astype(jnp.float32)

    def write(out, facet):
        left, has_left = jnp.maximum(facet - facet_rows, 0), facet >= facet_rows
        right, has_right = jnp.minimum(facet + facet_rows, facets - 1), facet < facets - facet_rows
        packed = jnp.zeros((height, LANES), jnp.float32)
        for group, first, count in row_groups(rows):
            after, before = sides(whole_of, group, count, right, has_right, left, has_left)
            side = pltpu.roll(after + before, margin + 2 * margin * group, axis=1)
            if count < height:
                side = jnp.concatenate(
                    [side, jnp.zeros((height - count, LANES), jnp.float32)], axis=0
                )
            packed = packed + side
        out[:rows, :] = extrapolated[facet]
        out[rows:, :] = packed.astype(jnp.bfloat16)

    if single:
        each(facets, lambda facet: write(leaving.at[facet], facet))
        stored.append(pltpu.make_async_copy(leaving, outs[0], stores.at[cols]))
        stored[-1].start()
    else:
        for place in reversed(range(facets)):
            write(leaving.at[place], me ^ place)
            stored.append(
                pltpu.make_async_copy(leaving.at[place], outs[place], stores.at[cols + place])
            )
            stored[-1].start()
    for copy in stored:
        copy.wait()


def update_step(stepped, image, edges, blocks, margin, single):
    cols, facet_rows, rows, lanes = stepped.shape
    facets = cols * facet_rows
    tall_rows = payload_rows(rows)
    arrivals = (
        [jax.ShapeDtypeStruct((facets, tall_rows, lanes), jnp.bfloat16)]
        if single
        else [jax.ShapeDtypeStruct((tall_rows, lanes), jnp.bfloat16)] * facets
    )
    anywhere = pl.BlockSpec(memory_space=pl.ANY)
    results = pl.pallas_call(
        functools.partial(update_kernel, margin=margin, facets=facets, single=single),
        out_shape=[
            jax.ShapeDtypeStruct((cols, facet_rows, rows - 2 * margin, lanes), jnp.bfloat16)
        ]
        + arrivals,
        in_specs=[anywhere] * 2 + [pl.BlockSpec(memory_space=pltpu.VMEM)] + [anywhere] * len(blocks),
        out_specs=[anywhere] * (1 + len(arrivals)),
        scratch_shapes=[
            pltpu.VMEM(stepped.shape, jnp.bfloat16),
            pltpu.VMEM(image.shape, jnp.bfloat16),
            pltpu.VMEM(image.shape, jnp.bfloat16),
            pltpu.VMEM((facets, tall_rows, lanes), jnp.bfloat16),
            pltpu.VMEM((facets, rows, lanes), jnp.bfloat16),
            pltpu.VMEM((facets, tall_rows, lanes), jnp.bfloat16),
            pltpu.SemaphoreType.DMA((2 * cols,)),
            pltpu.SemaphoreType.DMA((len(blocks),)),
            pltpu.SemaphoreType.DMA((cols + len(blocks),)),
        ],
        name="update",
    )(stepped, image, edges, *blocks)
    return results[0], results[1:]


def shrink_kernel(row_taps, col_taps, mask, dual, *rest, margin, channels, single):
    arrivals = 1 if single else channels
    blocks = rest[:arrivals]
    out = rest[arrivals]
    row_band, col_band, wide, tall = rest[arrivals + 1 :]
    me = lax.axis_index("chan")
    basis = pl.program_id(0)
    taps = row_taps.shape[1]
    halo = 2 * margin
    strip_rows = dual.shape[2]
    rows = strip_rows + halo
    height = pack_height(rows)

    @pl.when(basis == 0)
    def _():
        for each_basis in range(row_taps.shape[0]):
            seed = band_seed(row_taps, each_basis, [margin + tap for tap in range(taps)])
            fill_band(row_band.at[each_basis], 0, BAND_ROWS, seed)
            seed = band_seed(col_taps, each_basis, [tap - margin for tap in range(taps)])
            fill_band(col_band.at[each_basis], 0, LANES, seed)
        tall[...] = jnp.zeros(tall.shape, tall.dtype)

        def unpack(channel, block):
            wide[channel, :, :LANES] = block[:rows, :]
            packed = block[rows : rows + height, :].astype(jnp.float32)
            for group, first, count in row_groups(rows):
                side = unpacked(packed, group, count, margin)
                wide[channel, first : first + count, LANES:] = side.astype(jnp.bfloat16)

        if single:
            each(channels, lambda channel: unpack(channel, blocks[0].at[channel]))
        else:
            for place, block in enumerate(blocks):
                unpack(me ^ place, block)

    def columns(channel):
        lanes = pl.ds(hint(channel * LANES, LANES), LANES)
        value = lax.dot_general(
            wide[channel], col_band[basis], (((1,), (1,)), ((), ())),
            preferred_element_type=jnp.float32,
        )
        blank = jnp.zeros((halo - margin, LANES), jnp.float32)
        tall[halo : halo + strip_rows, lanes] = value[:strip_rows].astype(jnp.bfloat16)
        tall[:halo, lanes] = jnp.concatenate(
            [blank, value[strip_rows : strip_rows + margin]], axis=0
        ).astype(jnp.bfloat16)
        tall[halo + strip_rows : 2 * halo + strip_rows, lanes] = jnp.concatenate(
            [value[strip_rows + margin :], blank], axis=0
        ).astype(jnp.bfloat16)

    each(channels, columns)
    piece = min(channels, 8)
    for first in range(0, strip_rows, BAND_ROWS):
        count = min(BAND_ROWS, strip_rows - first)
        stepped = []
        total = jnp.zeros((count, LANES), jnp.float32)
        for channel in range(0, channels, piece):
            value = exact_dot(
                row_band[basis, :count],
                tall[first : first + WIDE, channel * LANES : (channel + piece) * LANES],
            )
            for side in range(piece):
                coefficient = value[:, side * LANES : (side + 1) * LANES]
                moved = (
                    dual[0, channel + side, first : first + count].astype(jnp.float32)
                    + dual_step * coefficient
                )
                stepped.append(moved)
                total = total + moved * moved
        kept = mask[first : first + count].astype(jnp.float32)
        shrink = radius * kept / jnp.maximum(jnp.sqrt(total), radius)
        for channel in range(channels):
            out[0, channel, first : first + count] = (stepped[channel] * shrink).astype(jnp.bfloat16)


def shrink_step(row_taps, col_taps, mask, dual, blocks, single):
    bases, channels, strip_rows, lanes = dual.shape
    margin = row_taps.shape[1] // 2
    rows = strip_rows + 2 * margin
    return pl.pallas_call(
        functools.partial(shrink_kernel, margin=margin, channels=channels, single=single),
        out_shape=jax.ShapeDtypeStruct(dual.shape, jnp.bfloat16),
        grid=(bases,),
        in_specs=[
            in_scalar_memory(),
            in_scalar_memory(),
            whole_block(mask.shape),
            pl.BlockSpec((1, channels, strip_rows, lanes), lambda n: (n, 0, 0, 0)),
        ]
        + [whole_block(block.shape) for block in blocks],
        out_specs=pl.BlockSpec((1, channels, strip_rows, lanes), lambda n: (n, 0, 0, 0)),
        scratch_shapes=[
            pltpu.VMEM((bases, BAND_ROWS, WIDE), jnp.bfloat16),
            pltpu.VMEM((bases, LANES, WIDE), jnp.bfloat16),
            pltpu.VMEM((channels, rows, WIDE), jnp.bfloat16),
            pltpu.VMEM((max(padded_rows(strip_rows), strip_rows + 4 * margin), channels * lanes), jnp.bfloat16),
        ],
        name="shrink",
    )(row_taps, col_taps, mask, dual, *blocks)


def swapped(value):
    return lax.ppermute(value, "split", [(0, 1), (1, 0)])


def along_chain(value, by, facet_rows):
    count = lax.axis_size("chan") * 2
    chain = 2 * facet_rows
    pairs = [
        (i, i + by) for i in range(count) if 0 <= i + by < count and i // chain == (i + by) // chain
    ]
    return lax.ppermute(value, ("chan", "split"), pairs)


def crossed(blocks, single):
    count = lax.axis_size("chan")
    if single:
        return [lax.all_to_all(blocks[0], "chan", split_axis=0, concat_axis=0, tiled=True)]
    result = list(blocks)
    for place in reversed(range(1, count)):
        result[place] = lax.ppermute(blocks[place], "chan", [(i, i ^ place) for i in range(count)])
    return result


def in_parts(count):
    return 4 <= count <= 8 and count & count - 1 == 0


def per_device(sky_image, dirty_image, uv_weights, dual_coeffs, support_mask, row_taps, col_taps):
    facet_cols, facet_rows, strip_rows, lanes = (sky_image.shape[i] for i in (1, 2, 4, 5))
    bases, channels = dual_coeffs.shape[:2]
    margin = row_taps.shape[1] // 2
    count = lax.axis_size("chan")
    single = not in_parts(count)
    image = sky_image.reshape(facet_cols, facet_rows, strip_rows, lanes)
    dirty = dirty_image.reshape(image.shape)
    counts = uv_weights.reshape(uv_weights.shape[1:])
    dual = dual_coeffs.reshape(bases, channels, strip_rows, lanes)
    mask = support_mask.reshape(strip_rows, lanes)
    halo = 2 * margin
    top_rows, low_rows = dual[:, :, :halo], dual[:, :, strip_rows - halo :]
    if facet_rows == 1:
        ends = jnp.where(lax.axis_index("split") == 0, low_rows, top_rows)
        above = below = swapped(ends)
    else:
        above = along_chain(low_rows, 1, facet_rows)
        below = along_chain(top_rows, -1, facet_rows)
    other_image = swapped(image)
    other_counts = swapped(counts)
    other_dirty = swapped(dirty)
    if single:
        blocks = [all_adjoint(dual, above, below, row_taps, col_taps, facet_rows)]
        far, near = blocks, ()
    else:
        near = tuple(range(count // 2))
        far = far_adjoint(
            dual, above, below, row_taps, col_taps, tuple(range(count // 2, count)), facet_rows
        )
    close, freq, kept, sent = spectrum(
        image, other_image, counts, other_counts, dual, above, below,
        row_taps, col_taps, near, margin, far[0],
    )
    if not single:
        blocks = list(close) + list(far)
    arrived = crossed(blocks, single)
    got = swapped(sent)
    stepped, edges = gradient_step(
        kept, got, freq, image, other_image, dirty, other_dirty, margin
    )
    new_image, blocks = update_step(stepped, image, edges, arrived, margin, single)
    arrived = crossed(blocks, single)
    new_dual = shrink_step(row_taps, col_taps, mask, dual, arrived, single)
    return (new_image.reshape(sky_image.shape), new_dual.reshape(dual_coeffs.shape))


def solution(mesh):
    placed = (
        P(("cube", "chan"), None, None, "split", None, None),
        P(("cube", "chan"), None, None, "split", None, None),
        P(("cube", "chan"), "split", None),
        P(None, "cube", "chan", "split", None, None),
        P("chan", "split", None, None),
        P(),
        P(),
    )

    mapped = jax.shard_map(
        per_device,
        mesh=mesh,
        in_specs=placed,
        out_specs=(
            P(("cube", "chan"), None, None, "split", None, None),
            P(None, "cube", "chan", "split", None, None),
        ),
        check_vma=False,
    )
    count = mesh.shape["chan"]
    if not in_parts(count):
        return mapped
    return mapped
```

profile of v0, /device:TPU:8, one launch (start us, length us, event | category | flops | bytes accessed | tf_op | source)
XLA Modules:
  0.0 110.9 jit_solution(12530798698327811215)
XLA Ops:
  1.3 1.0 slice_select_fusion
  2.8 4.0 %collective-permute-done.above.below = bf16[4,8,16,128]{3,2,1,0:T(8,128)(2,1)S(1)} collective-permute-done((bf16[4,8,16,128]{3,2,1,0:T(8,128)(2,1)S(1)}, bf16[4,8,16,128]{3,2,1,0:T(8,128)(2,1)S(1)}, u32[]{:S(2)}, u32[]{:S(2)}) %collective-permute-start) | collective-permute-done | bytes 131104 | tf_op jit(solution)/shard_map/ppermute | solution.py:933
  7.4 4.9 %far_adjoint.1 = (bf16[608,128]{1,0:T(8,128)(2,1)}, bf16[608,128]{1,0:T(8,128)(2,1)}, bf16[608,128]{1,0:T(8,128)(2,1)}, bf16[608,128]{1,0:T(8,128)(2,1)}) custom-call(f32[4,17]{1,0:T(4,128)} %row_taps.5, f32[4,17]{1,0:T(4,128)} %col_taps.5, bf16[4,8,512,128]{3,2,1,0:T(8,128)(2,1)} %bitcast.12, bf16[4,8,16,128]{3,2,1,0:T(8,128)(2,1)} %copy-done.2, ...), custom_call_target="tpu_custom_call" | custom-call | tf_op jit(solution)/shard_map/far_adjoint/pallas_call | solution.py:374
  13.6 10.8 %spectrum.1 = (bf16[608,128]{1,0:T(8,128)(2,1)}, bf16[608,128]{1,0:T(8,128)(2,1)}, bf16[608,128]{1,0:T(8,128)(2,1)}, bf16[608,128]{1,0:T(8,128)(2,1)}, bf16[1024...) custom-call(f32[4,17]{1,0:T(4,128)} %row_taps.5, f32[4,17]{1,0:T(4,128)} %col_taps.5, ...), custom_call_target="tpu_custom_call" | custom-call | tf_op jit(solution)/shard_map/spectrum/pallas_call | solution.py:565
  24.7 2.6 %collective-permute-start.8 = (bf16[608,128]{1,0:T(8,128)(2,1)S(1)}, bf16[608,128]{1,0:T(8,128)(2,1)S(1)}, u32[]{:S(2)}, u32[]{:S(2)}) collective-permute-start(bf16[608,128]{1,0:T(8,128)(2,1)S(1)} %copy-done.5), channel_id=1, source_target_pairs={{0,8},{2,10},{4,12},{6,14},{8,0},{10,2},{12,4},{14,6},{1,9},{3,11}... | collective-permute-start | bytes 466952 | tf_op jit(solution)/shard_map/ppermute | solution.py:951
  27.2 3.0 %collective-permute-start.11 = (bf16[608,128]{1,0:T(8,128)(2,1)}, bf16[608,128]{1,0:T(8,128)(2,1)S(1)}, u32[]{:S(2)}, u32[]{:S(2)}) collective-permute-start(bf16[608,128]{1,0:T(8,128)(2,1)} %get-tuple-element.36), channel_id=1, source_target_pairs={{0,14},{2,12},{4,10},{6,8},{8,6},{10,4},{12,2},{14,0},{1,15},{3,13... | collective-permute-start | bytes 466952 | tf_op jit(solution)/shard_map/ppermute | solution.py:951
  30.2 10.8 %collective-permute-done.8.rest_4_ = bf16[608,128]{1,0:T(8,128)(2,1)S(1)} collective-permute-done((bf16[608,128]{1,0:T(8,128)(2,1)S(1)}, bf16[608,128]{1,0:T(8,128)(2,1)S(1)}, u32[]{:S(2)}, u32[]{:S(2)}) %collective-permute-start.8) | collective-permute-done | bytes 155680 | tf_op jit(solution)/shard_map/ppermute | solution.py:951
  41.0 4.3 %collective-permute-start.9 = (bf16[608,128]{1,0:T(8,128)(2,1)S(1)}, bf16[608,128]{1,0:T(8,128)(2,1)S(1)}, u32[]{:S(2)}, u32[]{:S(2)}) collective-permute-start(bf16[608,128]{1,0:T(8,128)(2,1)S(1)} %copy-done.20), channel_id=1, source_target_pairs={{0,10},{2,8},{4,14},{6,12},{8,2},{10,0},{12,6},{14,4},{1,11},{3,9}... | collective-permute-start | bytes 466952 | tf_op jit(solution)/shard_map/ppermute | solution.py:951
  45.4 2.4 %collective-permute-done.10.rest_6_ = bf16[608,128]{1,0:T(8,128)(2,1)S(1)} collective-permute-done((bf16[608,128]{1,0:T(8,128)(2,1)}, bf16[608,128]{1,0:T(8,128)(2,1)S(1)}, u32[]{:S(2)}, u32[]{:S(2)}) %collective-permute-start.10) | collective-permute-done | bytes 155680 | tf_op jit(solution)/shard_map/ppermute | solution.py:951
  47.8 1.5 %collective-permute-start.5 = (bf16[608,128]{1,0:T(8,128)(2,1)}, bf16[608,128]{1,0:T(8,128)(2,1)S(1)}, u32[]{:S(2)}, u32[]{:S(2)}) collective-permute-start(bf16[608,128]{1,0:T(8,128)(2,1)} %get-tuple-element.31), channel_id=1, source_target_pairs={{0,2},{2,0},{4,6},{6,4},{8,10},{10,8},{12,14},{14,12},{1,3},{3,1},... | collective-permute-start | bytes 466952 | tf_op jit(solution)/shard_map/ppermute | solution.py:951
  49.3 1.9 %collective-permute-start.7 = (bf16[608,128]{1,0:T(8,128)(2,1)}, bf16[608,128]{1,0:T(8,128)(2,1)S(1)}, u32[]{:S(2)}, u32[]{:S(2)}) collective-permute-start(bf16[608,128]{1,0:T(8,128)(2,1)} %get-tuple-element.33), channel_id=1, source_target_pairs={{0,6},{2,4},{4,2},{6,0},{8,14},{10,12},{12,10},{14,8},{1,7},{3,5},... | collective-permute-start | bytes 466952 | tf_op jit(solution)/shard_map/ppermute | solution.py:951
  51.3 5.4 %gradient.1 = (bf16[8,1,528,128]{3,2,1,0:T(8,128)(2,1)}, bf16[8,1,16,128]{3,2,1,0:T(8,128)(2,1)}) custom-call(bf16[528,512]{1,0:T(8,128)(2,1)} %get-tuple-element.25.kept, bf16[528,512]{1,0:T(8,128)(2,1)} %copy-done.4, bf16[1024,1024]{1,0:T(8,128)(2,1)} %get-tuple-element.27.freq, bf16[8,1,512,128]{3,2,1,0:T(8,128)(2,1)} %bitcast.17, ...), custom_call_target="tpu_custom_call" | custom-call | tf_op jit(solution)/shard_map/gradient/pallas_call | solution.py:649
  56.8 2.9 %collective-permute-done.7.rest_3_ = bf16[608,128]{1,0:T(8,128)(2,1)S(1)} collective-permute-done((bf16[608,128]{1,0:T(8,128)(2,1)}, bf16[608,128]{1,0:T(8,128)(2,1)S(1)}, u32[]{:S(2)}, u32[]{:S(2)}) %collective-permute-start.7) | collective-permute-done | bytes 155680 | tf_op jit(solution)/shard_map/ppermute | solution.py:951
  60.3 5.9 %update.1 = (bf16[8,1,512,128]{3,2,1,0:T(8,128)(2,1)}, bf16[608,128]{1,0:T(8,128)(2,1)}, bf16[608,128]{1,0:T(8,128)(2,1)}, bf16[608,128]{1,0:T(8,128)(2,1)}, bf1...) custom-call(bf16[8,1,528,128]{3,2,1,0:T(8,128)(2,1)} %get-tuple-elem, ...), custom_call_target="tpu_custom_call" | custom-call | tf_op jit(solution)/shard_map/update/pallas_call | solution.py:807
  66.9 3.2 %collective-permute-start.13 = (bf16[608,128]{1,0:T(8,128)(2,1)}, bf16[608,128]{1,0:T(8,128)(2,1)S(1)}, u32[]{:S(2)}, u32[]{:S(2)}) collective-permute-start(bf16[608,128]{1,0:T(8,128)(2,1)} %get-tuple-element.40), channel_id=1, source_target_pairs={{0,4},{2,6},{4,0},{6,2},{8,12},{10,14},{12,8},{14,10},{1,5},{3,7},... | collective-permute-start | bytes 466952 | tf_op jit(solution)/shard_map/ppermute | solution.py:951
  70.2 3.8 %collective-permute-start.15 = (bf16[608,128]{1,0:T(8,128)(2,1)}, bf16[608,128]{1,0:T(8,128)(2,1)S(1)}, u32[]{:S(2)}, u32[]{:S(2)}) collective-permute-start(bf16[608,128]{1,0:T(8,128)(2,1)} %get-tuple-element.42), channel_id=1, source_target_pairs={{0,8},{2,10},{4,12},{6,14},{8,0},{10,2},{12,4},{14,6},{1,9},{3,11}... | collective-permute-start | bytes 466952 | tf_op jit(solution)/shard_map/ppermute | solution.py:951
  75.0 1.5 %collective-permute-start.17 = (bf16[608,128]{1,0:T(8,128)(2,1)}, bf16[608,128]{1,0:T(8,128)(2,1)S(1)}, u32[]{:S(2)}, u32[]{:S(2)}) collective-permute-start(bf16[608,128]{1,0:T(8,128)(2,1)} %get-tuple-element.44), channel_id=1, source_target_pairs={{0,12},{2,14},{4,8},{6,10},{8,4},{10,6},{12,0},{14,2},{1,13},{3,15... | collective-permute-start | bytes 466952 | tf_op jit(solution)/shard_map/ppermute | solution.py:951
  76.5 3.7 %collective-permute-done.13.rest_2_ = bf16[608,128]{1,0:T(8,128)(2,1)S(1)} collective-permute-done((bf16[608,128]{1,0:T(8,128)(2,1)}, bf16[608,128]{1,0:T(8,128)(2,1)S(1)}, u32[]{:S(2)}, u32[]{:S(2)}) %collective-permute-start.13) | collective-permute-done | bytes 155680 | tf_op jit(solution)/shard_map/ppermute | solution.py:951
  80.2 2.0 %collective-permute-done.14.rest_3_ = bf16[608,128]{1,0:T(8,128)(2,1)S(1)} collective-permute-done((bf16[608,128]{1,0:T(8,128)(2,1)}, bf16[608,128]{1,0:T(8,128)(2,1)S(1)}, u32[]{:S(2)}, u32[]{:S(2)}) %collective-permute-start.14) | collective-permute-done | bytes 155680 | tf_op jit(solution)/shard_map/ppermute | solution.py:951
  82.2 9.8 %collective-permute-done.15.rest_4_ = bf16[608,128]{1,0:T(8,128)(2,1)S(1)} collective-permute-done((bf16[608,128]{1,0:T(8,128)(2,1)}, bf16[608,128]{1,0:T(8,128)(2,1)S(1)}, u32[]{:S(2)}, u32[]{:S(2)}) %collective-permute-start.15) | collective-permute-done | bytes 155680 | tf_op jit(solution)/shard_map/ppermute | solution.py:951
  92.1 3.3 %collective-permute-done.16.rest_5_ = bf16[608,128]{1,0:T(8,128)(2,1)S(1)} collective-permute-done((bf16[608,128]{1,0:T(8,128)(2,1)}, bf16[608,128]{1,0:T(8,128)(2,1)S(1)}, u32[]{:S(2)}, u32[]{:S(2)}) %collective-permute-start.16) | collective-permute-done | bytes 155680 | tf_op jit(solution)/shard_map/ppermute | solution.py:951
  95.4 2.9 %collective-permute-done.17.rest_6_ = bf16[608,128]{1,0:T(8,128)(2,1)S(1)} collective-permute-done((bf16[608,128]{1,0:T(8,128)(2,1)}, bf16[608,128]{1,0:T(8,128)(2,1)S(1)}, u32[]{:S(2)}, u32[]{:S(2)}) %collective-permute-start.17) | collective-permute-done | bytes 155680 | tf_op jit(solution)/shard_map/ppermute | solution.py:951
  98.3 2.8 %collective-permute-done.18.rest_7_ = bf16[608,128]{1,0:T(8,128)(2,1)S(1)} collective-permute-done((bf16[608,128]{1,0:T(8,128)(2,1)}, bf16[608,128]{1,0:T(8,128)(2,1)S(1)}, u32[]{:S(2)}, u32[]{:S(2)}) %collective-permute-start.18) | collective-permute-done | bytes 155680 | tf_op jit(solution)/shard_map/ppermute | solution.py:951
  101.7 9.2 %shrink.1 = bf16[4,8,512,128]{3,2,1,0:T(8,128)(2,1)} custom-call(f32[4,17]{1,0:T(4,128)} %row_taps.5, f32[4,17]{1,0:T(4,128)} %col_taps.5, s32[512,128]{1,0:T(8,128)} %bitcast.24, bf16[4,8,512,128]{3,2,1,0:T(8,128)(2,1)} %bitcast.14, bf16[608,128]{1,0:T(8,128)(2,1)} %get-tuple-element.38.rest_0_, bf16[608,128]{1,0:T(8,128)(2,1)} %copy-done.13, ...), custom_call_target="tpu_custom_call" | custom-call | tf_op jit(solution)/shard_map/shrink/pallas_call | solution.py:910
  (62 shorter events, 6.3 us)
Async XLA Ops:
  0.6 11.7 %collective-permute-start.1 = (bf16[8,1,512,128]{3,2,1,0:T(8,128)(2,1)}, bf16[8,1,512,128]{3,2,1,0:T(8,128)(2,1)S(1)}, u32[]{:S(2)}, u32[]{:S(2)}) collective-permute-start(bf16[8,1,512,128]{3,2,1,0:T(8,128)(2,1)} %bitcast.15), channel_id=1, source_target_pairs={{0,1},{1,0},{2,3},{3,2},{4,5},{5,4},{6,7},{7,6},{8,9},{9,8},{10,11... | collective-permute-start | bytes 3145736 | tf_op jit(solution)/shard_map/ppermute | solution.py:933
  0.7 11.6 %collective-permute-start.2 = (s32[512,512]{1,0:T(8,128)}, s32[512,512]{1,0:T(8,128)S(1)}, u32[]{:S(2)}, u32[]{:S(2)}) collective-permute-start(s32[512,512]{1,0:T(8,128)} %bitcast.20), channel_id=1, source_target_pairs={{0,1},{1,0},{2,3},{3,2},{4,5},{5,4},{6,7},{7,6},{8,9},{9,8},{10,11... | collective-permute-start | bytes 3145736 | tf_op jit(solution)/shard_map/ppermute | solution.py:933
  1.2 48.1 %collective-permute-start.4 = (bf16[8,1,512,128]{3,2,1,0:T(8,128)(2,1)}, bf16[8,1,512,128]{3,2,1,0:T(8,128)(2,1)S(1)}, u32[]{:S(2)}, u32[]{:S(2)}) collective-permute-start(bf16[8,1,512,128]{3,2,1,0:T(8,128)(2,1)} %bitcast.22), channel_id=1, source_target_pairs={{0,1},{1,0},{2,3},{3,2},{4,5},{5,4},{6,7},{7,6},{8,9},{9,8},{10,11... | collective-permute-start | bytes 3145736 | tf_op jit(solution)/shard_map/ppermute | solution.py:933
  2.3 4.5 %collective-permute-start = (bf16[4,8,16,128]{3,2,1,0:T(8,128)(2,1)S(1)}, bf16[4,8,16,128]{3,2,1,0:T(8,128)(2,1)S(1)}, u32[]{:S(2)}, u32[]{:S(2)}) collective-permute-start(bf16[4,8,16,128]{3,2,1,0:T(8,128)(2,1)S(1)} %slice_select_fusion), channel_id=1, source_target_pairs={{0,1},{1,0},{2,3},{3,2},{4,5},{5,4},{6,7},{7,6},{8,9},{9,8},{10,11... | collective-permute-start | bytes 393224 | tf_op jit(solution)/shard_map/ppermute | solution.py:933
  13.6 27.4 %copy-start.20 = (bf16[608,128]{1,0:T(8,128)(2,1)S(1)}, bf16[608,128]{1,0:T(8,128)(2,1)}, u32[]{:S(2)}) copy-start(bf16[608,128]{1,0:T(8,128)(2,1)} %get-tuple-element.34) | copy-start | bytes 466948
  24.5 24.9 %collective-permute-start.3 = (bf16[528,512]{1,0:T(8,128)(2,1)}, bf16[528,512]{1,0:T(8,128)(2,1)S(1)}, u32[]{:S(2)}, u32[]{:S(2)}) collective-permute-start(bf16[528,512]{1,0:T(8,128)(2,1)} %get-tuple-element.26), channel_id=1, source_target_pairs={{0,1},{1,0},{2,3},{3,2},{4,5},{5,4},{6,7},{7,6},{8,9},{9,8},{10,11... | collective-permute-start | bytes 1622024 | tf_op jit(solution)/shard_map/ppermute | solution.py:933
  24.7 16.4 %collective-permute-start.8 = (bf16[608,128]{1,0:T(8,128)(2,1)S(1)}, bf16[608,128]{1,0:T(8,128)(2,1)S(1)}, u32[]{:S(2)}, u32[]{:S(2)}) collective-permute-start(bf16[608,128]{1,0:T(8,128)(2,1)S(1)} %copy-done.5), channel_id=1, source_target_pairs={{0,8},{2,10},{4,12},{6,14},{8,0},{10,2},{12,4},{14,6},{1,9},{3,11}... | collective-permute-start | bytes 466952 | tf_op jit(solution)/shard_map/ppermute | solution.py:951
  27.2 20.6 %collective-permute-start.10 = (bf16[608,128]{1,0:T(8,128)(2,1)}, bf16[608,128]{1,0:T(8,128)(2,1)S(1)}, u32[]{:S(2)}, u32[]{:S(2)}) collective-permute-start(bf16[608,128]{1,0:T(8,128)(2,1)} %get-tuple-element.35), channel_id=1, source_target_pairs={{0,12},{2,14},{4,8},{6,10},{8,4},{10,6},{12,0},{14,2},{1,13},{3,15... | collective-permute-start | bytes 466952 | tf_op jit(solution)/shard_map/ppermute | solution.py:951
  27.2 29.4 %collective-permute-start.11 = (bf16[608,128]{1,0:T(8,128)(2,1)}, bf16[608,128]{1,0:T(8,128)(2,1)S(1)}, u32[]{:S(2)}, u32[]{:S(2)}) collective-permute-start(bf16[608,128]{1,0:T(8,128)(2,1)} %get-tuple-element.36), channel_id=1, source_target_pairs={{0,14},{2,12},{4,10},{6,8},{8,6},{10,4},{12,2},{14,0},{1,15},{3,13... | collective-permute-start | bytes 466952 | tf_op jit(solution)/shard_map/ppermute | solution.py:951
  41.0 18.7 %copy-start.6 = (bf16[608,128]{1,0:T(8,128)(2,1)}, bf16[608,128]{1,0:T(8,128)(2,1)S(1)}, u32[]{:S(2)}) copy-start(bf16[608,128]{1,0:T(8,128)(2,1)S(1)} %collective-permute-done.8.rest_4_) | copy-start | bytes 466948
  41.0 15.7 %collective-permute-start.9 = (bf16[608,128]{1,0:T(8,128)(2,1)S(1)}, bf16[608,128]{1,0:T(8,128)(2,1)S(1)}, u32[]{:S(2)}, u32[]{:S(2)}) collective-permute-start(bf16[608,128]{1,0:T(8,128)(2,1)S(1)} %copy-done.20), channel_id=1, source_target_pairs={{0,10},{2,8},{4,14},{6,12},{8,2},{10,0},{12,6},{14,4},{1,11},{3,9}... | collective-permute-start | bytes 466952 | tf_op jit(solution)/shard_map/ppermute | solution.py:951
  47.8 8.9 %collective-permute-start.5 = (bf16[608,128]{1,0:T(8,128)(2,1)}, bf16[608,128]{1,0:T(8,128)(2,1)S(1)}, u32[]{:S(2)}, u32[]{:S(2)}) collective-permute-start(bf16[608,128]{1,0:T(8,128)(2,1)} %get-tuple-element.31), channel_id=1, source_target_pairs={{0,2},{2,0},{4,6},{6,4},{8,10},{10,8},{12,14},{14,12},{1,3},{3,1},... | collective-permute-start | bytes 466952 | tf_op jit(solution)/shard_map/ppermute | solution.py:951
  49.3 7.4 %collective-permute-start.6 = (bf16[608,128]{1,0:T(8,128)(2,1)}, bf16[608,128]{1,0:T(8,128)(2,1)S(1)}, u32[]{:S(2)}, u32[]{:S(2)}) collective-permute-start(bf16[608,128]{1,0:T(8,128)(2,1)} %get-tuple-element.32), channel_id=1, source_target_pairs={{0,4},{2,6},{4,0},{6,2},{8,12},{10,14},{12,8},{14,10},{1,5},{3,7},... | collective-permute-start | bytes 466952 | tf_op jit(solution)/shard_map/ppermute | solution.py:951
  49.3 10.3 %collective-permute-start.7 = (bf16[608,128]{1,0:T(8,128)(2,1)}, bf16[608,128]{1,0:T(8,128)(2,1)S(1)}, u32[]{:S(2)}, u32[]{:S(2)}) collective-permute-start(bf16[608,128]{1,0:T(8,128)(2,1)} %get-tuple-element.33), channel_id=1, source_target_pairs={{0,6},{2,4},{4,2},{6,0},{8,14},{10,12},{12,10},{14,8},{1,7},{3,5},... | collective-permute-start | bytes 466952 | tf_op jit(solution)/shard_map/ppermute | solution.py:951
  66.3 8.7 %collective-permute-start.12 = (bf16[608,128]{1,0:T(8,128)(2,1)}, bf16[608,128]{1,0:T(8,128)(2,1)S(1)}, u32[]{:S(2)}, u32[]{:S(2)}) collective-permute-start(bf16[608,128]{1,0:T(8,128)(2,1)} %get-tuple-element.39), channel_id=1, source_target_pairs={{0,2},{2,0},{4,6},{6,4},{8,10},{10,8},{12,14},{14,12},{1,3},{3,1},... | collective-permute-start | bytes 466952 | tf_op jit(solution)/shard_map/ppermute | solution.py:951
  66.9 13.3 %collective-permute-start.13 = (bf16[608,128]{1,0:T(8,128)(2,1)}, bf16[608,128]{1,0:T(8,128)(2,1)S(1)}, u32[]{:S(2)}, u32[]{:S(2)}) collective-permute-start(bf16[608,128]{1,0:T(8,128)(2,1)} %get-tuple-element.40), channel_id=1, source_target_pairs={{0,4},{2,6},{4,0},{6,2},{8,12},{10,14},{12,8},{14,10},{1,5},{3,7},... | collective-permute-start | bytes 466952 | tf_op jit(solution)/shard_map/ppermute | solution.py:951
  70.2 12.0 %collective-permute-start.14 = (bf16[608,128]{1,0:T(8,128)(2,1)}, bf16[608,128]{1,0:T(8,128)(2,1)S(1)}, u32[]{:S(2)}, u32[]{:S(2)}) collective-permute-start(bf16[608,128]{1,0:T(8,128)(2,1)} %get-tuple-element.41), channel_id=1, source_target_pairs={{0,6},{2,4},{4,2},{6,0},{8,14},{10,12},{12,10},{14,8},{1,7},{3,5},... | collective-permute-start | bytes 466952 | tf_op jit(solution)/shard_map/ppermute | solution.py:951
  70.2 21.9 %collective-permute-start.15 = (bf16[608,128]{1,0:T(8,128)(2,1)}, bf16[608,128]{1,0:T(8,128)(2,1)S(1)}, u32[]{:S(2)}, u32[]{:S(2)}) collective-permute-start(bf16[608,128]{1,0:T(8,128)(2,1)} %get-tuple-element.42), channel_id=1, source_target_pairs={{0,8},{2,10},{4,12},{6,14},{8,0},{10,2},{12,4},{14,6},{1,9},{3,11}... | collective-permute-start | bytes 466952 | tf_op jit(solution)/shard_map/ppermute | solution.py:951
  74.1 21.4 %collective-permute-start.16 = (bf16[608,128]{1,0:T(8,128)(2,1)}, bf16[608,128]{1,0:T(8,128)(2,1)S(1)}, u32[]{:S(2)}, u32[]{:S(2)}) collective-permute-start(bf16[608,128]{1,0:T(8,128)(2,1)} %get-tuple-element.43), channel_id=1, source_target_pairs={{0,10},{2,8},{4,14},{6,12},{8,2},{10,0},{12,6},{14,4},{1,11},{3,9}... | collective-permute-start | bytes 466952 | tf_op jit(solution)/shard_map/ppermute | solution.py:951
  75.0 26.0 %copy-start.13 = (bf16[608,128]{1,0:T(8,128)(2,1)}, bf16[608,128]{1,0:T(8,128)(2,1)S(1)}, u32[]{:S(2)}) copy-start(bf16[608,128]{1,0:T(8,128)(2,1)S(1)} %collective-permute-done.12.rest_1_) | copy-start | bytes 466948
  75.0 23.3 %collective-permute-start.17 = (bf16[608,128]{1,0:T(8,128)(2,1)}, bf16[608,128]{1,0:T(8,128)(2,1)S(1)}, u32[]{:S(2)}, u32[]{:S(2)}) collective-permute-start(bf16[608,128]{1,0:T(8,128)(2,1)} %get-tuple-element.44), channel_id=1, source_target_pairs={{0,12},{2,14},{4,8},{6,10},{8,4},{10,6},{12,0},{14,2},{1,13},{3,15... | collective-permute-start | bytes 466952 | tf_op jit(solution)/shard_map/ppermute | solution.py:951
  80.2 20.9 %copy-start.14 = (bf16[608,128]{1,0:T(8,128)(2,1)}, bf16[608,128]{1,0:T(8,128)(2,1)S(1)}, u32[]{:S(2)}) copy-start(bf16[608,128]{1,0:T(8,128)(2,1)S(1)} %collective-permute-done.13.rest_2_) | copy-start | bytes 466948
  80.2 20.8 %collective-permute-start.18 = (bf16[608,128]{1,0:T(8,128)(2,1)}, bf16[608,128]{1,0:T(8,128)(2,1)S(1)}, u32[]{:S(2)}, u32[]{:S(2)}) collective-permute-start(bf16[608,128]{1,0:T(8,128)(2,1)} %get-tuple-element.45), channel_id=1, source_target_pairs={{0,14},{2,12},{4,10},{6,8},{8,6},{10,4},{12,2},{14,0},{1,15},{3,13... | collective-permute-start | bytes 466952 | tf_op jit(solution)/shard_map/ppermute | solution.py:951
  82.2 18.8 %copy-start.15 = (bf16[608,128]{1,0:T(8,128)(2,1)}, bf16[608,128]{1,0:T(8,128)(2,1)S(1)}, u32[]{:S(2)}) copy-start(bf16[608,128]{1,0:T(8,128)(2,1)S(1)} %collective-permute-done.14.rest_3_) | copy-start | bytes 466948
  (16 other events, 60.5 us)
where the time goes:
time: 112 us; the launch traced here: 111 us
  waiting for transfers between devices  44.7 us (40%)
  Pallas kernels  36.2 us (32%)
  starting transfers between devices  24.9 us (22%)
  local copies, waits for them, and re-layouts  3.26 us (3%)
    ppermute x14, waiting for transfers between devices, crossed(): lax.ppermute(blocks[place], 'chan', [(i, i ^ place) for i in range(count)])  40.7 us
    ppermute x14, starting transfers between devices, crossed(): lax.ppermute(blocks[place], 'chan', [(i, i ^ place) for i in range(count)])  23.6 us
    pallas_call x1, Pallas kernels, spectrum(): pl.pallas_call(functools.partial(spectrum_kernel, places=places, margin=m...  10.8 us
    pallas_call x1, Pallas kernels, shrink_step(): pl.pallas_call(functools.partial(shrink_kernel, margin=margin, channels=c...  9.18 us
    pallas_call x1, Pallas kernels, update_step(): pl.pallas_call(functools.partial(update_kernel, margin=margin, facets=fac...  5.93 us
    pallas_call x1, Pallas kernels, gradient_step(): pl.pallas_call(functools.partial(gradient_kernel, margin=margin), out_sha...  5.38 us
    pallas_call x1, Pallas kernels, far_adjoint(): pl.pallas_call(functools.partial(far_adjoint_kernel, places=places, facet...  4.87 us
    ppermute x5, waiting for transfers between devices, swapped(): return lax.ppermute(value, 'split', [(0, 1), (1, 0)])  3.99 us
  transfers between devices with their start and end apart: 19, of which 10 were waited for; matrix products, arithmetic and copies ran while one was open for 1% of the time, Pallas kernels for 19%

commit v1 on v0

--- a/solution.py
+++ b/solution.py
@@ -17,6 +17,8 @@
 dual_step = 0.5
 radius = 6.0
 weight_unit = 0.25
+
+OWN_COPIES = pltpu.CompilerParams(vmem_limit_bytes=67043328)
 
 
 def whole_block(shape):
@@ -357,7 +359,7 @@
         return stores
 
 
-def far_adjoint_kernel(row_taps, col_taps, dual, above, below, *rest, places, facet_rows):
+def part_adjoint_kernel(row_taps, col_taps, dual, above, below, _, *rest, places, facet_rows):
     count = len(places)
     part = PartAdjoint(places, dual, above, below, rest[:count], rest[count:], facet_rows)
     part.start()
@@ -366,19 +368,20 @@
         copy.wait()
 
 
-def far_adjoint(dual, above, below, row_taps, col_taps, places, facet_rows):
+def part_adjoint(dual, above, below, row_taps, col_taps, places, facet_rows, after):
     bases, _, strip_rows, _ = dual.shape
     margin = row_taps.shape[1] // 2
-    anywhere = pl.BlockSpec(memory_space=pl.ANY)
+    anywhere = pl.BlockSpec(memory_space=pltpu.HBM)
     rows = payload_rows(strip_rows + 2 * margin)
     return pl.pallas_call(
-        functools.partial(far_adjoint_kernel, places=places, facet_rows=facet_rows),
+        functools.partial(part_adjoint_kernel, places=places, facet_rows=facet_rows),
         out_shape=[jax.ShapeDtypeStruct((rows, LANES), jnp.bfloat16)] * len(places),
-        in_specs=[in_scalar_memory()] * 2 + [anywhere] * 3,
+        in_specs=[in_scalar_memory()] * 2 + [anywhere] * 4,
         out_specs=[anywhere] * len(places),
         scratch_shapes=part_scratch(bases, strip_rows, margin, len(places)),
-        name="far_adjoint",
-    )(row_taps, col_taps, dual, above, below)
+        compiler_params=OWN_COPIES,
+        name="part_adjoint",
+    )(row_taps, col_taps, dual, above, below, after)
 
 
 def phase_seeds(pixels):
@@ -559,7 +562,7 @@
     half = pixels // 2
     rows = facet_rows * (strip_rows + 2 * margin)
     shape = jax.ShapeDtypeStruct((rows, half), jnp.bfloat16)
-    anywhere = pl.BlockSpec(memory_space=pl.ANY)
+    anywhere = pl.BlockSpec(memory_space=pltpu.HBM)
     inside = pl.BlockSpec(memory_space=pltpu.VMEM)
     payload = jax.ShapeDtypeStruct((payload_rows(strip_rows + 2 * margin), lanes), jnp.bfloat16)
     result = pl.pallas_call(
@@ -585,6 +588,7 @@
             pltpu.SemaphoreType.DMA((2 * cols * facet_rows + 3 + half // LANES,)),
         ]
         + (part_scratch(bases, strip_rows, margin, len(places)) if places else []),
+        compiler_params=OWN_COPIES,
         name="spectrum",
     )(
         row_taps, col_taps, dual, above, below, own, other, own_counts, other_counts,
@@ -594,18 +598,42 @@
 
 
 def gradient_kernel(
-    kept, got, freq, own, above, below, own_dirty, dirty_above, dirty_below,
-    stepped, edge_out, joined, *, margin
+    kept, got, freq_from, own_from, other, dirty_from, other_dirty, out, edge_out,
+    joined, freq, own, dirty, above, below, dirty_above, dirty_below, stepped, loads, stores,
+    *, margin
 ):
     split = lax.axis_index("split")
     cols, facet_rows, strip_rows, _ = own.shape
     half = kept.shape[1]
     rows = strip_rows + 2 * margin
-
-    @pl.when(pl.program_id(0) == 0)
-    def _():
-        joined[:, :half] = kept[...]
-        joined[:, half:] = got[...]
+    pair = 2 if cols % 2 == 0 else 1
+    started = []
+
+    def load(source, target):
+        copy = pltpu.make_async_copy(source, target, loads.at[len(started)])
+        copy.start()
+        started.append(copy)
+        return copy
+
+    first = [load(kept, joined.at[:, pl.ds(0, half)])]
+    steps = []
+    for step in range(cols // pair):
+        lines = pl.ds(step * pair * LANES, pair * LANES)
+        some = pl.ds(step * pair, pair)
+        steps.append(
+            [
+                load(freq_from.at[lines], freq.at[lines]),
+                load(own_from.at[some], own.at[some]),
+                load(dirty_from.at[some], dirty.at[some]),
+            ]
+        )
+        if step == 0:
+            first.append(load(got, joined.at[:, pl.ds(half, half)]))
+            last, start = pl.ds(strip_rows - 16, 16), pl.ds(0, 16)
+            first.append(load(other.at[:, :, last], above))
+            first.append(load(other.at[:, :, start], below))
+            first.append(load(other_dirty.at[:, :, last], dirty_above))
+            first.append(load(other_dirty.at[:, :, start], dirty_below))
 
     def edges(upper, lower, col, facet_row):
         over = jnp.maximum(facet_row - 1 + split, 0)
@@ -618,51 +646,67 @@
             axis=0,
         )
 
-    value = lax.dot_general(
-        joined[...], freq[...], (((1,), (1,)), ((), ())), preferred_element_type=jnp.float32
-    )
-    for col in range(cols):
-        for facet_row in range(facet_rows):
-            base = facet_row * rows
-            grad = value[base : base + rows, col * LANES : (col + 1) * LANES]
-            image = own[col, facet_row]
-            dirty = own_dirty[col, facet_row].astype(jnp.float32)
-            moved = image.astype(jnp.float32) - primal_step * (grad[:strip_rows] - dirty)
-            stepped[col, facet_row, :strip_rows] = moved.astype(jnp.bfloat16)
-            image = edges(above, below, col, facet_row)
-            dirty = edges(dirty_above, dirty_below, col, facet_row)
-            moved = image - primal_step * (grad[strip_rows:] - dirty)
-            stepped[col, facet_row, strip_rows:] = moved.astype(jnp.bfloat16)
-            edge_out[col, facet_row] = image.astype(jnp.bfloat16)
+    for copy in first:
+        copy.wait()
+    stored = []
+    for step in range(cols // pair):
+        for copy in steps[step]:
+            copy.wait()
+        value = lax.dot_general(
+            joined[...],
+            freq[step * pair * LANES : (step + 1) * pair * LANES, :],
+            (((1,), (1,)), ((), ())),
+            preferred_element_type=jnp.float32,
+        )
+        for side in range(pair):
+            col = step * pair + side
+            for facet_row in range(facet_rows):
+                base = facet_row * rows
+                grad = value[base : base + rows, side * LANES : (side + 1) * LANES]
+                moved = own[col, facet_row].astype(jnp.float32) - primal_step * (
+                    grad[:strip_rows] - dirty[col, facet_row].astype(jnp.float32)
+                )
+                stepped[col, facet_row, :strip_rows] = moved.astype(jnp.bfloat16)
+                image = edges(above, below, col, facet_row)
+                moved = image - primal_step * (
+                    grad[strip_rows:] - edges(dirty_above, dirty_below, col, facet_row)
+                )
+                stepped[col, facet_row, strip_rows:] = moved.astype(jnp.bfloat16)
+                edge_out[col, facet_row] = image.astype(jnp.bfloat16)
+        some = pl.ds(step * pair, pair)
+        stored.append(pltpu.make_async_copy(stepped.at[some], out.at[some], stores.at[step]))
+        stored[-1].start()
+    for copy in stored:
+        copy.wait()
 
 
 def gradient_step(kept, got, freq, own, other, own_dirty, other_dirty, margin):
     cols, facet_rows, strip_rows, lanes = own.shape
     pixels = cols * lanes
     rows = strip_rows + 2 * margin
-    pair = 2 if cols % 2 == 0 else 1
-
-    def block(height, place):
-        return pl.BlockSpec((pair, facet_rows, height, lanes), lambda j: (j, 0, place, 0))
-
-    whole_strip, last, first = block(strip_rows, 0), block(16, strip_rows // 16 - 1), block(16, 0)
+    anywhere = pl.BlockSpec(memory_space=pltpu.HBM)
+    edge = (cols, facet_rows, 16, lanes)
     return pl.pallas_call(
         functools.partial(gradient_kernel, margin=margin),
         out_shape=[
             jax.ShapeDtypeStruct((cols, facet_rows, rows, lanes), jnp.bfloat16),
             jax.ShapeDtypeStruct((cols, facet_rows, 2 * margin, lanes), jnp.bfloat16),
         ],
-        grid=(cols // pair,),
-        in_specs=[
-            whole_block(kept.shape),
-            whole_block(got.shape),
-            pl.BlockSpec((pair * lanes, pixels), lambda j: (j, 0)),
-            whole_strip, last, first, whole_strip, last, first,
+        in_specs=[anywhere] * 7,
+        out_specs=[anywhere, pl.BlockSpec(memory_space=pltpu.VMEM)],
+        scratch_shapes=[
+            pltpu.VMEM((kept.shape[0], pixels), jnp.bfloat16),
+            pltpu.VMEM(freq.shape, jnp.bfloat16),
+            pltpu.VMEM(own.shape, jnp.bfloat16),
+            pltpu.VMEM(own.shape, jnp.bfloat16),
+            *[pltpu.VMEM(edge, jnp.bfloat16)] * 4,
+            pltpu.VMEM((cols, facet_rows, rows, lanes), jnp.bfloat16),
+            pltpu.SemaphoreType.DMA((6 + 3 * cols,)),
+            pltpu.SemaphoreType.DMA((cols,)),
         ],
-        out_specs=[block(rows, 0), block(2 * margin, 0)],
-        scratch_shapes=[pltpu.VMEM((kept.shape[0], pixels), jnp.bfloat16)],
+        compiler_params=OWN_COPIES,
         name="gradient",
-    )(kept, got, freq, own, other, other, own_dirty, other_dirty, other_dirty)
+    )(kept, got, freq, own, other, own_dirty, other_dirty)
 
 
 def unpacked(packed, group, count, margin):
@@ -676,9 +720,8 @@
     blocks = rest[:arrivals]
     new_out = rest[arrivals]
     outs = rest[arrivals + 1 : 2 * arrivals + 1]
-    stepped, image, new_image, adjoint, extrapolated, leaving, loads, arriving, stores = rest[
-        2 * arrivals + 1 :
-    ]
+    stepped, image, new_image, adjoint, apart, extrapolated, leaving = rest[2 * arrivals + 1 : -3]
+    loads, arriving, stores = rest[-3:]
     me = lax.axis_index("chan")
     split = lax.axis_index("split")
     cols, facet_rows, rows, _ = stepped.shape
@@ -700,8 +743,20 @@
         )
         for copy in load[-1]:
             copy.start()
-    for copy in arrive:
+
+    def unpack(facet):
+        tile = adjoint[facet, rows : rows + height, :].astype(jnp.float32)
+        for group, first, count in row_groups(rows):
+            apart[facet, first : first + count, :] = unpacked(
+                tile, group, count, margin
+            ).astype(jnp.bfloat16)
+
+    for place, copy in enumerate(arrive):
         copy.wait()
+        if not single:
+            unpack(me ^ place)
+    if single:
+        each(facets, unpack)
 
     def sides(take, group, count, left, has_left, right, has_right):
         from_left = take(left, group, count)
@@ -711,9 +766,9 @@
             jnp.where(lane >= jnp.where(has_right, LANES - margin, LANES), from_right, 0.0),
         )
 
-    def packed_of(facet, group, count):
-        tile = adjoint[facet, rows : rows + height, :].astype(jnp.float32)
-        return unpacked(tile, group, count, margin)
+    def apart_of(facet, group, count):
+        first = group * height
+        return apart[facet, first : first + count, :].astype(jnp.float32)
 
     def update(facet):
         col = facet // facet_rows
@@ -721,7 +776,7 @@
         left, has_left = jnp.maximum(facet - facet_rows, 0), facet >= facet_rows
         right, has_right = jnp.minimum(facet + facet_rows, facets - 1), facet < facets - facet_rows
         for group, first, count in row_groups(rows):
-            add_left, add_right = sides(packed_of, group, count, left, has_left, right, has_right)
+            add_left, add_right = sides(apart_of, group, count, left, has_left, right, has_right)
             at = slice(first, first + count)
             total = adjoint[facet, at, :].astype(jnp.float32) + add_left + add_right
             value = stepped[col, facet_row, at, :].astype(jnp.float32) - primal_step * total
@@ -803,7 +858,7 @@
         if single
         else [jax.ShapeDtypeStruct((tall_rows, lanes), jnp.bfloat16)] * facets
     )
-    anywhere = pl.BlockSpec(memory_space=pl.ANY)
+    anywhere = pl.BlockSpec(memory_space=pltpu.HBM)
     results = pl.pallas_call(
         functools.partial(update_kernel, margin=margin, facets=facets, single=single),
         out_shape=[
@@ -818,11 +873,13 @@
             pltpu.VMEM(image.shape, jnp.bfloat16),
             pltpu.VMEM((facets, tall_rows, lanes), jnp.bfloat16),
             pltpu.VMEM((facets, rows, lanes), jnp.bfloat16),
+            pltpu.VMEM((facets, rows, lanes), jnp.bfloat16),
             pltpu.VMEM((facets, tall_rows, lanes), jnp.bfloat16),
             pltpu.SemaphoreType.DMA((2 * cols,)),
             pltpu.SemaphoreType.DMA((len(blocks),)),
             pltpu.SemaphoreType.DMA((cols + len(blocks),)),
         ],
+        compiler_params=OWN_COPIES,
         name="update",
     )(stepped, image, edges, *blocks)
     return results[0], results[1:]
@@ -929,6 +986,159 @@
     )(row_taps, col_taps, mask, dual, *blocks)
 
 
+def shrink_part_kernel(row_taps, col_taps, dual, *rest, places, margin, final):
+    count = len(places)
+    blocks, rest = rest[:count], rest[count:]
+    if final:
+        mask, before_from, total_from, out_to = rest[:4]
+        rest = rest[4:]
+    else:
+        out_to, total_to = rest[:2]
+        rest = rest[2:]
+    row_band, col_band, arrived, wide, tall, field, held, before, total, loads, stores = rest
+    me = lax.axis_index("chan")
+    bases, taps = row_taps.shape
+    halo = 2 * margin
+    strip_rows = dual.shape[2]
+    rows = strip_rows + halo
+    height = pack_height(rows)
+    started = []
+
+    def load(source, target):
+        copy = pltpu.make_async_copy(source, target, loads.at[len(started)])
+        copy.start()
+        started.append(copy)
+        return copy
+
+    stored = []
+
+    def store(source, target):
+        copy = pltpu.make_async_copy(source, target, stores.at[len(stored)])
+        copy.start()
+        stored.append(copy)
+
+    arrive = [load(block, arrived.at[at]) for at, block in enumerate(blocks)]
+    fields = []
+    for basis in range(bases):
+        group = [
+            load(dual.at[basis, me ^ place], field.at[basis, at]) for at, place in enumerate(places)
+        ]
+        if final:
+            group.append(load(before_from.at[basis], before.at[basis]))
+            group.append(load(total_from.at[basis], total.at[basis]))
+        fields.append(group)
+    for basis in range(bases):
+        seed = band_seed(row_taps, basis, [margin + tap for tap in range(taps)])
+        fill_band(row_band.at[basis], 0, BAND_ROWS, seed)
+        used = strip_rows + 2 * halo
+        if used < tall.shape[1]:
+            tall[basis, used:] = jnp.zeros((tall.shape[1] - used, tall.shape[2]), jnp.bfloat16)
+    fill_col_bands(col_band, col_taps, bases, margin)
+    for at in range(count):
+        arrive[at].wait()
+        block = arrived.at[at]
+        wide[at, :, :LANES] = block[:rows, :]
+        packed = block[rows : rows + height, :].astype(jnp.float32)
+        for group, first, some in row_groups(rows):
+            side = unpacked(packed, group, some, margin)
+            wide[at, first : first + some, LANES:] = side.astype(jnp.bfloat16)
+        value = lax.dot_general(
+            wide[at], col_band[...], (((1,), (1,)), ((), ())), preferred_element_type=jnp.float32
+        )
+        blank = jnp.zeros((halo - margin, LANES), jnp.float32)
+        lanes = slice(at * LANES, (at + 1) * LANES)
+        for basis in range(bases):
+            mine = value[:, basis * LANES : (basis + 1) * LANES]
+            tall[basis, halo : halo + strip_rows, lanes] = mine[:strip_rows].astype(jnp.bfloat16)
+            tall[basis, :halo, lanes] = jnp.concatenate(
+                [blank, mine[strip_rows : strip_rows + margin]], axis=0
+            ).astype(jnp.bfloat16)
+            tall[basis, halo + strip_rows : 2 * halo + strip_rows, lanes] = jnp.concatenate(
+                [mine[strip_rows + margin :], blank], axis=0
+            ).astype(jnp.bfloat16)
+    for basis in range(bases):
+        for copy in fields[basis]:
+            copy.wait()
+        for first in range(0, strip_rows, BAND_ROWS):
+            some = min(BAND_ROWS, strip_rows - first)
+            here = slice(first, first + some)
+            value = exact_dot(row_band[basis, :some], tall[basis, first : first + WIDE])
+            if final:
+                squares = total[basis, here]
+            else:
+                squares = jnp.zeros((some, LANES), jnp.float32)
+            stepped = []
+            for at in range(count):
+                moved = (
+                    field[basis, at, here].astype(jnp.float32)
+                    + dual_step * value[:, at * LANES : (at + 1) * LANES]
+                )
+                stepped.append(moved)
+                squares = squares + moved * moved
+            if final:
+                kept = mask[here].astype(jnp.float32)
+                scale = radius * kept / jnp.maximum(jnp.sqrt(squares), radius)
+                for at in range(count):
+                    held[basis, at, here] = (stepped[at] * scale).astype(jnp.bfloat16)
+                    earlier = before[basis, at, here].astype(jnp.float32)
+                    before[basis, at, here] = (earlier * scale).astype(jnp.bfloat16)
+            else:
+                total[basis, here] = squares
+                for at in range(count):
+                    held[basis, at, here] = stepped[at].astype(jnp.bfloat16)
+        if final:
+            for at, place in enumerate(places):
+                store(held.at[basis, at], out_to.at[basis, me ^ place])
+                store(before.at[basis, at], out_to.at[basis, me ^ place ^ count])
+        else:
+            store(held.at[basis], out_to.at[basis])
+            store(total.at[basis], total_to.at[basis])
+    for copy in stored:
+        copy.wait()
+
+
+def shrink_part(row_taps, col_taps, dual, blocks, places, earlier=None):
+    bases, _, strip_rows, lanes = dual.shape
+    count = len(places)
+    margin = row_taps.shape[1] // 2
+    rows = strip_rows + 2 * margin
+    anywhere = pl.BlockSpec(memory_space=pltpu.HBM)
+    part = (bases, count, strip_rows, lanes)
+    final = earlier is not None
+    if final:
+        more = (pl.BlockSpec(memory_space=pltpu.VMEM), anywhere, anywhere)
+        out_shape = jax.ShapeDtypeStruct(dual.shape, jnp.bfloat16)
+        out_specs = anywhere
+    else:
+        more, earlier = (), ()
+        out_shape = [
+            jax.ShapeDtypeStruct(part, jnp.bfloat16),
+            jax.ShapeDtypeStruct((bases, strip_rows, lanes), jnp.float32),
+        ]
+        out_specs = [anywhere, anywhere]
+    return pl.pallas_call(
+        functools.partial(shrink_part_kernel, places=places, margin=margin, final=final),
+        out_shape=out_shape,
+        in_specs=[in_scalar_memory()] * 2 + [anywhere] * (1 + count) + list(more),
+        out_specs=out_specs,
+        scratch_shapes=[
+            pltpu.VMEM((bases, BAND_ROWS, WIDE), jnp.bfloat16),
+            pltpu.VMEM((bases * LANES, WIDE), jnp.bfloat16),
+            pltpu.VMEM((count, payload_rows(rows), lanes), jnp.bfloat16),
+            pltpu.VMEM((count, rows, WIDE), jnp.bfloat16),
+            pltpu.VMEM((bases, tall_height(strip_rows, margin), count * lanes), jnp.bfloat16),
+            pltpu.VMEM(part, jnp.bfloat16),
+            pltpu.VMEM(part, jnp.bfloat16),
+            pltpu.VMEM(part if final else (1, 1, 16, lanes), jnp.bfloat16),
+            pltpu.VMEM((bases, strip_rows, lanes), jnp.float32),
+            pltpu.SemaphoreType.DMA((count + bases * (count + 2),)),
+            pltpu.SemaphoreType.DMA((2 * bases * count,)),
+        ],
+        compiler_params=OWN_COPIES,
+        name="shrink_part",
+    )(row_taps, col_taps, dual, *blocks, *earlier)
+
+
 def swapped(value):
     return lax.ppermute(value, "split", [(0, 1), (1, 0)])
 
@@ -980,18 +1190,16 @@
     other_dirty = swapped(dirty)
     if single:
         blocks = [all_adjoint(dual, above, below, row_taps, col_taps, facet_rows)]
-        far, near = blocks, ()
+        far = blocks
     else:
-        near = tuple(range(count // 2))
-        far = far_adjoint(
-            dual, above, below, row_taps, col_taps, tuple(range(count // 2, count)), facet_rows
-        )
-    close, freq, kept, sent = spectrum(
+        adjoint = functools.partial(part_adjoint, dual, above, below, row_taps, col_taps)
+        far = adjoint(tuple(range(count // 2, count)), facet_rows, row_taps)
+        near = adjoint(tuple(range(count // 2)), facet_rows, far[0])
+        blocks = [*near, *far]
+    _, freq, kept, sent = spectrum(
         image, other_image, counts, other_counts, dual, above, below,
-        row_taps, col_taps, near, margin, far[0],
+        row_taps, col_taps, (), margin, blocks[0],
     )
-    if not single:
-        blocks = list(close) + list(far)
     arrived = crossed(blocks, single)
     got = swapped(sent)
     stepped, edges = gradient_step(
@@ -999,7 +1207,13 @@
     )
     new_image, blocks = update_step(stepped, image, edges, arrived, margin, single)
     arrived = crossed(blocks, single)
-    new_dual = shrink_step(row_taps, col_taps, mask, dual, arrived, single)
+    if single:
+        new_dual = shrink_step(row_taps, col_taps, mask, dual, arrived, single)
+    else:
+        shrink = functools.partial(shrink_part, row_taps, col_taps, dual)
+        middle = count // 2
+        earlier = shrink(arrived[:middle], tuple(range(middle)))
+        new_dual = shrink(arrived[middle:], tuple(range(middle, count)), (mask, *earlier))
     return (new_image.reshape(sky_image.shape), new_dual.reshape(dual_coeffs.shape))
 
 

time: 112 us -> 107 us (0.955)
  Pallas kernels: 36.2 us -> 44 us
  waiting for transfers between devices: 44.7 us -> 39 us
  starting transfers between devices: 24.9 us -> 21.3 us
  local copies, waits for them, and re-layouts: 3.26 us -> 0 us
    pallas_call x2 -> x4, Pallas kernels: 14 us -> 23 us  [the longest x2 13.2 us: shrink_part(): pl.pallas_call(functools.partial(shrink_part_kernel, places=places, margi...]
    ppermute x14, waiting for transfers between devices: 40.7 us -> 34.9 us  [crossed(): lax.ppermute(blocks[place], 'chan', [(i, i ^ place) for i in range(count)])]
    ppermute x14, starting transfers between devices: 23.6 us -> 20 us  [crossed(): lax.ppermute(blocks[place], 'chan', [(i, i ^ place) for i in range(count)])]
    unnamed x42 -> x0, local copies, waits for them, and re-layouts: 3.26 us -> none
    pallas_call x1, Pallas kernels: 10.8 us -> 8.92 us  [spectrum(): pl.pallas_call(functools.partial(spectrum_kernel, places=places, margin=m...]
  transfers between devices with their start and end apart: 19 -> 19, of which waited for: 10 -> 10; matrix products, arithmetic and copies ran while one was open for 1% -> 1% of each run, Pallas kernels for 19% -> 29%
where the time goes in v1:
time: 107 us; the launch traced here: 106 us
  Pallas kernels  44 us (41%)
  waiting for transfers between devices  39 us (36%)
  starting transfers between devices  21.3 us (20%)
    ppermute x14, waiting for transfers between devices, crossed(): lax.ppermute(blocks[place], 'chan', [(i, i ^ place) for i in range(count)])  34.9 us
    ppermute x14, starting transfers between devices, crossed(): lax.ppermute(blocks[place], 'chan', [(i, i ^ place) for i in range(count)])  20 us
    pallas_call x2, Pallas kernels, shrink_part(): pl.pallas_call(functools.partial(shrink_part_kernel, places=places, margi...  13.2 us
    pallas_call x2, Pallas kernels, part_adjoint(): pl.pallas_call(functools.partial(part_adjoint_kernel, places=places, face...  9.76 us
    pallas_call x1, Pallas kernels, spectrum(): pl.pallas_call(functools.partial(spectrum_kernel, places=places, margin=m...  8.92 us
    pallas_call x1, Pallas kernels, gradient_step(): pl.pallas_call(functools.partial(gradient_kernel, margin=margin), out_sha...  6.18 us
    pallas_call x1, Pallas kernels, update_step(): pl.pallas_call(functools.partial(update_kernel, margin=margin, facets=fac...  5.88 us
    ppermute x5, waiting for transfers between devices, swapped(): return lax.ppermute(value, 'split', [(0, 1), (1, 0)])  4.12 us
  transfers between devices with their start and end apart: 19, of which 10 were waited for; matrix products, arithmetic and copies ran while one was open for 1% of the time, Pallas kernels for 29%

profile of v1, /device:TPU:8, one launch (start us, length us, event | category | flops | bytes accessed | tf_op | source)
XLA Modules:
  0.0 106.2 jit_solution(8974131004173847682)
XLA Ops:
  2.8 4.1 %collective-permute-done.above.below = bf16[4,8,16,128]{3,2,1,0:T(8,128)(2,1)} collective-permute-done((bf16[4,8,16,128]{3,2,1,0:T(8,128)(2,1)S(1)}, bf16[4,8,16,128]{3,2,1,0:T(8,128)(2,1)}, u32[]{:S(2)}, u32[]{:S(2)}) %collective-permute-start) | collective-permute-done | bytes 131104 | tf_op jit(solution)/shard_map/ppermute | solution.py:1143
  6.9 4.9 %part_adjoint.2 = (bf16[608,128]{1,0:T(8,128)(2,1)}, bf16[608,128]{1,0:T(8,128)(2,1)}, bf16[608,128]{1,0:T(8,128)(2,1)}, bf16[608,128]{1,0:T(8,128)(2,1)}) custom-call(f32[4,17]{1,0:T(4,128)} %row_taps.9, f32[4,17]{1,0:T(4,128)} %col_taps.9, bf16[4,8,512,128]{3,2,1,0:T(8,128)(2,1)} %bitcast.12, bf16[4,8,16,128]{3,2,1,0:T(8,128)(2,1)} %collective-permute-done.above.below, ...), custom_call_target="tpu_custom_call" | custom-call | tf_op jit(solution)/shard_map/part_adjoint/pallas_call | solution.py:376
  11.8 4.9 %part_adjoint.3 = (bf16[608,128]{1,0:T(8,128)(2,1)}, bf16[608,128]{1,0:T(8,128)(2,1)}, bf16[608,128]{1,0:T(8,128)(2,1)}, bf16[608,128]{1,0:T(8,128)(2,1)}) custom-call(f32[4,17]{1,0:T(4,128)} %row_taps.9, f32[4,17]{1,0:T(4,128)} %col_taps.9, bf16[4,8,512,128]{3,2,1,0:T(8,128)(2,1)} %bitcast.13, bf16[4,8,16,128]{3,2,1,0:T(8,128)(2,1)} %collective-permute-done.above.below, ...), custom_call_target="tpu_custom_call" | custom-call | tf_op jit(solution)/shard_map/part_adjoint/pallas_call | solution.py:376
  16.7 8.9 %spectrum.1 = (bf16[1024,1024]{1,0:T(8,128)(2,1)}, bf16[528,512]{1,0:T(8,128)(2,1)}, bf16[528,512]{1,0:T(8,128)(2,1)}) custom-call(f32[4,17]{1,0:T(4,128)} %row_taps.9, f32[4,17]{1,0:T(4,128)} %col_taps.9, bf16[4,8,512,128]{3,2,1,0:T(8,128)(2,1)} %bitcast.14, bf16[4,8,16,128]{3,2,1,0:T(8,128)(2,1)} %collective-permute-done.above.below, ...), custom_call_target="tpu_custom_call" | custom-call | tf_op jit(solution)/shard_map/spectrum/pallas_call | solution.py:568
  25.8 3.5 %collective-permute-start.9 = (bf16[608,128]{1,0:T(8,128)(2,1)}, bf16[608,128]{1,0:T(8,128)(2,1)}, u32[]{:S(2)}, u32[]{:S(2)}) collective-permute-start(bf16[608,128]{1,0:T(8,128)(2,1)} %get-tuple-element.36), channel_id=1, source_target_pairs={{0,10},{2,8},{4,14},{6,12},{8,2},{10,0},{12,6},{14,4},{1,11},{3,9}... | collective-permute-start | bytes 466952 | tf_op jit(solution)/shard_map/ppermute | solution.py:1161
  29.3 2.8 %collective-permute-start.8 = (bf16[608,128]{1,0:T(8,128)(2,1)}, bf16[608,128]{1,0:T(8,128)(2,1)}, u32[]{:S(2)}, u32[]{:S(2)}) collective-permute-start(bf16[608,128]{1,0:T(8,128)(2,1)} %get-tuple-element.26._), channel_id=1, source_target_pairs={{0,8},{2,10},{4,12},{6,14},{8,0},{10,2},{12,4},{14,6},{1,9},{3,11}... | collective-permute-start | bytes 466952 | tf_op jit(solution)/shard_map/ppermute | solution.py:1161
  32.1 11.3 %collective-permute-done.9.rest_5_ = bf16[608,128]{1,0:T(8,128)(2,1)} collective-permute-done((bf16[608,128]{1,0:T(8,128)(2,1)}, bf16[608,128]{1,0:T(8,128)(2,1)}, u32[]{:S(2)}, u32[]{:S(2)}) %collective-permute-start.9) | collective-permute-done | bytes 155680 | tf_op jit(solution)/shard_map/ppermute | solution.py:1161
  43.4 3.7 %collective-permute-done.10.rest_6_ = bf16[608,128]{1,0:T(8,128)(2,1)} collective-permute-done((bf16[608,128]{1,0:T(8,128)(2,1)}, bf16[608,128]{1,0:T(8,128)(2,1)}, u32[]{:S(2)}, u32[]{:S(2)}) %collective-permute-start.10) | collective-permute-done | bytes 155680 | tf_op jit(solution)/shard_map/ppermute | solution.py:1161
  47.4 2.3 %collective-permute-start.6 = (bf16[608,128]{1,0:T(8,128)(2,1)}, bf16[608,128]{1,0:T(8,128)(2,1)}, u32[]{:S(2)}, u32[]{:S(2)}) collective-permute-start(bf16[608,128]{1,0:T(8,128)(2,1)} %get-tuple-element.34), channel_id=1, source_target_pairs={{0,4},{2,6},{4,0},{6,2},{8,12},{10,14},{12,8},{14,10},{1,5},{3,7},... | collective-permute-start | bytes 466952 | tf_op jit(solution)/shard_map/ppermute | solution.py:1161
  50.7 6.2 %gradient.1 = (bf16[8,1,528,128]{3,2,1,0:T(8,128)(2,1)}, bf16[8,1,16,128]{3,2,1,0:T(8,128)(2,1)}) custom-call(bf16[528,512]{1,0:T(8,128)(2,1)} %get-tuple-element.28.kept, bf16[528,512]{1,0:T(8,128)(2,1)} %collective-permute-done.3.got, bf16[1024,1024]{1,0:T(8,128)(2,1)} %get-tuple-element.30.freq_from, bf16[8,1,512,128]{3,2,1,0:T(8,128)(2,1)} %bitcast.19, ...), custom_call_target="tpu_custom_call" | custom-call | tf_op jit(solution)/shard_map/gradient/pallas_call | solution.py:689
  56.9 1.8 %collective-permute-done.11.rest_7_ = bf16[608,128]{1,0:T(8,128)(2,1)} collective-permute-done((bf16[608,128]{1,0:T(8,128)(2,1)}, bf16[608,128]{1,0:T(8,128)(2,1)}, u32[]{:S(2)}, u32[]{:S(2)}) %collective-permute-start.11) | collective-permute-done | bytes 155680 | tf_op jit(solution)/shard_map/ppermute | solution.py:1161
  58.7 1.4 %collective-permute-done.7.rest_3_ = bf16[608,128]{1,0:T(8,128)(2,1)} collective-permute-done((bf16[608,128]{1,0:T(8,128)(2,1)}, bf16[608,128]{1,0:T(8,128)(2,1)}, u32[]{:S(2)}, u32[]{:S(2)}) %collective-permute-start.7) | collective-permute-done | bytes 155680 | tf_op jit(solution)/shard_map/ppermute | solution.py:1161
  60.1 5.9 %update.1 = (bf16[8,1,512,128]{3,2,1,0:T(8,128)(2,1)}, bf16[608,128]{1,0:T(8,128)(2,1)}, bf16[608,128]{1,0:T(8,128)(2,1)}, bf16[608,128]{1,0:T(8,128)(2,1)}, bf1...) custom-call(bf16[8,1,528,128]{3,2,1,0:T(8,128)(2,1)} %get-tuple-elem, ...), custom_call_target="tpu_custom_call" | custom-call | tf_op jit(solution)/shard_map/update/pallas_call | solution.py:862
  66.0 1.6 %collective-permute-start.16 = (bf16[608,128]{1,0:T(8,128)(2,1)}, bf16[608,128]{1,0:T(8,128)(2,1)}, u32[]{:S(2)}, u32[]{:S(2)}) collective-permute-start(bf16[608,128]{1,0:T(8,128)(2,1)} %get-tuple-element.45), channel_id=1, source_target_pairs={{0,2},{2,0},{4,6},{6,4},{8,10},{10,8},{12,14},{14,12},{1,3},{3,1},... | collective-permute-start | bytes 466952 | tf_op jit(solution)/shard_map/ppermute | solution.py:1161
  67.6 1.3 %collective-permute-start.17 = (bf16[608,128]{1,0:T(8,128)(2,1)}, bf16[608,128]{1,0:T(8,128)(2,1)}, u32[]{:S(2)}, u32[]{:S(2)}) collective-permute-start(bf16[608,128]{1,0:T(8,128)(2,1)} %get-tuple-element.46), channel_id=1, source_target_pairs={{0,4},{2,6},{4,0},{6,2},{8,12},{10,14},{12,8},{14,10},{1,5},{3,7},... | collective-permute-start | bytes 466952 | tf_op jit(solution)/shard_map/ppermute | solution.py:1161
  68.8 2.2 %collective-permute-start.12 = (bf16[608,128]{1,0:T(8,128)(2,1)}, bf16[608,128]{1,0:T(8,128)(2,1)}, u32[]{:S(2)}, u32[]{:S(2)}) collective-permute-start(bf16[608,128]{1,0:T(8,128)(2,1)} %get-tuple-element.40), channel_id=1, source_target_pairs={{0,8},{2,10},{4,12},{6,14},{8,0},{10,2},{12,4},{14,6},{1,9},{3,11}... | collective-permute-start | bytes 466952 | tf_op jit(solution)/shard_map/ppermute | solution.py:1161
  71.7 2.1 %collective-permute-start.18 = (bf16[608,128]{1,0:T(8,128)(2,1)}, bf16[608,128]{1,0:T(8,128)(2,1)}, u32[]{:S(2)}, u32[]{:S(2)}) collective-permute-start(bf16[608,128]{1,0:T(8,128)(2,1)} %get-tuple-element.47), channel_id=1, source_target_pairs={{0,6},{2,4},{4,2},{6,0},{8,14},{10,12},{12,10},{14,8},{1,7},{3,5},... | collective-permute-start | bytes 466952 | tf_op jit(solution)/shard_map/ppermute | solution.py:1161
  73.8 1.6 %collective-permute-start.14 = (bf16[608,128]{1,0:T(8,128)(2,1)}, bf16[608,128]{1,0:T(8,128)(2,1)}, u32[]{:S(2)}, u32[]{:S(2)}) collective-permute-start(bf16[608,128]{1,0:T(8,128)(2,1)} %get-tuple-element.42), channel_id=1, source_target_pairs={{0,12},{2,14},{4,8},{6,10},{8,4},{10,6},{12,0},{14,2},{1,13},{3,15... | collective-permute-start | bytes 466952 | tf_op jit(solution)/shard_map/ppermute | solution.py:1161
  77.1 7.6 %collective-permute-done.18.rest_3_ = bf16[608,128]{1,0:T(8,128)(2,1)} collective-permute-done((bf16[608,128]{1,0:T(8,128)(2,1)}, bf16[608,128]{1,0:T(8,128)(2,1)}, u32[]{:S(2)}, u32[]{:S(2)}) %collective-permute-start.18) | collective-permute-done | bytes 155680 | tf_op jit(solution)/shard_map/ppermute | solution.py:1161
  84.7 5.9 %shrink_part.2 = (bf16[4,4,512,128]{3,2,1,0:T(8,128)(2,1)}, f32[4,512,128]{2,1,0:T(8,128)}) custom-call(f32[4,17]{1,0:T(4,128)} %row_taps.9, f32[4,17]{1,0:T(4,128)} %col_taps.9, bf16[4,8,512,128]{3,2,1,0:T(8,128)(2,1)} %bitcast.15, bf16[608,128]{1,0:T(8,128)(2,1)} %get-tuple-element.44.rest_0_, bf16[608,128]{1,0:T(8,128)(2,1)} %collective-permute-done.16.rest_1_, ...), custom_call_target="tpu_custom_call" | custom-call | tf_op jit(solution)/shard_map/shrink_part/pallas_call | solution.py:1119
  90.6 1.7 %collective-permute-done.13.rest_1_ = bf16[608,128]{1,0:T(8,128)(2,1)} collective-permute-done((bf16[608,128]{1,0:T(8,128)(2,1)}, bf16[608,128]{1,0:T(8,128)(2,1)}, u32[]{:S(2)}, u32[]{:S(2)}) %collective-permute-start.13) | collective-permute-done | bytes 155680 | tf_op jit(solution)/shard_map/ppermute | solution.py:1161
  92.3 4.3 %collective-permute-done.14.rest_2_ = bf16[608,128]{1,0:T(8,128)(2,1)} collective-permute-done((bf16[608,128]{1,0:T(8,128)(2,1)}, bf16[608,128]{1,0:T(8,128)(2,1)}, u32[]{:S(2)}, u32[]{:S(2)}) %collective-permute-start.14) | collective-permute-done | bytes 155680 | tf_op jit(solution)/shard_map/ppermute | solution.py:1161
  96.6 2.1 %collective-permute-done.15.rest_3_ = bf16[608,128]{1,0:T(8,128)(2,1)} collective-permute-done((bf16[608,128]{1,0:T(8,128)(2,1)}, bf16[608,128]{1,0:T(8,128)(2,1)}, u32[]{:S(2)}, u32[]{:S(2)}) %collective-permute-start.15) | collective-permute-done | bytes 155680 | tf_op jit(solution)/shard_map/ppermute | solution.py:1161
  98.7 7.3 %shrink_part.3 = bf16[4,8,512,128]{3,2,1,0:T(8,128)(2,1)} custom-call(f32[4,17]{1,0:T(4,128)} %row_taps.9, f32[4,17]{1,0:T(4,128)} %col_taps.9, bf16[4,8,512,128]{3,2,1,0:T(8,128)(2,1)} %bitcast.16, bf16[608,128]{1,0:T(8,128)(2,1)} %collective-permute-done.12.rest_0_, bf16[608,128]{1,0:T(8,128)(2,1)} %collective-permute-done.13.rest_1_, ...), custom_call_target="tpu_custom_call" | custom-call | tf_op jit(solution)/shard_map/shrink_part/pallas_call | solution.py:1119
  (22 shorter events, 6.0 us)
Async XLA Ops:
  0.6 16.0 %collective-permute-start.1 = (bf16[8,1,512,128]{3,2,1,0:T(8,128)(2,1)}, bf16[8,1,512,128]{3,2,1,0:T(8,128)(2,1)}, u32[]{:S(2)}, u32[]{:S(2)}) collective-permute-start(bf16[8,1,512,128]{3,2,1,0:T(8,128)(2,1)} %bitcast.17), channel_id=1, source_target_pairs={{0,1},{1,0},{2,3},{3,2},{4,5},{5,4},{6,7},{7,6},{8,9},{9,8},{10,11... | collective-permute-start | bytes 3145736 | tf_op jit(solution)/shard_map/ppermute | solution.py:1143
  0.7 16.0 %collective-permute-start.2 = (s32[512,512]{1,0:T(8,128)}, s32[512,512]{1,0:T(8,128)}, u32[]{:S(2)}, u32[]{:S(2)}) collective-permute-start(s32[512,512]{1,0:T(8,128)} %bitcast.22), channel_id=1, source_target_pairs={{0,1},{1,0},{2,3},{3,2},{4,5},{5,4},{6,7},{7,6},{8,9},{9,8},{10,11... | collective-permute-start | bytes 3145736 | tf_op jit(solution)/shard_map/ppermute | solution.py:1143
  1.2 46.2 %collective-permute-start.4 = (bf16[8,1,512,128]{3,2,1,0:T(8,128)(2,1)}, bf16[8,1,512,128]{3,2,1,0:T(8,128)(2,1)}, u32[]{:S(2)}, u32[]{:S(2)}) collective-permute-start(bf16[8,1,512,128]{3,2,1,0:T(8,128)(2,1)} %bitcast.24), channel_id=1, source_target_pairs={{0,1},{1,0},{2,3},{3,2},{4,5},{5,4},{6,7},{7,6},{8,9},{9,8},{10,11... | collective-permute-start | bytes 3145736 | tf_op jit(solution)/shard_map/ppermute | solution.py:1143
  2.3 4.6 %collective-permute-start = (bf16[4,8,16,128]{3,2,1,0:T(8,128)(2,1)S(1)}, bf16[4,8,16,128]{3,2,1,0:T(8,128)(2,1)}, u32[]{:S(2)}, u32[]{:S(2)}) collective-permute-start(bf16[4,8,16,128]{3,2,1,0:T(8,128)(2,1)S(1)} %slice_select_fusion), channel_id=1, source_target_pairs={{0,1},{1,0},{2,3},{3,2},{4,5},{5,4},{6,7},{7,6},{8,9},{9,8},{10,11... | collective-permute-start | bytes 393224 | tf_op jit(solution)/shard_map/ppermute | solution.py:1143
  25.6 24.1 %collective-permute-start.3 = (bf16[528,512]{1,0:T(8,128)(2,1)}, bf16[528,512]{1,0:T(8,128)(2,1)}, u32[]{:S(2)}, u32[]{:S(2)}) collective-permute-start(bf16[528,512]{1,0:T(8,128)(2,1)} %get-tuple-element.29), channel_id=1, source_target_pairs={{0,1},{1,0},{2,3},{3,2},{4,5},{5,4},{6,7},{7,6},{8,9},{9,8},{10,11... | collective-permute-start | bytes 1622024 | tf_op jit(solution)/shard_map/ppermute | solution.py:1143
  25.8 17.6 %collective-permute-start.9 = (bf16[608,128]{1,0:T(8,128)(2,1)}, bf16[608,128]{1,0:T(8,128)(2,1)}, u32[]{:S(2)}, u32[]{:S(2)}) collective-permute-start(bf16[608,128]{1,0:T(8,128)(2,1)} %get-tuple-element.36), channel_id=1, source_target_pairs={{0,10},{2,8},{4,14},{6,12},{8,2},{10,0},{12,6},{14,4},{1,11},{3,9}... | collective-permute-start | bytes 466952 | tf_op jit(solution)/shard_map/ppermute | solution.py:1161
  29.3 17.8 %collective-permute-start.10 = (bf16[608,128]{1,0:T(8,128)(2,1)}, bf16[608,128]{1,0:T(8,128)(2,1)}, u32[]{:S(2)}, u32[]{:S(2)}) collective-permute-start(bf16[608,128]{1,0:T(8,128)(2,1)} %get-tuple-element.37), channel_id=1, source_target_pairs={{0,12},{2,14},{4,8},{6,10},{8,4},{10,6},{12,0},{14,2},{1,13},{3,15... | collective-permute-start | bytes 466952 | tf_op jit(solution)/shard_map/ppermute | solution.py:1161
  29.3 29.4 %collective-permute-start.8 = (bf16[608,128]{1,0:T(8,128)(2,1)}, bf16[608,128]{1,0:T(8,128)(2,1)}, u32[]{:S(2)}, u32[]{:S(2)}) collective-permute-start(bf16[608,128]{1,0:T(8,128)(2,1)} %get-tuple-element.26._), channel_id=1, source_target_pairs={{0,8},{2,10},{4,12},{6,14},{8,0},{10,2},{12,4},{14,6},{1,9},{3,11}... | collective-permute-start | bytes 466952 | tf_op jit(solution)/shard_map/ppermute | solution.py:1161
  43.4 15.3 %collective-permute-start.11 = (bf16[608,128]{1,0:T(8,128)(2,1)}, bf16[608,128]{1,0:T(8,128)(2,1)}, u32[]{:S(2)}, u32[]{:S(2)}) collective-permute-start(bf16[608,128]{1,0:T(8,128)(2,1)} %get-tuple-element.38), channel_id=1, source_target_pairs={{0,14},{2,12},{4,10},{6,8},{8,6},{10,4},{12,2},{14,0},{1,15},{3,13... | collective-permute-start | bytes 466952 | tf_op jit(solution)/shard_map/ppermute | solution.py:1161
  47.2 11.5 %collective-permute-start.5 = (bf16[608,128]{1,0:T(8,128)(2,1)}, bf16[608,128]{1,0:T(8,128)(2,1)}, u32[]{:S(2)}, u32[]{:S(2)}) collective-permute-start(bf16[608,128]{1,0:T(8,128)(2,1)} %get-tuple-element.33), channel_id=1, source_target_pairs={{0,2},{2,0},{4,6},{6,4},{8,10},{10,8},{12,14},{14,12},{1,3},{3,1},... | collective-permute-start | bytes 466952 | tf_op jit(solution)/shard_map/ppermute | solution.py:1161
  47.4 11.3 %collective-permute-start.6 = (bf16[608,128]{1,0:T(8,128)(2,1)}, bf16[608,128]{1,0:T(8,128)(2,1)}, u32[]{:S(2)}, u32[]{:S(2)}) collective-permute-start(bf16[608,128]{1,0:T(8,128)(2,1)} %get-tuple-element.34), channel_id=1, source_target_pairs={{0,4},{2,6},{4,0},{6,2},{8,12},{10,14},{12,8},{14,10},{1,5},{3,7},... | collective-permute-start | bytes 466952 | tf_op jit(solution)/shard_map/ppermute | solution.py:1161
  49.7 10.4 %collective-permute-start.7 = (bf16[608,128]{1,0:T(8,128)(2,1)}, bf16[608,128]{1,0:T(8,128)(2,1)}, u32[]{:S(2)}, u32[]{:S(2)}) collective-permute-start(bf16[608,128]{1,0:T(8,128)(2,1)} %get-tuple-element.35), channel_id=1, source_target_pairs={{0,6},{2,4},{4,2},{6,0},{8,14},{10,12},{12,10},{14,8},{1,7},{3,5},... | collective-permute-start | bytes 466952 | tf_op jit(solution)/shard_map/ppermute | solution.py:1161
  66.0 7.8 %collective-permute-start.16 = (bf16[608,128]{1,0:T(8,128)(2,1)}, bf16[608,128]{1,0:T(8,128)(2,1)}, u32[]{:S(2)}, u32[]{:S(2)}) collective-permute-start(bf16[608,128]{1,0:T(8,128)(2,1)} %get-tuple-element.45), channel_id=1, source_target_pairs={{0,2},{2,0},{4,6},{6,4},{8,10},{10,8},{12,14},{14,12},{1,3},{3,1},... | collective-permute-start | bytes 466952 | tf_op jit(solution)/shard_map/ppermute | solution.py:1161
  67.6 8.9 %collective-permute-start.17 = (bf16[608,128]{1,0:T(8,128)(2,1)}, bf16[608,128]{1,0:T(8,128)(2,1)}, u32[]{:S(2)}, u32[]{:S(2)}) collective-permute-start(bf16[608,128]{1,0:T(8,128)(2,1)} %get-tuple-element.46), channel_id=1, source_target_pairs={{0,4},{2,6},{4,0},{6,2},{8,12},{10,14},{12,8},{14,10},{1,5},{3,7},... | collective-permute-start | bytes 466952 | tf_op jit(solution)/shard_map/ppermute | solution.py:1161
  68.8 21.8 %collective-permute-start.12 = (bf16[608,128]{1,0:T(8,128)(2,1)}, bf16[608,128]{1,0:T(8,128)(2,1)}, u32[]{:S(2)}, u32[]{:S(2)}) collective-permute-start(bf16[608,128]{1,0:T(8,128)(2,1)} %get-tuple-element.40), channel_id=1, source_target_pairs={{0,8},{2,10},{4,12},{6,14},{8,0},{10,2},{12,4},{14,6},{1,9},{3,11}... | collective-permute-start | bytes 466952 | tf_op jit(solution)/shard_map/ppermute | solution.py:1161
  71.0 21.3 %collective-permute-start.13 = (bf16[608,128]{1,0:T(8,128)(2,1)}, bf16[608,128]{1,0:T(8,128)(2,1)}, u32[]{:S(2)}, u32[]{:S(2)}) collective-permute-start(bf16[608,128]{1,0:T(8,128)(2,1)} %get-tuple-element.41), channel_id=1, source_target_pairs={{0,10},{2,8},{4,14},{6,12},{8,2},{10,0},{12,6},{14,4},{1,11},{3,9}... | collective-permute-start | bytes 466952 | tf_op jit(solution)/shard_map/ppermute | solution.py:1161
  71.7 13.0 %collective-permute-start.18 = (bf16[608,128]{1,0:T(8,128)(2,1)}, bf16[608,128]{1,0:T(8,128)(2,1)}, u32[]{:S(2)}, u32[]{:S(2)}) collective-permute-start(bf16[608,128]{1,0:T(8,128)(2,1)} %get-tuple-element.47), channel_id=1, source_target_pairs={{0,6},{2,4},{4,2},{6,0},{8,14},{10,12},{12,10},{14,8},{1,7},{3,5},... | collective-permute-start | bytes 466952 | tf_op jit(solution)/shard_map/ppermute | solution.py:1161
  73.8 22.8 %collective-permute-start.14 = (bf16[608,128]{1,0:T(8,128)(2,1)}, bf16[608,128]{1,0:T(8,128)(2,1)}, u32[]{:S(2)}, u32[]{:S(2)}) collective-permute-start(bf16[608,128]{1,0:T(8,128)(2,1)} %get-tuple-element.42), channel_id=1, source_target_pairs={{0,12},{2,14},{4,8},{6,10},{8,4},{10,6},{12,0},{14,2},{1,13},{3,15... | collective-permute-start | bytes 466952 | tf_op jit(solution)/shard_map/ppermute | solution.py:1161
  76.5 22.2 %collective-permute-start.15 = (bf16[608,128]{1,0:T(8,128)(2,1)}, bf16[608,128]{1,0:T(8,128)(2,1)}, u32[]{:S(2)}, u32[]{:S(2)}) collective-permute-start(bf16[608,128]{1,0:T(8,128)(2,1)} %get-tuple-element.43), channel_id=1, source_target_pairs={{0,14},{2,12},{4,10},{6,8},{8,6},{10,4},{12,2},{14,0},{1,15},{3,13... | collective-permute-start | bytes 466952 | tf_op jit(solution)/shard_map/ppermute | solution.py:1161

commit v2 on v1

--- a/solution.py
+++ b/solution.py
@@ -19,6 +19,15 @@
 weight_unit = 0.25
 
 OWN_COPIES = pltpu.CompilerParams(vmem_limit_bytes=67043328)
+SOME_ROOM = pltpu.CompilerParams(vmem_limit_bytes=41943040)
+
+
+def held_inside(values):
+    return [pltpu.with_memory_space_constraint(value, pltpu.VMEM) for value in values]
+
+
+def held_outside(values):
+    return [pltpu.with_memory_space_constraint(value, pltpu.HBM) for value in values]
 
 
 def whole_block(shape):
@@ -282,48 +291,52 @@
         pltpu.VMEM((-(-count // 2), bases, height, 2 * LANES), jnp.bfloat16),
         pltpu.VMEM((2, rows, bases * LANES), jnp.bfloat16),
         pltpu.VMEM((2, rows, WIDE), jnp.float32),
-        pltpu.VMEM((count, payload_rows(rows), LANES), jnp.bfloat16),
-        pltpu.SemaphoreType.DMA((3 * count,)),
         pltpu.SemaphoreType.DMA((count,)),
     ]
 
 
 class PartAdjoint:
     def __init__(self, places, dual, above, below, outs, scratch, facet_rows):
-        *self.bands, self.tall, self.mixed, self.wide, self.held, loads, self.stores = scratch
+        *self.bands, self.tall, self.mixed, self.wide, loads = scratch
         self.places, self.outs = places, outs
         self.strip_rows = dual.shape[2]
         self.halo = above.shape[2]
         self.margin = self.halo // 2
         self.ends = is_at_ends(facet_rows)
         me = lax.axis_index("chan")
+        self.above, self.below = above, below
         self.copies = []
         for at, place in enumerate(places):
             lanes = pl.ds(at % 2 * LANES, LANES)
-            group = []
-            for source, first, height in (
-                (dual, self.halo, self.strip_rows),
-                (above, 0, self.halo),
-                (below, self.halo + self.strip_rows, self.halo),
-            ):
-                group.append(
-                    pltpu.make_async_copy(
-                        source.at[:, me ^ place],
-                        self.tall.at[at // 2, :, pl.ds(first, height), lanes],
-                        loads.at[3 * at + len(group)],
-                    )
+            self.copies.append(
+                pltpu.make_async_copy(
+                    dual.at[:, me ^ place],
+                    self.tall.at[at // 2, :, pl.ds(self.halo, self.strip_rows), lanes],
+                    loads.at[at],
                 )
-            self.copies.append(group)
+            )
 
     def start(self):
-        for group in self.copies:
-            for copy in group:
-                copy.start()
+        for copy in self.copies:
+            copy.start()
 
     def fill(self, row_taps, col_taps):
         fill_adjoint_bands(row_taps, col_taps, *self.bands, self.margin)
         used = self.strip_rows + 2 * self.halo
         pairs, bases, height, lanes = self.tall.shape
+        is_top, is_low = self.ends
+        me = lax.axis_index("chan")
+        for at, place in enumerate(self.places):
+            mine = slice(at % 2 * LANES, (at % 2 + 1) * LANES)
+            for basis in range(bases):
+                top = self.above[basis, me ^ place]
+                low = self.below[basis, me ^ place]
+                self.tall[at // 2, basis, : self.halo, mine] = jnp.where(
+                    is_top, jnp.zeros_like(top), top
+                )
+                self.tall[at // 2, basis, used - self.halo : used, mine] = jnp.where(
+                    is_low, jnp.zeros_like(low), low
+                )
         if used < height:
             blank = jnp.zeros((height - used, lanes), jnp.bfloat16)
             for pair in range(pairs):
@@ -331,32 +344,16 @@
                     self.tall[pair, basis, used:] = blank
 
     def run(self):
-        stores = []
-        halo, strip_rows = self.halo, self.strip_rows
-        bases, lanes = self.tall.shape[1], self.tall.shape[3]
+        strip_rows = self.strip_rows
         for pair in range(len(self.places) // 2):
-            for group in self.copies[2 * pair : 2 * pair + 2]:
-                for copy in group:
-                    copy.wait()
-            blank = jnp.zeros((halo, lanes), jnp.bfloat16)
-            for condition, first in zip(self.ends, (0, halo + strip_rows)):
-
-                @pl.when(condition)
-                def _(first=first):
-                    for basis in range(bases):
-                        self.tall[pair, basis, first : first + halo] = blank
-
+            for copy in self.copies[2 * pair : 2 * pair + 2]:
+                copy.wait()
             adjoint_of(
                 self.tall.at[pair], self.bands, self.mixed, self.wide, strip_rows, self.margin
             )
             for side in range(2):
                 at = 2 * pair + side
-                write_payload(self.held.at[at], self.wide.at[side], self.margin)
-                stores.append(
-                    pltpu.make_async_copy(self.held.at[at], self.outs[at], self.stores.at[at])
-                )
-                stores[-1].start()
-        return stores
+                write_payload(self.outs[at], self.wide.at[side], self.margin)
 
 
 def part_adjoint_kernel(row_taps, col_taps, dual, above, below, _, *rest, places, facet_rows):
@@ -364,8 +361,7 @@
     part = PartAdjoint(places, dual, above, below, rest[:count], rest[count:], facet_rows)
     part.start()
     part.fill(row_taps, col_taps)
-    for copy in part.run():
-        copy.wait()
+    part.run()
 
 
 def part_adjoint(dual, above, below, row_taps, col_taps, places, facet_rows, after):
@@ -375,13 +371,16 @@
     rows = payload_rows(strip_rows + 2 * margin)
     return pl.pallas_call(
         functools.partial(part_adjoint_kernel, places=places, facet_rows=facet_rows),
-        out_shape=[jax.ShapeDtypeStruct((rows, LANES), jnp.bfloat16)] * len(places),
-        in_specs=[in_scalar_memory()] * 2 + [anywhere] * 4,
-        out_specs=[anywhere] * len(places),
+        out_shape=[pltpu.VMEM((rows, LANES), jnp.bfloat16)] * len(places),
+        in_specs=[in_scalar_memory()] * 2
+        + [anywhere]
+        + [pl.BlockSpec(memory_space=pltpu.VMEM)] * 2
+        + [pl.BlockSpec(memory_space=pl.ANY)],
+        out_specs=[pl.BlockSpec(memory_space=pltpu.VMEM)] * len(places),
         scratch_shapes=part_scratch(bases, strip_rows, margin, len(places)),
-        compiler_params=OWN_COPIES,
+        compiler_params=SOME_ROOM,
         name="part_adjoint",
-    )(row_taps, col_taps, dual, above, below, after)
+    )(*held_outside((row_taps, col_taps, dual)), *held_inside((above, below)), after)
 
 
 def phase_seeds(pixels):
@@ -409,23 +408,16 @@
 
 
 def spectrum_kernel(
-    row_taps, col_taps, dual, above, below, own, other, own_counts, other_counts, *rest,
-    places, margin, facet_rows,
+    own, other, own_counts, other_counts, *rest, margin
 ):
     seeds, (turn_from_re, turn_from_im, _) = rest[:6], rest[6:9]
-    near_outs, rest = rest[9 : 9 + len(places)], rest[9 + len(places) :]
-    freq_out, keep, send = rest[:3]
-    (
-        picture, counts, cosine, sine, freq, turn_re, turn_im, top, low, whole, wide, loads
-    ) = rest[3:15]
+    freq, keep, send = rest[9:12]
+    picture, counts, cosine, sine, turn_re, turn_im, top, low, whole, wide, loads = rest[12:]
     split = lax.axis_index("split")
-    cols, _, strip_rows, _ = own.shape
+    cols, facet_rows, strip_rows, _ = own.shape
     pixels = picture.shape[0]
     half = pixels // 2
     part = half // 2
-    if places:
-        near = PartAdjoint(places, dual, above, below, near_outs, rest[15:], facet_rows)
-        near.start()
 
     def strip_at(facet_row, which):
         return pl.multiple_of((2 * facet_row + which) * strip_rows, strip_rows)
@@ -434,38 +426,36 @@
     for facet_row in range(facet_rows):
         for col in range(cols):
             lanes = pl.ds(col * LANES, LANES)
-            for source, which in ((own, split), (other, 1 - split)):
-                copies.append(
-                    pltpu.make_async_copy(
-                        source.at[col, facet_row],
-                        picture.at[pl.ds(strip_at(facet_row, which), strip_rows), lanes],
-                        loads.at[len(copies)],
-                    )
+            copies.append(
+                pltpu.make_async_copy(
+                    own.at[col, facet_row],
+                    picture.at[pl.ds(strip_at(facet_row, split), strip_rows), lanes],
+                    loads.at[len(copies)],
                 )
+            )
     for source, target in ((turn_from_re, turn_re), (turn_from_im, turn_im)):
         copies.append(pltpu.make_async_copy(source, target, loads.at[len(copies)]))
     count_copies = []
-    for source, which in ((own_counts, split), (other_counts, 1 - split)):
-        for tile in range(part // LANES):
-            lanes = pl.ds(pl.multiple_of(split * part + tile * LANES, LANES), LANES)
-            count_copies.append(
-                pltpu.make_async_copy(
-                    source.at[:, lanes],
-                    counts.at[tile, pl.ds(pl.multiple_of(which * half, half), half), :],
-                    loads.at[len(copies) + len(count_copies)],
-                )
+    for tile in range(part // LANES):
+        lanes = pl.ds(pl.multiple_of(split * part + tile * LANES, LANES), LANES)
+        count_copies.append(
+            pltpu.make_async_copy(
+                own_counts.at[:, lanes],
+                counts.at[tile, pl.ds(pl.multiple_of(split * half, half), half), :],
+                loads.at[len(copies) + len(count_copies)],
             )
+        )
     for copy in (*copies, *count_copies):
         copy.start()
-    if places:
-        near.fill(row_taps, col_taps)
     fill_transforms(seeds, cosine, sine, freq)
-    stores = [
-        pltpu.make_async_copy(freq, freq_out, loads.at[len(copies) + len(count_copies)])
-    ]
-    stores[0].start()
-    if places:
-        stores += near.run()
+    for facet_row in range(facet_rows):
+        there = pl.ds(strip_at(facet_row, 1 - split), strip_rows)
+        for col in range(cols):
+            picture[there, col * LANES : (col + 1) * LANES] = other[col, facet_row]
+    for tile in range(part // LANES):
+        lanes = pl.ds(pl.multiple_of(split * part + tile * LANES, LANES), LANES)
+        there = pl.ds(pl.multiple_of((1 - split) * half, half), half)
+        counts[tile, there, :] = other_counts[:, lanes]
     for copy in copies:
         copy.wait()
     block = min(256, half)
@@ -549,58 +539,52 @@
                 axis=0,
             )
             target[base + strip_rows : base + rows, :] = ends.astype(jnp.bfloat16)
-    for copy in stores:
-        copy.wait()
-
-
-def spectrum(
-    own, other, own_counts, other_counts, dual, above, below, row_taps, col_taps, places, margin, after
-):
+
+
+def spectrum(own, other, own_counts, other_counts, margin, after):
     cols, facet_rows, strip_rows, lanes = own.shape
-    bases = dual.shape[0]
     pixels = cols * lanes
     half = pixels // 2
     rows = facet_rows * (strip_rows + 2 * margin)
-    shape = jax.ShapeDtypeStruct((rows, half), jnp.bfloat16)
     anywhere = pl.BlockSpec(memory_space=pltpu.HBM)
     inside = pl.BlockSpec(memory_space=pltpu.VMEM)
-    payload = jax.ShapeDtypeStruct((payload_rows(strip_rows + 2 * margin), lanes), jnp.bfloat16)
-    result = pl.pallas_call(
-        functools.partial(
-            spectrum_kernel, places=places, margin=margin, facet_rows=facet_rows
-        ),
-        out_shape=[payload] * len(places)
-        + [jax.ShapeDtypeStruct((pixels, pixels), jnp.bfloat16), shape, shape],
-        in_specs=[in_scalar_memory()] * 2 + [anywhere] * 7 + [inside] * 6 + [anywhere] * 3,
-        out_specs=[anywhere] * (len(places) + 1) + [inside] * 2,
+    return pl.pallas_call(
+        functools.partial(spectrum_kernel, margin=margin),
+        out_shape=[
+            pltpu.VMEM((pixels, pixels), jnp.bfloat16),
+            pltpu.VMEM((rows, half), jnp.bfloat16),
+            pltpu.VMEM((rows, half), jnp.bfloat16),
+        ],
+        in_specs=[anywhere, inside] * 2
+        + [inside] * 6
+        + [anywhere] * 2
+        + [pl.BlockSpec(memory_space=pl.ANY)],
+        out_specs=[inside] * 3,
         scratch_shapes=[
             pltpu.VMEM((pixels, pixels), jnp.bfloat16),
             pltpu.VMEM((half // 2 // LANES, pixels, LANES), jnp.int32),
             pltpu.VMEM((half, half), jnp.bfloat16),
             pltpu.VMEM((half, half), jnp.bfloat16),
-            pltpu.VMEM((pixels, pixels), jnp.bfloat16),
             pltpu.VMEM((half, LANES), jnp.float32),
             pltpu.VMEM((half, LANES), jnp.float32),
             pltpu.VMEM((half, pixels), jnp.bfloat16),
             pltpu.VMEM((half, pixels), jnp.bfloat16),
             pltpu.VMEM((half, pixels), jnp.bfloat16),
             pltpu.VMEM((pixels, half), jnp.bfloat16),
-            pltpu.SemaphoreType.DMA((2 * cols * facet_rows + 3 + half // LANES,)),
-        ]
-        + (part_scratch(bases, strip_rows, margin, len(places)) if places else []),
-        compiler_params=OWN_COPIES,
+            pltpu.SemaphoreType.DMA((cols * facet_rows + 2 + half // LANES,)),
+        ],
+        compiler_params=SOME_ROOM,
         name="spectrum",
     )(
-        row_taps, col_taps, dual, above, below, own, other, own_counts, other_counts,
+        *held_outside((own,)), *held_inside((other,)),
+        *held_outside((own_counts,)), *held_inside((other_counts,)),
         *phase_seeds(pixels), *twiddles(pixels), after,
     )
-    return result[: len(places)], *result[len(places) :]
 
 
 def gradient_kernel(
-    kept, got, freq_from, own_from, other, dirty_from, other_dirty, out, edge_out,
-    joined, freq, own, dirty, above, below, dirty_above, dirty_below, stepped, loads, stores,
-    *, margin
+    kept, got, freq, own_from, other, dirty_from, other_dirty, stepped, edge_out, own,
+    joined, dirty, loads, *, margin
 ):
     split = lax.axis_index("split")
     cols, facet_rows, strip_rows, _ = own.shape
@@ -615,40 +599,29 @@
         started.append(copy)
         return copy
 
-    first = [load(kept, joined.at[:, pl.ds(0, half)])]
     steps = []
     for step in range(cols // pair):
-        lines = pl.ds(step * pair * LANES, pair * LANES)
         some = pl.ds(step * pair, pair)
         steps.append(
             [
-                load(freq_from.at[lines], freq.at[lines]),
                 load(own_from.at[some], own.at[some]),
                 load(dirty_from.at[some], dirty.at[some]),
             ]
         )
-        if step == 0:
-            first.append(load(got, joined.at[:, pl.ds(half, half)]))
-            last, start = pl.ds(strip_rows - 16, 16), pl.ds(0, 16)
-            first.append(load(other.at[:, :, last], above))
-            first.append(load(other.at[:, :, start], below))
-            first.append(load(other_dirty.at[:, :, last], dirty_above))
-            first.append(load(other_dirty.at[:, :, start], dirty_below))
-
-    def edges(upper, lower, col, facet_row):
+
+    def edges(source, col, facet_row):
         over = jnp.maximum(facet_row - 1 + split, 0)
         under = jnp.minimum(facet_row + split, facet_rows - 1)
         return jnp.concatenate(
             [
-                upper[col, over].astype(jnp.float32)[16 - margin :],
-                lower[col, under].astype(jnp.float32)[:margin],
+                source[col, over, strip_rows - 16 :].astype(jnp.float32)[16 - margin :],
+                source[col, under, :16].astype(jnp.float32)[:margin],
             ],
             axis=0,
         )
 
-    for copy in first:
-        copy.wait()
-    stored = []
+    joined[:, :half] = kept[...]
+    joined[:, half:] = got[...]
     for step in range(cols // pair):
         for copy in steps[step]:
             copy.wait()
@@ -667,17 +640,12 @@
                     grad[:strip_rows] - dirty[col, facet_row].astype(jnp.float32)
                 )
                 stepped[col, facet_row, :strip_rows] = moved.astype(jnp.bfloat16)
-                image = edges(above, below, col, facet_row)
+                image = edges(other, col, facet_row)
                 moved = image - primal_step * (
-                    grad[strip_rows:] - edges(dirty_above, dirty_below, col, facet_row)
+                    grad[strip_rows:] - edges(other_dirty, col, facet_row)
                 )
                 stepped[col, facet_row, strip_rows:] = moved.astype(jnp.bfloat16)
                 edge_out[col, facet_row] = image.astype(jnp.bfloat16)
-        some = pl.ds(step * pair, pair)
-        stored.append(pltpu.make_async_copy(stepped.at[some], out.at[some], stores.at[step]))
-        stored[-1].start()
-    for copy in stored:
-        copy.wait()
 
 
 def gradient_step(kept, got, freq, own, other, own_dirty, other_dirty, margin):
@@ -685,28 +653,27 @@
     pixels = cols * lanes
     rows = strip_rows + 2 * margin
     anywhere = pl.BlockSpec(memory_space=pltpu.HBM)
-    edge = (cols, facet_rows, 16, lanes)
+    inside = pl.BlockSpec(memory_space=pltpu.VMEM)
     return pl.pallas_call(
         functools.partial(gradient_kernel, margin=margin),
         out_shape=[
-            jax.ShapeDtypeStruct((cols, facet_rows, rows, lanes), jnp.bfloat16),
-            jax.ShapeDtypeStruct((cols, facet_rows, 2 * margin, lanes), jnp.bfloat16),
+            pltpu.VMEM((cols, facet_rows, rows, lanes), jnp.bfloat16),
+            pltpu.VMEM((cols, facet_rows, 2 * margin, lanes), jnp.bfloat16),
+            pltpu.VMEM(own.shape, jnp.bfloat16),
         ],
-        in_specs=[anywhere] * 7,
-        out_specs=[anywhere, pl.BlockSpec(memory_space=pltpu.VMEM)],
+        in_specs=[inside] * 3 + [anywhere, inside] * 2,
+        out_specs=[inside] * 3,
         scratch_shapes=[
             pltpu.VMEM((kept.shape[0], pixels), jnp.bfloat16),
-            pltpu.VMEM(freq.shape, jnp.bfloat16),
             pltpu.VMEM(own.shape, jnp.bfloat16),
-            pltpu.VMEM(own.shape, jnp.bfloat16),
-            *[pltpu.VMEM(edge, jnp.bfloat16)] * 4,
-            pltpu.VMEM((cols, facet_rows, rows, lanes), jnp.bfloat16),
-            pltpu.SemaphoreType.DMA((6 + 3 * cols,)),
-            pltpu.SemaphoreType.DMA((cols,)),
+            pltpu.SemaphoreType.DMA((2 * cols,)),
         ],
-        compiler_params=OWN_COPIES,
+        compiler_params=SOME_ROOM,
         name="gradient",
-    )(kept, got, freq, own, other, own_dirty, other_dirty)
+    )(
+        *held_inside((kept, got, freq)), *held_outside((own,)), *held_inside((other,)),
+        *held_outside((own_dirty,)), *held_inside((other_dirty,)),
+    )
 
 
 def unpacked(packed, group, count, margin):
@@ -715,34 +682,18 @@
     )
 
 
-def update_kernel(stepped_from, image_from, edges, *rest, margin, facets, single):
+def update_kernel(stepped, edges, image, *rest, margin, facets, single):
     arrivals = 1 if single else facets
     blocks = rest[:arrivals]
     new_out = rest[arrivals]
     outs = rest[arrivals + 1 : 2 * arrivals + 1]
-    stepped, image, new_image, adjoint, apart, extrapolated, leaving = rest[2 * arrivals + 1 : -3]
-    loads, arriving, stores = rest[-3:]
+    new_image, adjoint, apart, extrapolated, stores = rest[2 * arrivals + 1 :]
     me = lax.axis_index("chan")
     split = lax.axis_index("split")
     cols, facet_rows, rows, _ = stepped.shape
     strip_rows = rows - 2 * margin
     height = pack_height(rows)
     lane = lax.broadcasted_iota(jnp.int32, (1, LANES), 1)
-    arrive = []
-    for place, block in enumerate(blocks):
-        target = adjoint if single else adjoint.at[me ^ place]
-        arrive.append(pltpu.make_async_copy(block, target, arriving.at[place]))
-        arrive[-1].start()
-    load = []
-    for col in range(cols):
-        load.append(
-            (
-                pltpu.make_async_copy(stepped_from.at[col], stepped.at[col], loads.at[2 * col]),
-                pltpu.make_async_copy(image_from.at[col], image.at[col], loads.at[2 * col + 1]),
-            )
-        )
-        for copy in load[-1]:
-            copy.start()
 
     def unpack(facet):
         tile = adjoint[facet, rows : rows + height, :].astype(jnp.float32)
@@ -751,12 +702,13 @@
                 tile, group, count, margin
             ).astype(jnp.bfloat16)
 
-    for place, copy in enumerate(arrive):
-        copy.wait()
-        if not single:
+    if single:
+        adjoint = blocks[0]
+        each(facets, unpack)
+    else:
+        for place, block in enumerate(blocks):
+            adjoint[me ^ place] = block[...]
             unpack(me ^ place)
-    if single:
-        each(facets, unpack)
 
     def sides(take, group, count, left, has_left, right, has_right):
         from_left = take(left, group, count)
@@ -806,8 +758,6 @@
 
     stored = []
     for col in range(cols):
-        for copy in load[col]:
-            copy.wait()
         for facet_row in range(facet_rows):
             update(col * facet_rows + facet_row)
         stored.append(
@@ -835,28 +785,22 @@
         out[rows:, :] = packed.astype(jnp.bfloat16)
 
     if single:
-        each(facets, lambda facet: write(leaving.at[facet], facet))
-        stored.append(pltpu.make_async_copy(leaving, outs[0], stores.at[cols]))
-        stored[-1].start()
+        each(facets, lambda facet: write(outs[0].at[facet], facet))
     else:
-        for place in reversed(range(facets)):
-            write(leaving.at[place], me ^ place)
-            stored.append(
-                pltpu.make_async_copy(leaving.at[place], outs[place], stores.at[cols + place])
-            )
-            stored[-1].start()
+        for place, out in enumerate(outs):
+            write(out, me ^ place)
     for copy in stored:
         copy.wait()
 
 
-def update_step(stepped, image, edges, blocks, margin, single):
+def update_step(stepped, edges, image, blocks, margin, single):
     cols, facet_rows, rows, lanes = stepped.shape
     facets = cols * facet_rows
     tall_rows = payload_rows(rows)
     arrivals = (
-        [jax.ShapeDtypeStruct((facets, tall_rows, lanes), jnp.bfloat16)]
+        [pltpu.VMEM((facets, tall_rows, lanes), jnp.bfloat16)]
         if single
-        else [jax.ShapeDtypeStruct((tall_rows, lanes), jnp.bfloat16)] * facets
+        else [pltpu.VMEM((tall_rows, lanes), jnp.bfloat16)] * facets
     )
     anywhere = pl.BlockSpec(memory_space=pltpu.HBM)
     results = pl.pallas_call(
@@ -865,23 +809,18 @@
             jax.ShapeDtypeStruct((cols, facet_rows, rows - 2 * margin, lanes), jnp.bfloat16)
         ]
         + arrivals,
-        in_specs=[anywhere] * 2 + [pl.BlockSpec(memory_space=pltpu.VMEM)] + [anywhere] * len(blocks),
-        out_specs=[anywhere] * (1 + len(arrivals)),
+        in_specs=[pl.BlockSpec(memory_space=pltpu.VMEM)] * (3 + len(blocks)),
+        out_specs=[anywhere] + [pl.BlockSpec(memory_space=pltpu.VMEM)] * len(arrivals),
         scratch_shapes=[
-            pltpu.VMEM(stepped.shape, jnp.bfloat16),
             pltpu.VMEM(image.shape, jnp.bfloat16),
-            pltpu.VMEM(image.shape, jnp.bfloat16),
-            pltpu.VMEM((facets, tall_rows, lanes), jnp.bfloat16),
+            pltpu.VMEM((1, 16, lanes) if single else (facets, tall_rows, lanes), jnp.bfloat16),
             pltpu.VMEM((facets, rows, lanes), jnp.bfloat16),
             pltpu.VMEM((facets, rows, lanes), jnp.bfloat16),
-            pltpu.VMEM((facets, tall_rows, lanes), jnp.bfloat16),
-            pltpu.SemaphoreType.DMA((2 * cols,)),
-            pltpu.SemaphoreType.DMA((len(blocks),)),
-            pltpu.SemaphoreType.DMA((cols + len(blocks),)),
+            pltpu.SemaphoreType.DMA((cols,)),
         ],
-        compiler_params=OWN_COPIES,
+        compiler_params=SOME_ROOM,
         name="update",
-    )(stepped, image, edges, *blocks)
+    )(*held_inside((stepped, edges, image, *blocks)))
     return results[0], results[1:]
 
 
@@ -990,12 +929,11 @@
     count = len(places)
     blocks, rest = rest[:count], rest[count:]
     if final:
-        mask, before_from, total_from, out_to = rest[:4]
-        rest = rest[4:]
+        mask, before, total, field, out_to = rest[:5]
+        row_band, col_band, wide, tall, held, scaled, loads, stores = rest[5:]
     else:
-        out_to, total_to = rest[:2]
-        rest = rest[2:]
-    row_band, col_band, arrived, wide, tall, field, held, before, total, loads, stores = rest
+        held, total, ahead = rest[:3]
+        row_band, col_band, wide, tall, field, loads, stores = rest[3:]
     me = lax.axis_index("chan")
     bases, taps = row_taps.shape
     halo = 2 * margin
@@ -1017,16 +955,18 @@
         copy.start()
         stored.append(copy)
 
-    arrive = [load(block, arrived.at[at]) for at, block in enumerate(blocks)]
     fields = []
-    for basis in range(bases):
-        group = [
-            load(dual.at[basis, me ^ place], field.at[basis, at]) for at, place in enumerate(places)
-        ]
-        if final:
-            group.append(load(before_from.at[basis], before.at[basis]))
-            group.append(load(total_from.at[basis], total.at[basis]))
-        fields.append(group)
+    for basis in range(0 if final else bases):
+        fields.append(
+            [
+                load(dual.at[basis, me ^ place], field.at[basis, at])
+                for at, place in enumerate(places)
+            ]
+        )
+    further = []
+    for basis in range(0 if final else bases):
+        for at, place in enumerate(places):
+            further.append(load(dual.at[basis, me ^ place ^ count], ahead.at[basis, at]))
     for basis in range(bases):
         seed = band_seed(row_taps, basis, [margin + tap for tap in range(taps)])
         fill_band(row_band.at[basis], 0, BAND_ROWS, seed)
@@ -1035,8 +975,7 @@
             tall[basis, used:] = jnp.zeros((tall.shape[1] - used, tall.shape[2]), jnp.bfloat16)
     fill_col_bands(col_band, col_taps, bases, margin)
     for at in range(count):
-        arrive[at].wait()
-        block = arrived.at[at]
+        block = blocks[at]
         wide[at, :, :LANES] = block[:rows, :]
         packed = block[rows : rows + height, :].astype(jnp.float32)
         for group, first, some in row_groups(rows):
@@ -1057,8 +996,9 @@
                 [mine[strip_rows + margin :], blank], axis=0
             ).astype(jnp.bfloat16)
     for basis in range(bases):
-        for copy in fields[basis]:
-            copy.wait()
+        if not final:
+            for copy in fields[basis]:
+                copy.wait()
         for first in range(0, strip_rows, BAND_ROWS):
             some = min(BAND_ROWS, strip_rows - first)
             here = slice(first, first + some)
@@ -1081,7 +1021,7 @@
                 for at in range(count):
                     held[basis, at, here] = (stepped[at] * scale).astype(jnp.bfloat16)
                     earlier = before[basis, at, here].astype(jnp.float32)
-                    before[basis, at, here] = (earlier * scale).astype(jnp.bfloat16)
+                    scaled[basis, at, here] = (earlier * scale).astype(jnp.bfloat16)
             else:
                 total[basis, here] = squares
                 for at in range(count):
@@ -1089,11 +1029,8 @@
         if final:
             for at, place in enumerate(places):
                 store(held.at[basis, at], out_to.at[basis, me ^ place])
-                store(before.at[basis, at], out_to.at[basis, me ^ place ^ count])
-        else:
-            store(held.at[basis], out_to.at[basis])
-            store(total.at[basis], total_to.at[basis])
-    for copy in stored:
+                store(scaled.at[basis, at], out_to.at[basis, me ^ place ^ count])
+    for copy in (*stored, *further):
         copy.wait()
 
 
@@ -1105,38 +1042,40 @@
     anywhere = pl.BlockSpec(memory_space=pltpu.HBM)
     part = (bases, count, strip_rows, lanes)
     final = earlier is not None
+    inside = pl.BlockSpec(memory_space=pltpu.VMEM)
+    bands = [
+        pltpu.VMEM((bases, BAND_ROWS, WIDE), jnp.bfloat16),
+        pltpu.VMEM((bases * LANES, WIDE), jnp.bfloat16),
+        pltpu.VMEM((count, rows, WIDE), jnp.bfloat16),
+        pltpu.VMEM((bases, tall_height(strip_rows, margin), count * lanes), jnp.bfloat16),
+    ]
+    field = pltpu.VMEM(part, jnp.bfloat16)
     if final:
-        more = (pl.BlockSpec(memory_space=pltpu.VMEM), anywhere, anywhere)
         out_shape = jax.ShapeDtypeStruct(dual.shape, jnp.bfloat16)
         out_specs = anywhere
+        scratch = [field, field]
     else:
-        more, earlier = (), ()
-        out_shape = [
-            jax.ShapeDtypeStruct(part, jnp.bfloat16),
-            jax.ShapeDtypeStruct((bases, strip_rows, lanes), jnp.float32),
-        ]
-        out_specs = [anywhere, anywhere]
+        earlier = ()
+        out_shape = [field, pltpu.VMEM((bases, strip_rows, lanes), jnp.float32), field]
+        out_specs = [inside] * 3
+        scratch = [field]
     return pl.pallas_call(
         functools.partial(shrink_part_kernel, places=places, margin=margin, final=final),
         out_shape=out_shape,
-        in_specs=[in_scalar_memory()] * 2 + [anywhere] * (1 + count) + list(more),
+        in_specs=[in_scalar_memory()] * 2 + [anywhere] + [inside] * (count + len(earlier)),
         out_specs=out_specs,
-        scratch_shapes=[
-            pltpu.VMEM((bases, BAND_ROWS, WIDE), jnp.bfloat16),
-            pltpu.VMEM((bases * LANES, WIDE), jnp.bfloat16),
-            pltpu.VMEM((count, payload_rows(rows), lanes), jnp.bfloat16),
-            pltpu.VMEM((count, rows, WIDE), jnp.bfloat16),
-            pltpu.VMEM((bases, tall_height(strip_rows, margin), count * lanes), jnp.bfloat16),
-            pltpu.VMEM(part, jnp.bfloat16),
-            pltpu.VMEM(part, jnp.bfloat16),
-            pltpu.VMEM(part if final else (1, 1, 16, lanes), jnp.bfloat16),
-            pltpu.VMEM((bases, strip_rows, lanes), jnp.float32),
-            pltpu.SemaphoreType.DMA((count + bases * (count + 2),)),
+        scratch_shapes=bands
+        + scratch
+        + [
+            pltpu.SemaphoreType.DMA((2 * bases * count,)),
             pltpu.SemaphoreType.DMA((2 * bases * count,)),
         ],
-        compiler_params=OWN_COPIES,
+        compiler_params=SOME_ROOM,
         name="shrink_part",
-    )(row_taps, col_taps, dual, *blocks, *earlier)
+    )(
+        *held_outside((row_taps, col_taps, dual)),
+        *held_inside((*blocks, *earlier)),
+    )
 
 
 def swapped(value):
@@ -1196,16 +1135,13 @@
         far = adjoint(tuple(range(count // 2, count)), facet_rows, row_taps)
         near = adjoint(tuple(range(count // 2)), facet_rows, far[0])
         blocks = [*near, *far]
-    _, freq, kept, sent = spectrum(
-        image, other_image, counts, other_counts, dual, above, below,
-        row_taps, col_taps, (), margin, blocks[0],
-    )
+    freq, kept, sent = spectrum(image, other_image, counts, other_counts, margin, blocks[0])
     arrived = crossed(blocks, single)
     got = swapped(sent)
-    stepped, edges = gradient_step(
+    stepped, edges, pixels = gradient_step(
         kept, got, freq, image, other_image, dirty, other_dirty, margin
     )
-    new_image, blocks = update_step(stepped, image, edges, arrived, margin, single)
+    new_image, blocks = update_step(stepped, edges, pixels, arrived, margin, single)
     arrived = crossed(blocks, single)
     if single:
         new_dual = shrink_step(row_taps, col_taps, mask, dual, arrived, single)

time: 107 us -> 96.4 us (0.901)
  Pallas kernels: 44 us -> 31.2 us
  waiting for transfers between devices: 39 us -> 41.7 us
    pallas_call x2, Pallas kernels: 13.2 us -> 9.82 us  [shrink_part(): pl.pallas_call(functools.partial(shrink_part_kernel, places=places, margi...]
    pallas_call x1, Pallas kernels: 5.88 us -> 2.61 us  [update_step(): pl.pallas_call(functools.partial(update_kernel, margin=margin, facets=fac...]
    ppermute x14, waiting for transfers between devices: 34.9 us -> 37.7 us  [crossed(): lax.ppermute(blocks[place], 'chan', [(i, i ^ place) for i in range(count)])]
    pallas_call x1, Pallas kernels: 8.92 us -> 6.53 us  [spectrum(): pl.pallas_call(functools.partial(spectrum_kernel, margin=margin), out_sha...]
    pallas_call x1, Pallas kernels: 6.18 us -> 4.16 us  [gradient_step(): pl.pallas_call(functools.partial(gradient_kernel, margin=margin), out_sha...]
    pallas_call x2, Pallas kernels: 9.76 us -> 8.08 us  [part_adjoint(): pl.pallas_call(functools.partial(part_adjoint_kernel, places=places, face...]
  transfers between devices with their start and end apart: 19 -> 19, of which waited for: 10 -> 10; matrix products, arithmetic and copies ran while one was open for 1% -> 1% of each run, Pallas kernels for 29% -> 24%
where the time goes in v2:
time: 96.4 us; the launch traced here: 96.1 us
  waiting for transfers between devices  41.7 us (43%)
  Pallas kernels  31.2 us (32%)
  starting transfers between devices  21.2 us (22%)
  between operations  1.02 us (1%)
  other arithmetic  0.99 us (1%)
    ppermute x14, waiting for transfers between devices, crossed(): lax.ppermute(blocks[place], 'chan', [(i, i ^ place) for i in range(count)])  37.7 us
    ppermute x14, starting transfers between devices, crossed(): lax.ppermute(blocks[place], 'chan', [(i, i ^ place) for i in range(count)])  19.9 us
    pallas_call x2, Pallas kernels, shrink_part(): pl.pallas_call(functools.partial(shrink_part_kernel, places=places, margi...  9.82 us
    pallas_call x2, Pallas kernels, part_adjoint(): pl.pallas_call(functools.partial(part_adjoint_kernel, places=places, face...  8.08 us
    pallas_call x1, Pallas kernels, spectrum(): pl.pallas_call(functools.partial(spectrum_kernel, margin=margin), out_sha...  6.53 us
    pallas_call x1, Pallas kernels, gradient_step(): pl.pallas_call(functools.partial(gradient_kernel, margin=margin), out_sha...  4.16 us
    ppermute x5, waiting for transfers between devices, swapped(): return lax.ppermute(value, 'split', [(0, 1), (1, 0)])  3.99 us
    pallas_call x1, Pallas kernels, update_step(): pl.pallas_call(functools.partial(update_kernel, margin=margin, facets=fac...  2.61 us
  transfers between devices with their start and end apart: 19, of which 10 were waited for; matrix products, arithmetic and copies ran while one was open for 1% of the time, Pallas kernels for 24%

profile of v2, /device:TPU:8, one launch (start us, length us, event | category | flops | bytes accessed | tf_op | source)
XLA Modules:
  0.0 96.1 jit_solution(5295675387928292835)
XLA Ops:
  2.8 4.0 %collective-permute-done.2.above.below = bf16[4,8,16,128]{3,2,1,0:T(8,128)(2,1)S(1)} collective-permute-done((bf16[4,8,16,128]{3,2,1,0:T(8,128)(2,1)S(1)}, bf16[4,8,16,128]{3,2,1,0:T(8,128)(2,1)S(1)}, u32[]{:S(2)}, u32[]{:S(2)}) %collective-permute-start.2) | collective-permute-done | bytes 131104 | tf_op jit(solution)/shard_map/ppermute | solution.py:1082
  6.8 4.0 %part_adjoint.2 = (bf16[608,128]{1,0:T(8,128)(2,1)S(1)}, bf16[608,128]{1,0:T(8,128)(2,1)S(1)}, bf16[608,128]{1,0:T(8,128)(2,1)S(1)}, bf16[608,128]{1,0:T(8,128)(2,1)S(1)}) custom-call(f32[4,17]{1,0:T(4,128)} %row_taps.7, f32[4,17]{1,0:T(4,128)} %col_taps.7, bf16[4,8,512,128]{3,2,1,0:T(8,128)(2,1)} %bitcast.13, ...), custom_call_target="tpu_custom_call" | custom-call | tf_op jit(solution)/shard_map/part_adjoint/pallas_call | solution.py:372
  10.8 4.1 %part_adjoint.3 = (bf16[608,128]{1,0:T(8,128)(2,1)S(1)}, bf16[608,128]{1,0:T(8,128)(2,1)S(1)}, bf16[608,128]{1,0:T(8,128)(2,1)S(1)}, bf16[608,128]{1,0:T(8,128)(2,1)S(1)}) custom-call(f32[4,17]{1,0:T(4,128)} %row_taps.7, f32[4,17]{1,0:T(4,128)} %col_taps.7, bf16[4,8,512,128]{3,2,1,0:T(8,128)(2,1)} %bitcast.14, ...), custom_call_target="tpu_custom_call" | custom-call | tf_op jit(solution)/shard_map/part_adjoint/pallas_call | solution.py:372
  15.1 6.5 %spectrum.1 = (bf16[1024,1024]{1,0:T(8,128)(2,1)S(1)}, bf16[528,512]{1,0:T(8,128)(2,1)S(1)}, bf16[528,512]{1,0:T(8,128)(2,1)S(1)}) custom-call(bf16[8,1,512,128]{3,2,1,0:T(8,128)(2,1)} %bitcast.18, bf16[8,1,512,128]{3,2,1,0:T(8,128)(2,1)S(1)} %collective-permute-done.other, s32[512,512]{1,0:T(8,128)} %bitcast.24, ...), custom_call_target="tpu_custom_call" | custom-call | tf_op jit(solution)/shard_map/spectrum/pallas_call | solution.py:551
  21.8 3.5 %collective-permute-start.9 = (bf16[608,128]{1,0:T(8,128)(2,1)S(1)}, bf16[608,128]{1,0:T(8,128)(2,1)S(1)}, u32[]{:S(2)}, u32[]{:S(2)}) collective-permute-start(bf16[608,128]{1,0:T(8,128)(2,1)S(1)} %get-tuple-element.39), channel_id=1, source_target_pairs={{0,10},{2,8},{4,14},{6,12},{8,2},{10,0},{12,6},{14,4},{1,11},{3,9}... | collective-permute-start | bytes 466952 | tf_op jit(solution)/shard_map/ppermute | solution.py:1100
  25.3 2.8 %collective-permute-start.8 = (bf16[608,128]{1,0:T(8,128)(2,1)S(1)}, bf16[608,128]{1,0:T(8,128)(2,1)S(1)}, u32[]{:S(2)}, u32[]{:S(2)}) collective-permute-start(bf16[608,128]{1,0:T(8,128)(2,1)S(1)} %get-tuple-element.28._), channel_id=1, source_target_pairs={{0,8},{2,10},{4,12},{6,14},{8,0},{10,2},{12,4},{14,6},{1,9},{3,11}... | collective-permute-start | bytes 466952 | tf_op jit(solution)/shard_map/ppermute | solution.py:1100
  28.1 11.0 %collective-permute-done.9.rest_5_ = bf16[608,128]{1,0:T(8,128)(2,1)S(1)} collective-permute-done((bf16[608,128]{1,0:T(8,128)(2,1)S(1)}, bf16[608,128]{1,0:T(8,128)(2,1)S(1)}, u32[]{:S(2)}, u32[]{:S(2)}) %collective-permute-start.9) | collective-permute-done | bytes 155680 | tf_op jit(solution)/shard_map/ppermute | solution.py:1100
  39.1 3.8 %collective-permute-done.10.rest_6_ = bf16[608,128]{1,0:T(8,128)(2,1)S(1)} collective-permute-done((bf16[608,128]{1,0:T(8,128)(2,1)S(1)}, bf16[608,128]{1,0:T(8,128)(2,1)S(1)}, u32[]{:S(2)}, u32[]{:S(2)}) %collective-permute-start.10) | collective-permute-done | bytes 155680 | tf_op jit(solution)/shard_map/ppermute | solution.py:1100
  43.1 2.3 %collective-permute-start.6 = (bf16[608,128]{1,0:T(8,128)(2,1)S(1)}, bf16[608,128]{1,0:T(8,128)(2,1)S(1)}, u32[]{:S(2)}, u32[]{:S(2)}) collective-permute-start(bf16[608,128]{1,0:T(8,128)(2,1)S(1)} %get-tuple-element.37), channel_id=1, source_target_pairs={{0,4},{2,6},{4,0},{6,2},{8,12},{10,14},{12,8},{14,10},{1,5},{3,7},... | collective-permute-start | bytes 466952 | tf_op jit(solution)/shard_map/ppermute | solution.py:1100
  46.4 4.2 %gradient.1 = (bf16[8,1,528,128]{3,2,1,0:T(8,128)(2,1)S(1)}, bf16[8,1,16,128]{3,2,1,0:T(8,128)(2,1)S(1)}, bf16[8,1,512,128]{3,2,1,0:T(8,128)(2,1)S(1)}) custom-call(bf16[528,512]{1,0:T(8,128)(2,1)S(1)} %get-tuple-element.30.kept, bf16[528,512]{1,0:T(8,128)(2,1)S(1)} %collective-permute-done.3.got, bf16[1024,1024]{1,0:T(8,128)(2,1)S(1)} %get-tuple-element.32.freq, ...), custom_call_target="tpu_custom_call" | custom-call | tf_op jit(solution)/shard_map/gradient/pallas_call | solution.py:657
  50.6 4.0 %collective-permute-done.11.rest_7_ = bf16[608,128]{1,0:T(8,128)(2,1)S(1)} collective-permute-done((bf16[608,128]{1,0:T(8,128)(2,1)S(1)}, bf16[608,128]{1,0:T(8,128)(2,1)S(1)}, u32[]{:S(2)}, u32[]{:S(2)}) %collective-permute-start.11) | collective-permute-done | bytes 155680 | tf_op jit(solution)/shard_map/ppermute | solution.py:1100
  54.5 1.1 %collective-permute-done.7.rest_3_ = bf16[608,128]{1,0:T(8,128)(2,1)S(1)} collective-permute-done((bf16[608,128]{1,0:T(8,128)(2,1)S(1)}, bf16[608,128]{1,0:T(8,128)(2,1)S(1)}, u32[]{:S(2)}, u32[]{:S(2)}) %collective-permute-start.7) | collective-permute-done | bytes 155680 | tf_op jit(solution)/shard_map/ppermute | solution.py:1100
  55.6 2.6 %update.1 = (bf16[8,1,512,128]{3,2,1,0:T(8,128)(2,1)}, bf16[608,128]{1,0:T(8,128)(2,1)S(1)}, bf16[608,128]{1,0:T(8,128)(2,1)S(1)}, bf16[608,128]{1,0:T(8,128)(2,...) custom-call(bf16[8,1,528,128]{3,2,1,0:T(8,128)(2,1)S(1)} %get-tuple-, ...), custom_call_target="tpu_custom_call" | custom-call | tf_op jit(solution)/shard_map/update/pallas_call | solution.py:806
  58.2 1.6 %collective-permute-start.16 = (bf16[608,128]{1,0:T(8,128)(2,1)S(1)}, bf16[608,128]{1,0:T(8,128)(2,1)S(1)}, u32[]{:S(2)}, u32[]{:S(2)}) collective-permute-start(bf16[608,128]{1,0:T(8,128)(2,1)S(1)} %get-tuple-element.48), channel_id=1, source_target_pairs={{0,2},{2,0},{4,6},{6,4},{8,10},{10,8},{12,14},{14,12},{1,3},{3,1},... | collective-permute-start | bytes 466952 | tf_op jit(solution)/shard_map/ppermute | solution.py:1100
  59.8 1.4 %collective-permute-start.17 = (bf16[608,128]{1,0:T(8,128)(2,1)S(1)}, bf16[608,128]{1,0:T(8,128)(2,1)S(1)}, u32[]{:S(2)}, u32[]{:S(2)}) collective-permute-start(bf16[608,128]{1,0:T(8,128)(2,1)S(1)} %get-tuple-element.49), channel_id=1, source_target_pairs={{0,4},{2,6},{4,0},{6,2},{8,12},{10,14},{12,8},{14,10},{1,5},{3,7},... | collective-permute-start | bytes 466952 | tf_op jit(solution)/shard_map/ppermute | solution.py:1100
  61.2 2.1 %collective-permute-start.12 = (bf16[608,128]{1,0:T(8,128)(2,1)S(1)}, bf16[608,128]{1,0:T(8,128)(2,1)S(1)}, u32[]{:S(2)}, u32[]{:S(2)}) collective-permute-start(bf16[608,128]{1,0:T(8,128)(2,1)S(1)} %get-tuple-element.43), channel_id=1, source_target_pairs={{0,8},{2,10},{4,12},{6,14},{8,0},{10,2},{12,4},{14,6},{1,9},{3,11}... | collective-permute-start | bytes 466952 | tf_op jit(solution)/shard_map/ppermute | solution.py:1100
  64.1 2.1 %collective-permute-start.18 = (bf16[608,128]{1,0:T(8,128)(2,1)S(1)}, bf16[608,128]{1,0:T(8,128)(2,1)S(1)}, u32[]{:S(2)}, u32[]{:S(2)}) collective-permute-start(bf16[608,128]{1,0:T(8,128)(2,1)S(1)} %get-tuple-element.50), channel_id=1, source_target_pairs={{0,6},{2,4},{4,2},{6,0},{8,14},{10,12},{12,10},{14,8},{1,7},{3,5},... | collective-permute-start | bytes 466952 | tf_op jit(solution)/shard_map/ppermute | solution.py:1100
  66.2 1.5 %collective-permute-start.14 = (bf16[608,128]{1,0:T(8,128)(2,1)S(1)}, bf16[608,128]{1,0:T(8,128)(2,1)S(1)}, u32[]{:S(2)}, u32[]{:S(2)}) collective-permute-start(bf16[608,128]{1,0:T(8,128)(2,1)S(1)} %get-tuple-element.45), channel_id=1, source_target_pairs={{0,12},{2,14},{4,8},{6,10},{8,4},{10,6},{12,0},{14,2},{1,13},{3,15... | collective-permute-start | bytes 466952 | tf_op jit(solution)/shard_map/ppermute | solution.py:1100
  69.2 7.6 %collective-permute-done.18.rest_3_ = bf16[608,128]{1,0:T(8,128)(2,1)S(1)} collective-permute-done((bf16[608,128]{1,0:T(8,128)(2,1)S(1)}, bf16[608,128]{1,0:T(8,128)(2,1)S(1)}, u32[]{:S(2)}, u32[]{:S(2)}) %collective-permute-start.18) | collective-permute-done | bytes 155680 | tf_op jit(solution)/shard_map/ppermute | solution.py:1100
  76.8 4.7 %shrink_part.2 = (bf16[4,4,512,128]{3,2,1,0:T(8,128)(2,1)S(1)}, f32[4,512,128]{2,1,0:T(8,128)S(1)}, bf16[4,4,512,128]{3,2,1,0:T(8,128)(2,1)S(1)}) custom-call(f32[4,17]{1,0:T(4,128)} %row_taps.7, f32[4,17]{1,0:T(4,128)} %col_taps.7, bf16[4,8,512,128]{3,2,1,0:T(8,128)(2,1)} %bitcast.15, bf16[608,128]{1,0:T(8,128)(2,1)S(1)} %get-tuple-element.47.rest_0_, ...), custom_call_target="tpu_custom_call" | custom-call | tf_op jit(solution)/shard_map/shrink_part/pallas_call | solution.py:1062
  81.4 2.9 %collective-permute-done.13.rest_1_ = bf16[608,128]{1,0:T(8,128)(2,1)S(1)} collective-permute-done((bf16[608,128]{1,0:T(8,128)(2,1)S(1)}, bf16[608,128]{1,0:T(8,128)(2,1)S(1)}, u32[]{:S(2)}, u32[]{:S(2)}) %collective-permute-start.13) | collective-permute-done | bytes 155680 | tf_op jit(solution)/shard_map/ppermute | solution.py:1100
  84.4 4.3 %collective-permute-done.14.rest_2_ = bf16[608,128]{1,0:T(8,128)(2,1)S(1)} collective-permute-done((bf16[608,128]{1,0:T(8,128)(2,1)S(1)}, bf16[608,128]{1,0:T(8,128)(2,1)S(1)}, u32[]{:S(2)}, u32[]{:S(2)}) %collective-permute-start.14) | collective-permute-done | bytes 155680 | tf_op jit(solution)/shard_map/ppermute | solution.py:1100
  88.7 2.1 %collective-permute-done.15.rest_3_ = bf16[608,128]{1,0:T(8,128)(2,1)S(1)} collective-permute-done((bf16[608,128]{1,0:T(8,128)(2,1)S(1)}, bf16[608,128]{1,0:T(8,128)(2,1)S(1)}, u32[]{:S(2)}, u32[]{:S(2)}) %collective-permute-start.15) | collective-permute-done | bytes 155680 | tf_op jit(solution)/shard_map/ppermute | solution.py:1100
  90.8 5.2 %shrink_part.3 = bf16[4,8,512,128]{3,2,1,0:T(8,128)(2,1)} custom-call(f32[4,17]{1,0:T(4,128)} %row_taps.7, f32[4,17]{1,0:T(4,128)} %col_taps.7, bf16[4,8,512,128]{3,2,1,0:T(8,128)(2,1)} %bitcast.16, bf16[608,128]{1,0:T(8,128)(2,1)S(1)} %collective-permute-done.12.rest_0_, bf16[608,128]{1,0:T(8,128)(2,1)S(1)} %collective-permute-done.13.rest_1_, ...), custom_call_target="tpu_custom_call" | custom-call | tf_op jit(solution)/shard_map/shrink_part/pallas_call | solution.py:1062
  (40 shorter events, 6.0 us)
Async XLA Ops:
  0.6 14.3 %collective-permute-start = (bf16[8,1,512,128]{3,2,1,0:T(8,128)(2,1)}, bf16[8,1,512,128]{3,2,1,0:T(8,128)(2,1)S(1)}, u32[]{:S(2)}, u32[]{:S(2)}) collective-permute-start(bf16[8,1,512,128]{3,2,1,0:T(8,128)(2,1)} %bitcast.17), channel_id=1, source_target_pairs={{0,1},{1,0},{2,3},{3,2},{4,5},{5,4},{6,7},{7,6},{8,9},{9,8},{10,11... | collective-permute-start | bytes 3145736 | tf_op jit(solution)/shard_map/ppermute | solution.py:1082
  0.7 14.3 %collective-permute-start.1 = (s32[512,512]{1,0:T(8,128)}, s32[512,512]{1,0:T(8,128)S(1)}, u32[]{:S(2)}, u32[]{:S(2)}) collective-permute-start(s32[512,512]{1,0:T(8,128)} %bitcast.23), channel_id=1, source_target_pairs={{0,1},{1,0},{2,3},{3,2},{4,5},{5,4},{6,7},{7,6},{8,9},{9,8},{10,11... | collective-permute-start | bytes 3145736 | tf_op jit(solution)/shard_map/ppermute | solution.py:1082
  1.2 41.9 %collective-permute-start.4 = (bf16[8,1,512,128]{3,2,1,0:T(8,128)(2,1)}, bf16[8,1,512,128]{3,2,1,0:T(8,128)(2,1)S(1)}, u32[]{:S(2)}, u32[]{:S(2)}) collective-permute-start(bf16[8,1,512,128]{3,2,1,0:T(8,128)(2,1)} %bitcast.21), channel_id=1, source_target_pairs={{0,1},{1,0},{2,3},{3,2},{4,5},{5,4},{6,7},{7,6},{8,9},{9,8},{10,11... | collective-permute-start | bytes 3145736 | tf_op jit(solution)/shard_map/ppermute | solution.py:1082
  2.3 4.5 %collective-permute-start.2 = (bf16[4,8,16,128]{3,2,1,0:T(8,128)(2,1)S(1)}, bf16[4,8,16,128]{3,2,1,0:T(8,128)(2,1)S(1)}, u32[]{:S(2)}, u32[]{:S(2)}) collective-permute-start(bf16[4,8,16,128]{3,2,1,0:T(8,128)(2,1)S(1)} %slice_select_fusion), channel_id=1, source_target_pairs={{0,1},{1,0},{2,3},{3,2},{4,5},{5,4},{6,7},{7,6},{8,9},{9,8},{10,11... | collective-permute-start | bytes 393224 | tf_op jit(solution)/shard_map/ppermute | solution.py:1082
  10.7 4.2 %copy-start.1 = (f32[512,128]{1,0:T(8,128)S(1)}, f32[512,128]{1,0:T(8,128)}, u32[]{:S(2)}) copy-start(f32[512,128]{1,0:T(8,128)} %constant.29.clone.rest_7_) | copy-start | bytes 786436
  10.7 4.2 %copy-start.2 = (f32[512,128]{1,0:T(8,128)S(1)}, f32[512,128]{1,0:T(8,128)}, u32[]{:S(2)}) copy-start(f32[512,128]{1,0:T(8,128)} %constant.28.clone.rest_6_) | copy-start | bytes 786436
  10.8 4.2 %copy-start.3 = (f32[48,512]{1,0:T(8,128)S(1)}, f32[48,512]{1,0:T(8,128)}, u32[]{:S(2)}) copy-start(f32[48,512]{1,0:T(8,128)} %constant.27.clone.rest_5_) | copy-start | bytes 294916
  10.8 4.2 %copy-start.4 = (f32[48,512]{1,0:T(8,128)S(1)}, f32[48,512]{1,0:T(8,128)}, u32[]{:S(2)}) copy-start(f32[48,512]{1,0:T(8,128)} %constant.26.clone.rest_4_) | copy-start | bytes 294916
  21.6 23.8 %collective-permute-start.3 = (bf16[528,512]{1,0:T(8,128)(2,1)S(1)}, bf16[528,512]{1,0:T(8,128)(2,1)S(1)}, u32[]{:S(2)}, u32[]{:S(2)}) collective-permute-start(bf16[528,512]{1,0:T(8,128)(2,1)S(1)} %get-tuple-element.31), channel_id=1, source_target_pairs={{0,1},{1,0},{2,3},{3,2},{4,5},{5,4},{6,7},{7,6},{8,9},{9,8},{10,11... | collective-permute-start | bytes 1622024 | tf_op jit(solution)/shard_map/ppermute | solution.py:1082
  21.8 17.3 %collective-permute-start.9 = (bf16[608,128]{1,0:T(8,128)(2,1)S(1)}, bf16[608,128]{1,0:T(8,128)(2,1)S(1)}, u32[]{:S(2)}, u32[]{:S(2)}) collective-permute-start(bf16[608,128]{1,0:T(8,128)(2,1)S(1)} %get-tuple-element.39), channel_id=1, source_target_pairs={{0,10},{2,8},{4,14},{6,12},{8,2},{10,0},{12,6},{14,4},{1,11},{3,9}... | collective-permute-start | bytes 466952 | tf_op jit(solution)/shard_map/ppermute | solution.py:1100
  25.3 17.5 %collective-permute-start.10 = (bf16[608,128]{1,0:T(8,128)(2,1)S(1)}, bf16[608,128]{1,0:T(8,128)(2,1)S(1)}, u32[]{:S(2)}, u32[]{:S(2)}) collective-permute-start(bf16[608,128]{1,0:T(8,128)(2,1)S(1)} %get-tuple-element.40), channel_id=1, source_target_pairs={{0,12},{2,14},{4,8},{6,10},{8,4},{10,6},{12,0},{14,2},{1,13},{3,15... | collective-permute-start | bytes 466952 | tf_op jit(solution)/shard_map/ppermute | solution.py:1100
  25.3 29.2 %collective-permute-start.8 = (bf16[608,128]{1,0:T(8,128)(2,1)S(1)}, bf16[608,128]{1,0:T(8,128)(2,1)S(1)}, u32[]{:S(2)}, u32[]{:S(2)}) collective-permute-start(bf16[608,128]{1,0:T(8,128)(2,1)S(1)} %get-tuple-element.28._), channel_id=1, source_target_pairs={{0,8},{2,10},{4,12},{6,14},{8,0},{10,2},{12,4},{14,6},{1,9},{3,11}... | collective-permute-start | bytes 466952 | tf_op jit(solution)/shard_map/ppermute | solution.py:1100
  39.1 15.4 %collective-permute-start.11 = (bf16[608,128]{1,0:T(8,128)(2,1)S(1)}, bf16[608,128]{1,0:T(8,128)(2,1)S(1)}, u32[]{:S(2)}, u32[]{:S(2)}) collective-permute-start(bf16[608,128]{1,0:T(8,128)(2,1)S(1)} %get-tuple-element.41), channel_id=1, source_target_pairs={{0,14},{2,12},{4,10},{6,8},{8,6},{10,4},{12,2},{14,0},{1,15},{3,13... | collective-permute-start | bytes 466952 | tf_op jit(solution)/shard_map/ppermute | solution.py:1100
  42.9 11.6 %collective-permute-start.5 = (bf16[608,128]{1,0:T(8,128)(2,1)S(1)}, bf16[608,128]{1,0:T(8,128)(2,1)S(1)}, u32[]{:S(2)}, u32[]{:S(2)}) collective-permute-start(bf16[608,128]{1,0:T(8,128)(2,1)S(1)} %get-tuple-element.36), channel_id=1, source_target_pairs={{0,2},{2,0},{4,6},{6,4},{8,10},{10,8},{12,14},{14,12},{1,3},{3,1},... | collective-permute-start | bytes 466952 | tf_op jit(solution)/shard_map/ppermute | solution.py:1100
  43.1 11.4 %collective-permute-start.6 = (bf16[608,128]{1,0:T(8,128)(2,1)S(1)}, bf16[608,128]{1,0:T(8,128)(2,1)S(1)}, u32[]{:S(2)}, u32[]{:S(2)}) collective-permute-start(bf16[608,128]{1,0:T(8,128)(2,1)S(1)} %get-tuple-element.37), channel_id=1, source_target_pairs={{0,4},{2,6},{4,0},{6,2},{8,12},{10,14},{12,8},{14,10},{1,5},{3,7},... | collective-permute-start | bytes 466952 | tf_op jit(solution)/shard_map/ppermute | solution.py:1100
  45.4 10.2 %collective-permute-start.7 = (bf16[608,128]{1,0:T(8,128)(2,1)S(1)}, bf16[608,128]{1,0:T(8,128)(2,1)S(1)}, u32[]{:S(2)}, u32[]{:S(2)}) collective-permute-start(bf16[608,128]{1,0:T(8,128)(2,1)S(1)} %get-tuple-element.38), channel_id=1, source_target_pairs={{0,6},{2,4},{4,2},{6,0},{8,14},{10,12},{12,10},{14,8},{1,7},{3,5},... | collective-permute-start | bytes 466952 | tf_op jit(solution)/shard_map/ppermute | solution.py:1100
  58.2 8.0 %collective-permute-start.16 = (bf16[608,128]{1,0:T(8,128)(2,1)S(1)}, bf16[608,128]{1,0:T(8,128)(2,1)S(1)}, u32[]{:S(2)}, u32[]{:S(2)}) collective-permute-start(bf16[608,128]{1,0:T(8,128)(2,1)S(1)} %get-tuple-element.48), channel_id=1, source_target_pairs={{0,2},{2,0},{4,6},{6,4},{8,10},{10,8},{12,14},{14,12},{1,3},{3,1},... | collective-permute-start | bytes 466952 | tf_op jit(solution)/shard_map/ppermute | solution.py:1100
  59.8 8.8 %collective-permute-start.17 = (bf16[608,128]{1,0:T(8,128)(2,1)S(1)}, bf16[608,128]{1,0:T(8,128)(2,1)S(1)}, u32[]{:S(2)}, u32[]{:S(2)}) collective-permute-start(bf16[608,128]{1,0:T(8,128)(2,1)S(1)} %get-tuple-element.49), channel_id=1, source_target_pairs={{0,4},{2,6},{4,0},{6,2},{8,12},{10,14},{12,8},{14,10},{1,5},{3,7},... | collective-permute-start | bytes 466952 | tf_op jit(solution)/shard_map/ppermute | solution.py:1100
  61.2 20.2 %collective-permute-start.12 = (bf16[608,128]{1,0:T(8,128)(2,1)S(1)}, bf16[608,128]{1,0:T(8,128)(2,1)S(1)}, u32[]{:S(2)}, u32[]{:S(2)}) collective-permute-start(bf16[608,128]{1,0:T(8,128)(2,1)S(1)} %get-tuple-element.43), channel_id=1, source_target_pairs={{0,8},{2,10},{4,12},{6,14},{8,0},{10,2},{12,4},{14,6},{1,9},{3,11}... | collective-permute-start | bytes 466952 | tf_op jit(solution)/shard_map/ppermute | solution.py:1100
  63.3 21.1 %collective-permute-start.13 = (bf16[608,128]{1,0:T(8,128)(2,1)S(1)}, bf16[608,128]{1,0:T(8,128)(2,1)S(1)}, u32[]{:S(2)}, u32[]{:S(2)}) collective-permute-start(bf16[608,128]{1,0:T(8,128)(2,1)S(1)} %get-tuple-element.44), channel_id=1, source_target_pairs={{0,10},{2,8},{4,14},{6,12},{8,2},{10,0},{12,6},{14,4},{1,11},{3,9}... | collective-permute-start | bytes 466952 | tf_op jit(solution)/shard_map/ppermute | solution.py:1100
  64.1 12.7 %collective-permute-start.18 = (bf16[608,128]{1,0:T(8,128)(2,1)S(1)}, bf16[608,128]{1,0:T(8,128)(2,1)S(1)}, u32[]{:S(2)}, u32[]{:S(2)}) collective-permute-start(bf16[608,128]{1,0:T(8,128)(2,1)S(1)} %get-tuple-element.50), channel_id=1, source_target_pairs={{0,6},{2,4},{4,2},{6,0},{8,14},{10,12},{12,10},{14,8},{1,7},{3,5},... | collective-permute-start | bytes 466952 | tf_op jit(solution)/shard_map/ppermute | solution.py:1100
  66.2 22.5 %collective-permute-start.14 = (bf16[608,128]{1,0:T(8,128)(2,1)S(1)}, bf16[608,128]{1,0:T(8,128)(2,1)S(1)}, u32[]{:S(2)}, u32[]{:S(2)}) collective-permute-start(bf16[608,128]{1,0:T(8,128)(2,1)S(1)} %get-tuple-element.45), channel_id=1, source_target_pairs={{0,12},{2,14},{4,8},{6,10},{8,4},{10,6},{12,0},{14,2},{1,13},{3,15... | collective-permute-start | bytes 466952 | tf_op jit(solution)/shard_map/ppermute | solution.py:1100
  68.6 22.2 %collective-permute-start.15 = (bf16[608,128]{1,0:T(8,128)(2,1)S(1)}, bf16[608,128]{1,0:T(8,128)(2,1)S(1)}, u32[]{:S(2)}, u32[]{:S(2)}) collective-permute-start(bf16[608,128]{1,0:T(8,128)(2,1)S(1)} %get-tuple-element.46), channel_id=1, source_target_pairs={{0,14},{2,12},{4,10},{6,8},{8,6},{10,4},{12,2},{14,0},{1,15},{3,13... | collective-permute-start | bytes 466952 | tf_op jit(solution)/shard_map/ppermute | solution.py:1100
  76.8 14.0 %copy-start = (s32[1,1,512,128]{3,2,1,0:T(8,128)S(1)}, s32[1,1,512,128]{3,2,1,0:T(8,128)}, u32[]{:S(2)}) copy-start(s32[1,1,512,128]{3,2,1,0:T(8,128)} %param.19) | copy-start | bytes 786436
  (4 other events, 16.9 us)

commit v3 on v2

--- a/solution.py
+++ b/solution.py
@@ -423,39 +423,21 @@
         return pl.multiple_of((2 * facet_row + which) * strip_rows, strip_rows)
 
     copies = []
-    for facet_row in range(facet_rows):
-        for col in range(cols):
-            lanes = pl.ds(col * LANES, LANES)
-            copies.append(
-                pltpu.make_async_copy(
-                    own.at[col, facet_row],
-                    picture.at[pl.ds(strip_at(facet_row, split), strip_rows), lanes],
-                    loads.at[len(copies)],
-                )
-            )
     for source, target in ((turn_from_re, turn_re), (turn_from_im, turn_im)):
         copies.append(pltpu.make_async_copy(source, target, loads.at[len(copies)]))
-    count_copies = []
-    for tile in range(part // LANES):
-        lanes = pl.ds(pl.multiple_of(split * part + tile * LANES, LANES), LANES)
-        count_copies.append(
-            pltpu.make_async_copy(
-                own_counts.at[:, lanes],
-                counts.at[tile, pl.ds(pl.multiple_of(split * half, half), half), :],
-                loads.at[len(copies) + len(count_copies)],
-            )
-        )
-    for copy in (*copies, *count_copies):
+    for copy in copies:
         copy.start()
     fill_transforms(seeds, cosine, sine, freq)
     for facet_row in range(facet_rows):
-        there = pl.ds(strip_at(facet_row, 1 - split), strip_rows)
-        for col in range(cols):
-            picture[there, col * LANES : (col + 1) * LANES] = other[col, facet_row]
+        for source, which in ((own, split), (other, 1 - split)):
+            there = pl.ds(strip_at(facet_row, which), strip_rows)
+            for col in range(cols):
+                picture[there, col * LANES : (col + 1) * LANES] = source[col, facet_row]
     for tile in range(part // LANES):
         lanes = pl.ds(pl.multiple_of(split * part + tile * LANES, LANES), LANES)
-        there = pl.ds(pl.multiple_of((1 - split) * half, half), half)
-        counts[tile, there, :] = other_counts[:, lanes]
+        for source, which in ((own_counts, split), (other_counts, 1 - split)):
+            there = pl.ds(pl.multiple_of(which * half, half), half)
+            counts[tile, there, :] = source[:, lanes]
     for copy in copies:
         copy.wait()
     block = min(256, half)
@@ -482,8 +464,6 @@
         return carry
 
     lax.fori_loop(0, half // block, first, 0)
-    for copy in count_copies:
-        copy.wait()
 
     def second(step, carry):
         at = pl.ds(pl.multiple_of(step * block, block), block)
@@ -555,7 +535,7 @@
             pltpu.VMEM((rows, half), jnp.bfloat16),
             pltpu.VMEM((rows, half), jnp.bfloat16),
         ],
-        in_specs=[anywhere, inside] * 2
+        in_specs=[inside] * 4
         + [inside] * 6
         + [anywhere] * 2
         + [pl.BlockSpec(memory_space=pl.ANY)],
@@ -571,43 +551,24 @@
             pltpu.VMEM((half, pixels), jnp.bfloat16),
             pltpu.VMEM((half, pixels), jnp.bfloat16),
             pltpu.VMEM((pixels, half), jnp.bfloat16),
-            pltpu.SemaphoreType.DMA((cols * facet_rows + 2 + half // LANES,)),
+            pltpu.SemaphoreType.DMA((2,)),
         ],
         compiler_params=SOME_ROOM,
         name="spectrum",
     )(
-        *held_outside((own,)), *held_inside((other,)),
-        *held_outside((own_counts,)), *held_inside((other_counts,)),
+        *held_inside((own, other, own_counts, other_counts)),
         *phase_seeds(pixels), *twiddles(pixels), after,
     )
 
 
 def gradient_kernel(
-    kept, got, freq, own_from, other, dirty_from, other_dirty, stepped, edge_out, own,
-    joined, dirty, loads, *, margin
+    kept, got, freq, own, other, dirty, other_dirty, stepped, edge_out, joined, *, margin
 ):
     split = lax.axis_index("split")
     cols, facet_rows, strip_rows, _ = own.shape
     half = kept.shape[1]
     rows = strip_rows + 2 * margin
     pair = 2 if cols % 2 == 0 else 1
-    started = []
-
-    def load(source, target):
-        copy = pltpu.make_async_copy(source, target, loads.at[len(started)])
-        copy.start()
-        started.append(copy)
-        return copy
-
-    steps = []
-    for step in range(cols // pair):
-        some = pl.ds(step * pair, pair)
-        steps.append(
-            [
-                load(own_from.at[some], own.at[some]),
-                load(dirty_from.at[some], dirty.at[some]),
-            ]
-        )
 
     def edges(source, col, facet_row):
         over = jnp.maximum(facet_row - 1 + split, 0)
@@ -623,8 +584,6 @@
     joined[:, :half] = kept[...]
     joined[:, half:] = got[...]
     for step in range(cols // pair):
-        for copy in steps[step]:
-            copy.wait()
         value = lax.dot_general(
             joined[...],
             freq[step * pair * LANES : (step + 1) * pair * LANES, :],
@@ -659,20 +618,14 @@
         out_shape=[
             pltpu.VMEM((cols, facet_rows, rows, lanes), jnp.bfloat16),
             pltpu.VMEM((cols, facet_rows, 2 * margin, lanes), jnp.bfloat16),
-            pltpu.VMEM(own.shape, jnp.bfloat16),
         ],
-        in_specs=[inside] * 3 + [anywhere, inside] * 2,
-        out_specs=[inside] * 3,
-        scratch_shapes=[
-            pltpu.VMEM((kept.shape[0], pixels), jnp.bfloat16),
-            pltpu.VMEM(own.shape, jnp.bfloat16),
-            pltpu.SemaphoreType.DMA((2 * cols,)),
-        ],
+        in_specs=[inside] * 7,
+        out_specs=[inside] * 2,
+        scratch_shapes=[pltpu.VMEM((kept.shape[0], pixels), jnp.bfloat16)],
         compiler_params=SOME_ROOM,
         name="gradient",
     )(
-        *held_inside((kept, got, freq)), *held_outside((own,)), *held_inside((other,)),
-        *held_outside((own_dirty,)), *held_inside((other_dirty,)),
+        *held_inside((kept, got, freq, own, other, own_dirty, other_dirty))
     )
 
 
@@ -1138,10 +1091,10 @@
     freq, kept, sent = spectrum(image, other_image, counts, other_counts, margin, blocks[0])
     arrived = crossed(blocks, single)
     got = swapped(sent)
-    stepped, edges, pixels = gradient_step(
+    stepped, edges = gradient_step(
         kept, got, freq, image, other_image, dirty, other_dirty, margin
     )
-    new_image, blocks = update_step(stepped, edges, pixels, arrived, margin, single)
+    new_image, blocks = update_step(stepped, edges, image, arrived, margin, single)
     arrived = crossed(blocks, single)
     if single:
         new_dual = shrink_step(row_taps, col_taps, mask, dual, arrived, single)

time: 96.4 us -> 96.6 us (level)
  waiting for transfers between devices: 41.7 us -> 44.4 us
  Pallas kernels: 31.2 us -> 28.7 us
    pallas_call x1, Pallas kernels: 4.16 us -> 1.43 us  [gradient_step(): pl.pallas_call(functools.partial(gradient_kernel, margin=margin), out_sha...]
    ppermute x14, waiting for transfers between devices: 37.7 us -> 40.4 us  [crossed(): lax.ppermute(blocks[place], 'chan', [(i, i ^ place) for i in range(count)])]
  transfers between devices with their start and end apart: 19 -> 19, of which waited for: 10 -> 10; matrix products, arithmetic and copies ran while one was open for 1% -> 1% of each run, Pallas kernels for 24% -> 22%
where the time goes in v3:
time: 96.6 us; the launch traced here: 96.4 us
  waiting for transfers between devices  44.4 us (46%)
  Pallas kernels  28.7 us (30%)
  starting transfers between devices  21.2 us (22%)
  between operations  1.06 us (1%)
  other arithmetic  0.99 us (1%)
    ppermute x14, waiting for transfers between devices, crossed(): lax.ppermute(blocks[place], 'chan', [(i, i ^ place) for i in range(count)])  40.4 us
    ppermute x14, starting transfers between devices, crossed(): lax.ppermute(blocks[place], 'chan', [(i, i ^ place) for i in range(count)])  19.9 us
    pallas_call x2, Pallas kernels, shrink_part(): pl.pallas_call(functools.partial(shrink_part_kernel, places=places, margi...  9.75 us
    pallas_call x2, Pallas kernels, part_adjoint(): pl.pallas_call(functools.partial(part_adjoint_kernel, places=places, face...  8.08 us
    pallas_call x1, Pallas kernels, spectrum(): pl.pallas_call(functools.partial(spectrum_kernel, margin=margin), out_sha...  6.8 us
    ppermute x5, waiting for transfers between devices, swapped(): return lax.ppermute(value, 'split', [(0, 1), (1, 0)])  3.99 us
    pallas_call x1, Pallas kernels, update_step(): pl.pallas_call(functools.partial(update_kernel, margin=margin, facets=fac...  2.61 us
  transfers between devices with their start and end apart: 19, of which 10 were waited for; matrix products, arithmetic and copies ran while one was open for 1% of the time, Pallas kernels for 22%

profile of v3, /device:TPU:8, one launch (start us, length us, event | category | flops | bytes accessed | tf_op | source)
XLA Modules:
  0.0 96.4 jit_solution(6680166443495449677)
XLA Ops:
  2.8 4.0 %collective-permute-done.2.above.below = bf16[4,8,16,128]{3,2,1,0:T(8,128)(2,1)S(1)} collective-permute-done((bf16[4,8,16,128]{3,2,1,0:T(8,128)(2,1)S(1)}, bf16[4,8,16,128]{3,2,1,0:T(8,128)(2,1)S(1)}, u32[]{:S(2)}, u32[]{:S(2)}) %collective-permute-start.2) | collective-permute-done | bytes 131104 | tf_op jit(solution)/shard_map/ppermute | solution.py:1035
  6.8 4.0 %part_adjoint.2 = (bf16[608,128]{1,0:T(8,128)(2,1)S(1)}, bf16[608,128]{1,0:T(8,128)(2,1)S(1)}, bf16[608,128]{1,0:T(8,128)(2,1)S(1)}, bf16[608,128]{1,0:T(8,128)(2,1)S(1)}) custom-call(f32[4,17]{1,0:T(4,128)} %row_taps.7, f32[4,17]{1,0:T(4,128)} %col_taps.7, bf16[4,8,512,128]{3,2,1,0:T(8,128)(2,1)} %bitcast.21, ...), custom_call_target="tpu_custom_call" | custom-call | tf_op jit(solution)/shard_map/part_adjoint/pallas_call | solution.py:372
  10.9 4.1 %part_adjoint.3 = (bf16[608,128]{1,0:T(8,128)(2,1)S(1)}, bf16[608,128]{1,0:T(8,128)(2,1)S(1)}, bf16[608,128]{1,0:T(8,128)(2,1)S(1)}, bf16[608,128]{1,0:T(8,128)(2,1)S(1)}) custom-call(f32[4,17]{1,0:T(4,128)} %row_taps.7, f32[4,17]{1,0:T(4,128)} %col_taps.7, bf16[4,8,512,128]{3,2,1,0:T(8,128)(2,1)} %bitcast.22, ...), custom_call_target="tpu_custom_call" | custom-call | tf_op jit(solution)/shard_map/part_adjoint/pallas_call | solution.py:372
  15.1 6.8 %spectrum.1 = (bf16[1024,1024]{1,0:T(8,128)(2,1)S(1)}, bf16[528,512]{1,0:T(8,128)(2,1)S(1)}, bf16[528,512]{1,0:T(8,128)(2,1)S(1)}) custom-call(bf16[8,1,512,128]{3,2,1,0:T(8,128)(2,1)S(1)} %bitcast.12, bf16[8,1,512,128]{3,2,1,0:T(8,128)(2,1)S(1)} %collective-permute-done.other, s32[512,512]{1,0:T(8,128)S(1)} %bitcast.18, ...), custom_call_target="tpu_custom_call" | custom-call | tf_op jit(solution)/shard_map/spectrum/pallas_call | solution.py:531
  22.1 3.5 %collective-permute-start.9 = (bf16[608,128]{1,0:T(8,128)(2,1)S(1)}, bf16[608,128]{1,0:T(8,128)(2,1)S(1)}, u32[]{:S(2)}, u32[]{:S(2)}) collective-permute-start(bf16[608,128]{1,0:T(8,128)(2,1)S(1)} %get-tuple-element.37), channel_id=1, source_target_pairs={{0,10},{2,8},{4,14},{6,12},{8,2},{10,0},{12,6},{14,4},{1,11},{3,9}... | collective-permute-start | bytes 466952 | tf_op jit(solution)/shard_map/ppermute | solution.py:1053
  25.7 2.8 %collective-permute-start.8 = (bf16[608,128]{1,0:T(8,128)(2,1)S(1)}, bf16[608,128]{1,0:T(8,128)(2,1)S(1)}, u32[]{:S(2)}, u32[]{:S(2)}) collective-permute-start(bf16[608,128]{1,0:T(8,128)(2,1)S(1)} %get-tuple-element.27._), channel_id=1, source_target_pairs={{0,8},{2,10},{4,12},{6,14},{8,0},{10,2},{12,4},{14,6},{1,9},{3,11}... | collective-permute-start | bytes 466952 | tf_op jit(solution)/shard_map/ppermute | solution.py:1053
  28.5 10.9 %collective-permute-done.9.rest_5_ = bf16[608,128]{1,0:T(8,128)(2,1)S(1)} collective-permute-done((bf16[608,128]{1,0:T(8,128)(2,1)S(1)}, bf16[608,128]{1,0:T(8,128)(2,1)S(1)}, u32[]{:S(2)}, u32[]{:S(2)}) %collective-permute-start.9) | collective-permute-done | bytes 155680 | tf_op jit(solution)/shard_map/ppermute | solution.py:1053
  39.4 3.8 %collective-permute-done.10.rest_6_ = bf16[608,128]{1,0:T(8,128)(2,1)S(1)} collective-permute-done((bf16[608,128]{1,0:T(8,128)(2,1)S(1)}, bf16[608,128]{1,0:T(8,128)(2,1)S(1)}, u32[]{:S(2)}, u32[]{:S(2)}) %collective-permute-start.10) | collective-permute-done | bytes 155680 | tf_op jit(solution)/shard_map/ppermute | solution.py:1053
  43.4 2.2 %collective-permute-start.6 = (bf16[608,128]{1,0:T(8,128)(2,1)S(1)}, bf16[608,128]{1,0:T(8,128)(2,1)S(1)}, u32[]{:S(2)}, u32[]{:S(2)}) collective-permute-start(bf16[608,128]{1,0:T(8,128)(2,1)S(1)} %get-tuple-element.35), channel_id=1, source_target_pairs={{0,4},{2,6},{4,0},{6,2},{8,12},{10,14},{12,8},{14,10},{1,5},{3,7},... | collective-permute-start | bytes 466952 | tf_op jit(solution)/shard_map/ppermute | solution.py:1053
  46.7 1.4 %gradient.1 = (bf16[8,1,528,128]{3,2,1,0:T(8,128)(2,1)S(1)}, bf16[8,1,16,128]{3,2,1,0:T(8,128)(2,1)S(1)}) custom-call(bf16[528,512]{1,0:T(8,128)(2,1)S(1)} %get-tuple-element.29.kept, bf16[528,512]{1,0:T(8,128)(2,1)S(1)} %collective-permute-done.3.got, bf16[1024,1024]{1,0:T(8,128)(2,1)S(1)} %get-tuple-element.31.freq, bf16[8,1,512,128]{3,2,1,0:T(8,128)(2,1)S(1)} %bitcast.13, ...), custom_call_target="tpu_custom_call" | custom-call | tf_op jit(solution)/shard_map/gradient/pallas_call | solution.py:616
  48.2 6.7 %collective-permute-done.11.rest_7_ = bf16[608,128]{1,0:T(8,128)(2,1)S(1)} collective-permute-done((bf16[608,128]{1,0:T(8,128)(2,1)S(1)}, bf16[608,128]{1,0:T(8,128)(2,1)S(1)}, u32[]{:S(2)}, u32[]{:S(2)}) %collective-permute-start.11) | collective-permute-done | bytes 155680 | tf_op jit(solution)/shard_map/ppermute | solution.py:1053
  54.8 1.1 %collective-permute-done.7.rest_3_ = bf16[608,128]{1,0:T(8,128)(2,1)S(1)} collective-permute-done((bf16[608,128]{1,0:T(8,128)(2,1)S(1)}, bf16[608,128]{1,0:T(8,128)(2,1)S(1)}, u32[]{:S(2)}, u32[]{:S(2)}) %collective-permute-start.7) | collective-permute-done | bytes 155680 | tf_op jit(solution)/shard_map/ppermute | solution.py:1053
  55.9 2.6 %update.1 = (bf16[8,1,512,128]{3,2,1,0:T(8,128)(2,1)}, bf16[608,128]{1,0:T(8,128)(2,1)S(1)}, bf16[608,128]{1,0:T(8,128)(2,1)S(1)}, bf16[608,128]{1,0:T(8,128)(2,...) custom-call(bf16[8,1,528,128]{3,2,1,0:T(8,128)(2,1)S(1)} %get-tuple-, ...), custom_call_target="tpu_custom_call" | custom-call | tf_op jit(solution)/shard_map/update/pallas_call | solution.py:759
  58.5 1.6 %collective-permute-start.16 = (bf16[608,128]{1,0:T(8,128)(2,1)S(1)}, bf16[608,128]{1,0:T(8,128)(2,1)S(1)}, u32[]{:S(2)}, u32[]{:S(2)}) collective-permute-start(bf16[608,128]{1,0:T(8,128)(2,1)S(1)} %get-tuple-element.46), channel_id=1, source_target_pairs={{0,2},{2,0},{4,6},{6,4},{8,10},{10,8},{12,14},{14,12},{1,3},{3,1},... | collective-permute-start | bytes 466952 | tf_op jit(solution)/shard_map/ppermute | solution.py:1053
  60.1 1.4 %collective-permute-start.17 = (bf16[608,128]{1,0:T(8,128)(2,1)S(1)}, bf16[608,128]{1,0:T(8,128)(2,1)S(1)}, u32[]{:S(2)}, u32[]{:S(2)}) collective-permute-start(bf16[608,128]{1,0:T(8,128)(2,1)S(1)} %get-tuple-element.47), channel_id=1, source_target_pairs={{0,4},{2,6},{4,0},{6,2},{8,12},{10,14},{12,8},{14,10},{1,5},{3,7},... | collective-permute-start | bytes 466952 | tf_op jit(solution)/shard_map/ppermute | solution.py:1053
  61.5 2.1 %collective-permute-start.12 = (bf16[608,128]{1,0:T(8,128)(2,1)S(1)}, bf16[608,128]{1,0:T(8,128)(2,1)S(1)}, u32[]{:S(2)}, u32[]{:S(2)}) collective-permute-start(bf16[608,128]{1,0:T(8,128)(2,1)S(1)} %get-tuple-element.41), channel_id=1, source_target_pairs={{0,8},{2,10},{4,12},{6,14},{8,0},{10,2},{12,4},{14,6},{1,9},{3,11}... | collective-permute-start | bytes 466952 | tf_op jit(solution)/shard_map/ppermute | solution.py:1053
  64.4 2.1 %collective-permute-start.18 = (bf16[608,128]{1,0:T(8,128)(2,1)S(1)}, bf16[608,128]{1,0:T(8,128)(2,1)S(1)}, u32[]{:S(2)}, u32[]{:S(2)}) collective-permute-start(bf16[608,128]{1,0:T(8,128)(2,1)S(1)} %get-tuple-element.48), channel_id=1, source_target_pairs={{0,6},{2,4},{4,2},{6,0},{8,14},{10,12},{12,10},{14,8},{1,7},{3,5},... | collective-permute-start | bytes 466952 | tf_op jit(solution)/shard_map/ppermute | solution.py:1053
  66.5 1.5 %collective-permute-start.14 = (bf16[608,128]{1,0:T(8,128)(2,1)S(1)}, bf16[608,128]{1,0:T(8,128)(2,1)S(1)}, u32[]{:S(2)}, u32[]{:S(2)}) collective-permute-start(bf16[608,128]{1,0:T(8,128)(2,1)S(1)} %get-tuple-element.43), channel_id=1, source_target_pairs={{0,12},{2,14},{4,8},{6,10},{8,4},{10,6},{12,0},{14,2},{1,13},{3,15... | collective-permute-start | bytes 466952 | tf_op jit(solution)/shard_map/ppermute | solution.py:1053
  69.5 7.6 %collective-permute-done.18.rest_3_ = bf16[608,128]{1,0:T(8,128)(2,1)S(1)} collective-permute-done((bf16[608,128]{1,0:T(8,128)(2,1)S(1)}, bf16[608,128]{1,0:T(8,128)(2,1)S(1)}, u32[]{:S(2)}, u32[]{:S(2)}) %collective-permute-start.18) | collective-permute-done | bytes 155680 | tf_op jit(solution)/shard_map/ppermute | solution.py:1053
  77.1 4.7 %shrink_part.2 = (bf16[4,4,512,128]{3,2,1,0:T(8,128)(2,1)S(1)}, f32[4,512,128]{2,1,0:T(8,128)S(1)}, bf16[4,4,512,128]{3,2,1,0:T(8,128)(2,1)S(1)}) custom-call(f32[4,17]{1,0:T(4,128)} %row_taps.7, f32[4,17]{1,0:T(4,128)} %col_taps.7, bf16[4,8,512,128]{3,2,1,0:T(8,128)(2,1)} %bitcast.23, bf16[608,128]{1,0:T(8,128)(2,1)S(1)} %get-tuple-element.45.rest_0_, ...), custom_call_target="tpu_custom_call" | custom-call | tf_op jit(solution)/shard_map/shrink_part/pallas_call | solution.py:1015
  81.8 2.9 %collective-permute-done.13.rest_1_ = bf16[608,128]{1,0:T(8,128)(2,1)S(1)} collective-permute-done((bf16[608,128]{1,0:T(8,128)(2,1)S(1)}, bf16[608,128]{1,0:T(8,128)(2,1)S(1)}, u32[]{:S(2)}, u32[]{:S(2)}) %collective-permute-start.13) | collective-permute-done | bytes 155680 | tf_op jit(solution)/shard_map/ppermute | solution.py:1053
  84.7 4.3 %collective-permute-done.14.rest_2_ = bf16[608,128]{1,0:T(8,128)(2,1)S(1)} collective-permute-done((bf16[608,128]{1,0:T(8,128)(2,1)S(1)}, bf16[608,128]{1,0:T(8,128)(2,1)S(1)}, u32[]{:S(2)}, u32[]{:S(2)}) %collective-permute-start.14) | collective-permute-done | bytes 155680 | tf_op jit(solution)/shard_map/ppermute | solution.py:1053
  89.0 2.1 %collective-permute-done.15.rest_3_ = bf16[608,128]{1,0:T(8,128)(2,1)S(1)} collective-permute-done((bf16[608,128]{1,0:T(8,128)(2,1)S(1)}, bf16[608,128]{1,0:T(8,128)(2,1)S(1)}, u32[]{:S(2)}, u32[]{:S(2)}) %collective-permute-start.15) | collective-permute-done | bytes 155680 | tf_op jit(solution)/shard_map/ppermute | solution.py:1053
  91.1 5.1 %shrink_part.3 = bf16[4,8,512,128]{3,2,1,0:T(8,128)(2,1)} custom-call(f32[4,17]{1,0:T(4,128)} %row_taps.7, f32[4,17]{1,0:T(4,128)} %col_taps.7, bf16[4,8,512,128]{3,2,1,0:T(8,128)(2,1)} %bitcast.24, bf16[608,128]{1,0:T(8,128)(2,1)S(1)} %collective-permute-done.12.rest_0_, bf16[608,128]{1,0:T(8,128)(2,1)S(1)} %collective-permute-done.13.rest_1_, ...), custom_call_target="tpu_custom_call" | custom-call | tf_op jit(solution)/shard_map/shrink_part/pallas_call | solution.py:1015
  (46 shorter events, 6.0 us)
Async XLA Ops:
  0.6 14.3 %collective-permute-start = (bf16[8,1,512,128]{3,2,1,0:T(8,128)(2,1)}, bf16[8,1,512,128]{3,2,1,0:T(8,128)(2,1)S(1)}, u32[]{:S(2)}, u32[]{:S(2)}) collective-permute-start(bf16[8,1,512,128]{3,2,1,0:T(8,128)(2,1)} %bitcast.11), channel_id=1, source_target_pairs={{0,1},{1,0},{2,3},{3,2},{4,5},{5,4},{6,7},{7,6},{8,9},{9,8},{10,11... | collective-permute-start | bytes 3145736 | tf_op jit(solution)/shard_map/ppermute | solution.py:1035
  0.7 14.3 %collective-permute-start.1 = (s32[512,512]{1,0:T(8,128)}, s32[512,512]{1,0:T(8,128)S(1)}, u32[]{:S(2)}, u32[]{:S(2)}) collective-permute-start(s32[512,512]{1,0:T(8,128)} %bitcast.17), channel_id=1, source_target_pairs={{0,1},{1,0},{2,3},{3,2},{4,5},{5,4},{6,7},{7,6},{8,9},{9,8},{10,11... | collective-permute-start | bytes 3145736 | tf_op jit(solution)/shard_map/ppermute | solution.py:1035
  1.2 42.2 %collective-permute-start.4 = (bf16[8,1,512,128]{3,2,1,0:T(8,128)(2,1)}, bf16[8,1,512,128]{3,2,1,0:T(8,128)(2,1)S(1)}, u32[]{:S(2)}, u32[]{:S(2)}) collective-permute-start(bf16[8,1,512,128]{3,2,1,0:T(8,128)(2,1)} %bitcast.15), channel_id=1, source_target_pairs={{0,1},{1,0},{2,3},{3,2},{4,5},{5,4},{6,7},{7,6},{8,9},{9,8},{10,11... | collective-permute-start | bytes 3145736 | tf_op jit(solution)/shard_map/ppermute | solution.py:1035
  2.3 4.5 %collective-permute-start.2 = (bf16[4,8,16,128]{3,2,1,0:T(8,128)(2,1)S(1)}, bf16[4,8,16,128]{3,2,1,0:T(8,128)(2,1)S(1)}, u32[]{:S(2)}, u32[]{:S(2)}) collective-permute-start(bf16[4,8,16,128]{3,2,1,0:T(8,128)(2,1)S(1)} %slice_select_fusion), channel_id=1, source_target_pairs={{0,1},{1,0},{2,3},{3,2},{4,5},{5,4},{6,7},{7,6},{8,9},{9,8},{10,11... | collective-permute-start | bytes 393224 | tf_op jit(solution)/shard_map/ppermute | solution.py:1035
  10.7 4.3 %copy-start = (bf16[1,8,1,1,512,128]{5,4,3,2,1,0:T(8,128)(2,1)S(1)}, bf16[1,8,1,1,512,128]{5,4,3,2,1,0:T(8,128)(2,1)}, u32[]{:S(2)}) copy-start(bf16[1,8,1,1,512,128]{5,4,3,2,1,0:T(8,128)(2,1)} %param.15) | copy-start | bytes 3145732
  10.7 4.3 %copy-start.2 = (s32[1,512,512]{2,1,0:T(8,128)S(1)}, s32[1,512,512]{2,1,0:T(8,128)}, u32[]{:S(2)}) copy-start(s32[1,512,512]{2,1,0:T(8,128)} %param.17) | copy-start | bytes 3145732
  10.8 4.3 %copy-start.4 = (f32[512,128]{1,0:T(8,128)S(1)}, f32[512,128]{1,0:T(8,128)}, u32[]{:S(2)}) copy-start(f32[512,128]{1,0:T(8,128)} %constant.29.clone.rest_7_) | copy-start | bytes 786436
  15.1 31.6 %copy-start.1 = (bf16[1,8,1,1,512,128]{5,4,3,2,1,0:T(8,128)(2,1)S(1)}, bf16[1,8,1,1,512,128]{5,4,3,2,1,0:T(8,128)(2,1)}, u32[]{:S(2)}) copy-start(bf16[1,8,1,1,512,128]{5,4,3,2,1,0:T(8,128)(2,1)} %param.16) | copy-start | bytes 3145732
  21.9 23.8 %collective-permute-start.3 = (bf16[528,512]{1,0:T(8,128)(2,1)S(1)}, bf16[528,512]{1,0:T(8,128)(2,1)S(1)}, u32[]{:S(2)}, u32[]{:S(2)}) collective-permute-start(bf16[528,512]{1,0:T(8,128)(2,1)S(1)} %get-tuple-element.30), channel_id=1, source_target_pairs={{0,1},{1,0},{2,3},{3,2},{4,5},{5,4},{6,7},{7,6},{8,9},{9,8},{10,11... | collective-permute-start | bytes 1622024 | tf_op jit(solution)/shard_map/ppermute | solution.py:1035
  22.1 17.3 %collective-permute-start.9 = (bf16[608,128]{1,0:T(8,128)(2,1)S(1)}, bf16[608,128]{1,0:T(8,128)(2,1)S(1)}, u32[]{:S(2)}, u32[]{:S(2)}) collective-permute-start(bf16[608,128]{1,0:T(8,128)(2,1)S(1)} %get-tuple-element.37), channel_id=1, source_target_pairs={{0,10},{2,8},{4,14},{6,12},{8,2},{10,0},{12,6},{14,4},{1,11},{3,9}... | collective-permute-start | bytes 466952 | tf_op jit(solution)/shard_map/ppermute | solution.py:1053
  25.7 17.5 %collective-permute-start.10 = (bf16[608,128]{1,0:T(8,128)(2,1)S(1)}, bf16[608,128]{1,0:T(8,128)(2,1)S(1)}, u32[]{:S(2)}, u32[]{:S(2)}) collective-permute-start(bf16[608,128]{1,0:T(8,128)(2,1)S(1)} %get-tuple-element.38), channel_id=1, source_target_pairs={{0,12},{2,14},{4,8},{6,10},{8,4},{10,6},{12,0},{14,2},{1,13},{3,15... | collective-permute-start | bytes 466952 | tf_op jit(solution)/shard_map/ppermute | solution.py:1053
  25.7 29.2 %collective-permute-start.8 = (bf16[608,128]{1,0:T(8,128)(2,1)S(1)}, bf16[608,128]{1,0:T(8,128)(2,1)S(1)}, u32[]{:S(2)}, u32[]{:S(2)}) collective-permute-start(bf16[608,128]{1,0:T(8,128)(2,1)S(1)} %get-tuple-element.27._), channel_id=1, source_target_pairs={{0,8},{2,10},{4,12},{6,14},{8,0},{10,2},{12,4},{14,6},{1,9},{3,11}... | collective-permute-start | bytes 466952 | tf_op jit(solution)/shard_map/ppermute | solution.py:1053
  39.4 15.4 %collective-permute-start.11 = (bf16[608,128]{1,0:T(8,128)(2,1)S(1)}, bf16[608,128]{1,0:T(8,128)(2,1)S(1)}, u32[]{:S(2)}, u32[]{:S(2)}) collective-permute-start(bf16[608,128]{1,0:T(8,128)(2,1)S(1)} %get-tuple-element.39), channel_id=1, source_target_pairs={{0,14},{2,12},{4,10},{6,8},{8,6},{10,4},{12,2},{14,0},{1,15},{3,13... | collective-permute-start | bytes 466952 | tf_op jit(solution)/shard_map/ppermute | solution.py:1053
  43.2 11.6 %collective-permute-start.5 = (bf16[608,128]{1,0:T(8,128)(2,1)S(1)}, bf16[608,128]{1,0:T(8,128)(2,1)S(1)}, u32[]{:S(2)}, u32[]{:S(2)}) collective-permute-start(bf16[608,128]{1,0:T(8,128)(2,1)S(1)} %get-tuple-element.34), channel_id=1, source_target_pairs={{0,2},{2,0},{4,6},{6,4},{8,10},{10,8},{12,14},{14,12},{1,3},{3,1},... | collective-permute-start | bytes 466952 | tf_op jit(solution)/shard_map/ppermute | solution.py:1053
  43.4 11.4 %collective-permute-start.6 = (bf16[608,128]{1,0:T(8,128)(2,1)S(1)}, bf16[608,128]{1,0:T(8,128)(2,1)S(1)}, u32[]{:S(2)}, u32[]{:S(2)}) collective-permute-start(bf16[608,128]{1,0:T(8,128)(2,1)S(1)} %get-tuple-element.35), channel_id=1, source_target_pairs={{0,4},{2,6},{4,0},{6,2},{8,12},{10,14},{12,8},{14,10},{1,5},{3,7},... | collective-permute-start | bytes 466952 | tf_op jit(solution)/shard_map/ppermute | solution.py:1053
  45.7 10.2 %collective-permute-start.7 = (bf16[608,128]{1,0:T(8,128)(2,1)S(1)}, bf16[608,128]{1,0:T(8,128)(2,1)S(1)}, u32[]{:S(2)}, u32[]{:S(2)}) collective-permute-start(bf16[608,128]{1,0:T(8,128)(2,1)S(1)} %get-tuple-element.36), channel_id=1, source_target_pairs={{0,6},{2,4},{4,2},{6,0},{8,14},{10,12},{12,10},{14,8},{1,7},{3,5},... | collective-permute-start | bytes 466952 | tf_op jit(solution)/shard_map/ppermute | solution.py:1053
  58.5 8.0 %collective-permute-start.16 = (bf16[608,128]{1,0:T(8,128)(2,1)S(1)}, bf16[608,128]{1,0:T(8,128)(2,1)S(1)}, u32[]{:S(2)}, u32[]{:S(2)}) collective-permute-start(bf16[608,128]{1,0:T(8,128)(2,1)S(1)} %get-tuple-element.46), channel_id=1, source_target_pairs={{0,2},{2,0},{4,6},{6,4},{8,10},{10,8},{12,14},{14,12},{1,3},{3,1},... | collective-permute-start | bytes 466952 | tf_op jit(solution)/shard_map/ppermute | solution.py:1053
  60.1 8.8 %collective-permute-start.17 = (bf16[608,128]{1,0:T(8,128)(2,1)S(1)}, bf16[608,128]{1,0:T(8,128)(2,1)S(1)}, u32[]{:S(2)}, u32[]{:S(2)}) collective-permute-start(bf16[608,128]{1,0:T(8,128)(2,1)S(1)} %get-tuple-element.47), channel_id=1, source_target_pairs={{0,4},{2,6},{4,0},{6,2},{8,12},{10,14},{12,8},{14,10},{1,5},{3,7},... | collective-permute-start | bytes 466952 | tf_op jit(solution)/shard_map/ppermute | solution.py:1053
  61.5 20.2 %collective-permute-start.12 = (bf16[608,128]{1,0:T(8,128)(2,1)S(1)}, bf16[608,128]{1,0:T(8,128)(2,1)S(1)}, u32[]{:S(2)}, u32[]{:S(2)}) collective-permute-start(bf16[608,128]{1,0:T(8,128)(2,1)S(1)} %get-tuple-element.41), channel_id=1, source_target_pairs={{0,8},{2,10},{4,12},{6,14},{8,0},{10,2},{12,4},{14,6},{1,9},{3,11}... | collective-permute-start | bytes 466952 | tf_op jit(solution)/shard_map/ppermute | solution.py:1053
  63.6 21.1 %collective-permute-start.13 = (bf16[608,128]{1,0:T(8,128)(2,1)S(1)}, bf16[608,128]{1,0:T(8,128)(2,1)S(1)}, u32[]{:S(2)}, u32[]{:S(2)}) collective-permute-start(bf16[608,128]{1,0:T(8,128)(2,1)S(1)} %get-tuple-element.42), channel_id=1, source_target_pairs={{0,10},{2,8},{4,14},{6,12},{8,2},{10,0},{12,6},{14,4},{1,11},{3,9}... | collective-permute-start | bytes 466952 | tf_op jit(solution)/shard_map/ppermute | solution.py:1053
  64.4 12.7 %collective-permute-start.18 = (bf16[608,128]{1,0:T(8,128)(2,1)S(1)}, bf16[608,128]{1,0:T(8,128)(2,1)S(1)}, u32[]{:S(2)}, u32[]{:S(2)}) collective-permute-start(bf16[608,128]{1,0:T(8,128)(2,1)S(1)} %get-tuple-element.48), channel_id=1, source_target_pairs={{0,6},{2,4},{4,2},{6,0},{8,14},{10,12},{12,10},{14,8},{1,7},{3,5},... | collective-permute-start | bytes 466952 | tf_op jit(solution)/shard_map/ppermute | solution.py:1053
  66.5 22.5 %collective-permute-start.14 = (bf16[608,128]{1,0:T(8,128)(2,1)S(1)}, bf16[608,128]{1,0:T(8,128)(2,1)S(1)}, u32[]{:S(2)}, u32[]{:S(2)}) collective-permute-start(bf16[608,128]{1,0:T(8,128)(2,1)S(1)} %get-tuple-element.43), channel_id=1, source_target_pairs={{0,12},{2,14},{4,8},{6,10},{8,4},{10,6},{12,0},{14,2},{1,13},{3,15... | collective-permute-start | bytes 466952 | tf_op jit(solution)/shard_map/ppermute | solution.py:1053
  69.0 22.2 %collective-permute-start.15 = (bf16[608,128]{1,0:T(8,128)(2,1)S(1)}, bf16[608,128]{1,0:T(8,128)(2,1)S(1)}, u32[]{:S(2)}, u32[]{:S(2)}) collective-permute-start(bf16[608,128]{1,0:T(8,128)(2,1)S(1)} %get-tuple-element.44), channel_id=1, source_target_pairs={{0,14},{2,12},{4,10},{6,8},{8,6},{10,4},{12,2},{14,0},{1,15},{3,13... | collective-permute-start | bytes 466952 | tf_op jit(solution)/shard_map/ppermute | solution.py:1053
  77.1 14.0 %copy-start.3 = (s32[1,1,512,128]{3,2,1,0:T(8,128)S(1)}, s32[1,1,512,128]{3,2,1,0:T(8,128)}, u32[]{:S(2)}) copy-start(s32[1,1,512,128]{3,2,1,0:T(8,128)} %param.19) | copy-start | bytes 786436
  (7 other events, 29.7 us)
